TPU v7x, 32 devices: a whole 2x2x4 slice. The times are simulated.
32 devices in a mesh: dp: 8 (over z, core), fsdp: 4 (over y, x).
Axes of the slice: x: 2, y: 2, z: 4, core: 2. Of those that a mesh axis runs over, the one named last changes fastest.
Arguments:
- features: bfloat16 [4, 8, 32, 32, 512], P('fsdp', None, 'dp'), may hold values from -6 to 6
- conv_weight: bfloat16 [3, 3, 512, 8], replicated, may hold values from -0.046875 to 0.046875
- vae_noise: float32 [8, 4, 4096], P('dp', 'fsdp'), may hold values from -6 to 6
- flips: int32 [8, 4, 4], P('dp', 'fsdp'), may hold values from 0 to 1
- crops: int32 [8, 4, 4, 2], P('dp', 'fsdp'), may hold values from 0 to 4
- tsteps: int32 [8, 4, 4], P('dp', 'fsdp'), may hold values from 0 to 999
- diffusion_noise: float32 [8, 4, 4, 4096], P('dp', 'fsdp'), may hold values from -6 to 6
- selected: int32 [8, 4], P('dp', 'fsdp'), may hold values from 0 to 1, as said below
- w_patch: bfloat16 [16, 384], replicated, may hold values from -1.5 to 1.5
- w_time: bfloat16 [256, 384], replicated, may hold values from -0.375 to 0.375
- w_ada: bfloat16 [384, 1152], replicated, may hold values from -0.3125 to 0.3125
- w_fc1: bfloat16 [384, 1536], P(None, 'fsdp'), may hold values from -1 to 1
- w_fc2: bfloat16 [384, 1536], P(None, 'fsdp'), may hold values from -1 to 1
- w_final: bfloat16 [384, 16], replicated, may hold values from -0.3125 to 0.3125
- noise_fc1: float32 [384, 1536], P(None, 'fsdp'), may hold values from -6 to 6
- noise_fc2: float32 [384, 1536], P(None, 'fsdp'), may hold values from -6 to 6
Outputs:
- update_fc1: float32 [384, 1536], P(None, 'fsdp')
- update_fc2: float32 [384, 1536], P(None, 'fsdp')
- mean_loss: float32 [], replicated
- latent_moments: float32 [8, 4, 8192], P('dp', 'fsdp')
Inputs may be any that keep to these rules, and one draw needn't show every extreme that they name: `selected`: exactly 16 slots are 1.
All inputs are finite; a program needn't handle non-finite values.
Results may differ from a plain program's by a relative error of at most 0.00091.
Values may be sent and summed in bfloat16 or wider, within the bound.
No kernel may reach another device: no remote copies, remote signals or barrier semaphores. Data moves between devices by JAX's collectives and lax.ppermute only.
A program may use at most 64 MiB of HBM per device.

v0:
```python
from functools import partial
import math

import jax
import jax.numpy as jnp
from jax import lax
from jax.sharding import PartitionSpec as P

TSTEPS = 1000


clip_offset = 1e-05
noise_weight = 16.0
norm_epsilon = 1e-06


def layer_norm(values):
    center = values - jnp.mean(values, axis=-1, keepdims=True)
    variance = jnp.mean(center * center, axis=-1, keepdims=True)
    return center * lax.rsqrt(variance + norm_epsilon)


def position_table(side_cells, width):
    quarter = width // 4
    frequency = 1.0 / 10000.0 ** (jnp.arange(quarter, dtype=jnp.float32) / quarter)
    positions = jnp.arange(side_cells, dtype=jnp.float32)
    angles = positions[:, None] * frequency[None, :]
    line_table = jnp.concatenate([jnp.sin(angles), jnp.cos(angles)], axis=1)
    row_part = jnp.repeat(line_table, side_cells, axis=0)
    col_part = jnp.tile(line_table, (side_cells, 1))
    return jnp.concatenate([row_part, col_part], axis=1)


def time_features(steps_in, width):
    half_width = width // 2
    rates = jnp.exp(-math.log(10000.0) * jnp.arange(half_width, dtype=jnp.float32) / half_width)
    phases = steps_in.astype(jnp.float32)[:, None] * rates[None, :]
    return jnp.concatenate([jnp.cos(phases), jnp.sin(phases)], axis=1)


def alpha_bars(steps_in, horizon):
    beta_table = jnp.linspace(0.0001, 0.02, horizon, dtype=jnp.float32)
    alpha_bar = jnp.cumprod(1.0 - beta_table)
    matches = jnp.arange(horizon, dtype=jnp.int32)[None, :] == steps_in[:, None]
    return jnp.sum(jnp.where(matches, alpha_bar[None, :], 0.0), axis=1)


def augment(latent, mirror, crop_at):
    side_cells = latent.shape[0]
    mirrored = jnp.where(mirror == 1, latent[:, ::-1, :], latent)
    padded = jnp.pad(mirrored, ((2, 2), (2, 2), (0, 0)))
    starts = (crop_at[0], crop_at[1], jnp.int32(0))
    return lax.dynamic_slice(padded, starts, (side_cells, side_cells, latent.shape[2]))


def patchify(grid):
    views_count = grid.shape[0]
    half_side = grid.shape[1] // 2
    channels = grid.shape[3]
    blocks = grid.reshape(views_count, half_side, 2, half_side, 2, channels)
    blocks = blocks.transpose(0, 1, 3, 2, 4, 5)
    return blocks.reshape(views_count * half_side * half_side, 4 * channels)


def conv_moments(padded, kernel):
    image_count, padded_rows, side_cells, channels = padded.shape
    out_width = kernel.shape[3]
    tap_matrix = kernel.transpose(2, 0, 1, 3).reshape(channels, 9 * out_width)
    tap_values = jnp.dot(
        padded.reshape(-1, channels), tap_matrix, preferred_element_type=jnp.float32
    )
    tap_values = tap_values.reshape(image_count, padded_rows, side_cells, 3, 3, out_width)
    tap_values = jnp.pad(tap_values, ((0, 0), (0, 0), (1, 1), (0, 0), (0, 0), (0, 0)))
    out_rows = padded_rows - 2
    summed = jnp.zeros((image_count, out_rows, side_cells, out_width), jnp.float32)
    for row_tap in range(3):
        for col_tap in range(3):
            summed = (
                summed
                + tap_values[
                    :,
                    row_tap : row_tap + out_rows,
                    col_tap : col_tap + side_cells,
                    row_tap,
                    col_tap,
                    :,
                ]
            )
    return summed


def example_terms(mean_part, logvar, vae_eps, mirror, crop_at, steps_in, noise, weights):
    w_patch, w_time, w_ada, w_fc1, w_fc2, w_final = weights
    side_cells = mean_part.shape[0]
    channels = mean_part.shape[2]
    views_count = mirror.shape[0]
    width = w_fc1.shape[0]
    latent = mean_part + jnp.exp(0.5 * logvar) * vae_eps.reshape(mean_part.shape)
    augmented = jax.vmap(augment, in_axes=(None, 0, 0))(latent, mirror, crop_at)
    alpha_bar = alpha_bars(steps_in, TSTEPS)
    noise_grid = noise.reshape(views_count, side_cells, side_cells, channels)
    keep_part = jnp.sqrt(alpha_bar)[:, None, None, None]
    blend_part = jnp.sqrt(1.0 - alpha_bar)[:, None, None, None]
    noised = keep_part * augmented + blend_part * noise_grid
    patches = patchify(noised).astype(jnp.bfloat16)
    target = patchify(noise_grid)
    half_side = side_cells // 2
    per_view = half_side * half_side
    tokens = jnp.dot(patches, w_patch, preferred_element_type=jnp.float32)
    tokens = tokens + jnp.tile(position_table(half_side, width), (views_count, 1))
    stamp = time_features(steps_in, w_time.shape[0]).astype(jnp.bfloat16)
    conditioning = jax.nn.silu(jnp.dot(stamp, w_time, preferred_element_type=jnp.float32))
    modulation = jnp.dot(
        conditioning.astype(jnp.bfloat16), w_ada, preferred_element_type=jnp.float32
    )
    offset_rows = jnp.repeat(modulation[:, :width], per_view, axis=0)
    scale_rows = jnp.repeat(modulation[:, width : 2 * width], per_view, axis=0)
    gate_rows = jnp.repeat(modulation[:, 2 * width :], per_view, axis=0)
    modulated = (layer_norm(tokens) * (1.0 + scale_rows) + offset_rows).astype(jnp.bfloat16)
    preact = jnp.dot(modulated, w_fc1, preferred_element_type=jnp.float32)
    hidden, gelu_back = jax.vjp(partial(jax.nn.gelu, approximate=True), preact)
    hidden_low = hidden.astype(jnp.bfloat16)
    branch = lax.dot_general(
        hidden_low, w_fc2, (((1,), (1,)), ((), ())), preferred_element_type=jnp.float32
    )
    mixed_rows = tokens + gate_rows * branch
    final_norm, norm_back = jax.vjp(layer_norm, mixed_rows)
    final_low = final_norm.astype(jnp.bfloat16)
    predicted = jnp.dot(final_low, w_final, preferred_element_type=jnp.float32)
    residue = predicted - target
    entries = residue.shape[0] * residue.shape[1]
    loss_value = jnp.sum(residue * residue) / entries
    grad_pred = (residue * (2.0 / entries)).astype(jnp.bfloat16)
    grad_final = lax.dot_general(
        grad_pred, w_final, (((1,), (1,)), ((), ())), preferred_element_type=jnp.float32
    )
    grad_mixed = norm_back(grad_final)[0]
    grad_branch = (gate_rows * grad_mixed).astype(jnp.bfloat16)
    grad_fc2 = lax.dot_general(
        grad_branch, hidden_low, (((0,), (0,)), ((), ())), preferred_element_type=jnp.float32
    )
    grad_hidden = jnp.dot(grad_branch, w_fc2, preferred_element_type=jnp.float32)
    grad_pre = gelu_back(grad_hidden)[0].astype(jnp.bfloat16)
    grad_fc1 = lax.dot_general(
        modulated, grad_pre, (((0,), (0,)), ((), ())), preferred_element_type=jnp.float32
    )
    return (loss_value, grad_fc1, grad_fc2)


def clip_pair(grad_fc1, grad_fc2):
    squares = jnp.sum(grad_fc1 * grad_fc1) + jnp.sum(grad_fc2 * grad_fc2)
    root_mean = jnp.sqrt(squares / (grad_fc1.size + grad_fc2.size))
    factor = 1.0 / (root_mean + clip_offset)
    return (grad_fc1 * factor, grad_fc2 * factor)


def selected_terms(chosen, mean_part, logvar, vae_eps, mirror, crop_at, steps_in, noise, weights):

    def compute():
        loss_value, grad_fc1, grad_fc2 = example_terms(
            mean_part, logvar, vae_eps, mirror, crop_at, steps_in, noise, weights
        )
        clipped_fc1, clipped_fc2 = clip_pair(grad_fc1, grad_fc2)
        return (loss_value, clipped_fc1, clipped_fc2)

    def skipped():
        zeros = jnp.zeros((weights[3].shape[0], weights[3].shape[1]), jnp.float32)
        return (jnp.zeros((), jnp.float32), zeros, zeros)

    return lax.cond(chosen == 1, compute, skipped)


def per_device(
    features,
    conv_weight,
    vae_noise,
    flips,
    crops,
    tsteps,
    diffusion_noise,
    selected,
    w_patch,
    w_time,
    w_ada,
    w_fc1,
    w_fc2,
    w_final,
    noise_fc1,
    noise_fc2,
):
    local_rows = features[0]
    side_cells = local_rows.shape[2]
    out_width = conv_weight.shape[3]
    channels = out_width // 2
    whole_images = lax.all_to_all(local_rows, "dp", split_axis=0, concat_axis=1, tiled=True)
    moments = conv_moments(jnp.pad(whole_images, ((0, 0), (1, 1), (0, 0), (0, 0))), conv_weight)
    latent_moments = moments.reshape(moments.shape[0], 1, side_cells * side_cells * out_width)
    full_fc1, full_fc2 = (
        lax.all_gather(w_fc1, "fsdp", axis=1, tiled=True),
        lax.all_gather(w_fc2, "fsdp", axis=1, tiled=True),
    )
    weights = (w_patch, w_time, w_ada, full_fc1, full_fc2, w_final)
    loss_local = jnp.zeros((), jnp.float32)
    summed_fc1 = jnp.zeros(full_fc1.shape, jnp.float32)
    summed_fc2 = jnp.zeros(full_fc2.shape, jnp.float32)
    moment = moments[0]
    loss_value, clipped_fc1, clipped_fc2 = selected_terms(
        selected[0, 0],
        moment[..., :channels],
        moment[..., channels:],
        vae_noise[0, 0],
        flips[0, 0],
        crops[0, 0],
        tsteps[0, 0],
        diffusion_noise[0, 0],
        weights,
    )
    loss_local = loss_local + loss_value
    summed_fc1 = summed_fc1 + clipped_fc1
    summed_fc2 = summed_fc2 + clipped_fc2
    selected_count = selected.shape[0] * lax.axis_size("dp") * lax.axis_size("fsdp") // 2
    owned_fc1, owned_fc2 = (
        lax.psum_scatter(summed_fc1, "fsdp", scatter_dimension=1, tiled=True),
        lax.psum_scatter(summed_fc2, "fsdp", scatter_dimension=1, tiled=True),
    )
    shard_fc1, shard_fc2 = lax.psum((owned_fc1, owned_fc2), "dp")
    loss_all = lax.psum(loss_local, ("dp", "fsdp"))
    update_fc1 = (shard_fc1 + noise_weight * noise_fc1) / selected_count
    update_fc2 = (shard_fc2 + noise_weight * noise_fc2) / selected_count
    return (update_fc1, update_fc2, loss_all / selected_count, latent_moments)


def solution(mesh):
    in_specs = (
        P("fsdp", None, "dp", None, None),
        P(),
        P("dp", "fsdp", None),
        P("dp", "fsdp", None),
        P("dp", "fsdp", None, None),
        P("dp", "fsdp", None),
        P("dp", "fsdp", None, None),
        P("dp", "fsdp"),
        P(),
        P(),
        P(),
        P(None, "fsdp"),
        P(None, "fsdp"),
        P(),
        P(None, "fsdp"),
        P(None, "fsdp"),
    )
    out_specs = (P(None, "fsdp"), P(None, "fsdp"), P(), P("dp", "fsdp", None))
    return jax.shard_map(
        per_device, mesh=mesh, in_specs=in_specs, out_specs=out_specs, check_vma=False
    )
```

profile of v0, /device:TPU:0, one launch (start us, length us, event | category | flops | bytes accessed | tf_op | source)
XLA Modules:
  0.0 316.7 jit_solution(5034264727460269783)
XLA Ops:
  7.2 0.0 copy-start
  7.2 0.0 all-gather.3.cloned.1.call-start
  7.2 0.7 all-gather.3.cloned.1.call-update
  7.9 6.4 %all-to-all-start = ((bf16[8,4,32,512]{3,2,1,0:T(8,128)(2,1)}), bf16[8,4,32,512]{3,2,1,0:T(8,128)(2,1)S(1)}, u32[]{:S(2)}, u32[]{:S(2)}) async-start(bf16[8,4,32,512]{3,2,1,0:T(8,128)(2,1)} %bitcast.106), calls=%async_computation | async-start | bytes 2097152 | tf_op jit(solution)/shard_map/all_to_all | solution.py:195
  14.3 0.0 all-gather.5.cloned.1.call-start
  14.3 0.7 all-gather.5.cloned.1.call-update
  15.0 0.0 reduce-scatter.3.cloned.1.call-start
  15.7 25.1 %all-to-all-done = bf16[8,4,32,512]{3,2,1,0:T(8,128)(2,1)S(1)} async-done(((bf16[8,4,32,512]{3,2,1,0:T(8,128)(2,1)}), bf16[8,4,32,512]{3,2,1,0:T(8,128)(2,1)S(1)}, u32[]{:S(2)}, u32[]{:S(2)}) %all-to-all-start) | async-done | bytes 1048608 | tf_op jit(solution)/shard_map/all_to_all | solution.py:195
  40.8 0.0 copy-done
  40.8 1.0 convolution_bitcast_fusion
  41.8 0.0 copy-start.11
  41.9 0.0 copy-start.18
  41.9 0.0 copy-start.21
  41.9 0.0 copy-start.23
  41.9 0.0 copy-start.26
  41.9 0.0 copy-start.28
  41.9 1.2 add_add_fusion.1
  43.1 0.0 all-gather.3.cloned.1.call-done
  43.1 26.2 %all-gather.5.cloned.1.call-done = bf16[384,1536]{1,0:T(8,128)(2,1)} async-done(((bf16[384,384]{1,0:T(8,128)(2,1)}), bf16[384,1536]{1,0:T(8,128)(2,1)}) %all-gather.5.cloned.1.call-update) | async-done | bytes 1179664 | tf_op jit(solution)/shard_map/all_gather | solution.py:200
  69.3 0.0 copy-done.11
  69.3 0.0 copy-done.18
  69.3 0.0 copy-done.21
  69.3 0.0 copy-done.23
  69.3 0.0 copy-done.26
  69.3 0.0 copy-done.28
  69.3 3.4 %conditional.1 = (f32[]{:T(128)}, f32[384,1536]{1,0:T(8,128)}, f32[384,1536]{1,0:T(8,128)}) conditional(s32[]{:T(128)} %bitcast.12, () %tuple.16, (s32[1,1,4]{2,1,0:T(1,128)S(1)}, s32[1,1,4]{2,1,0:T(1,128)S(1)}, f32[1,32,32,1,1,8]{2,5,4,3,1,0:T(8,128)}, f32[1,32,32,1,1,8]{2,5,4,3,1,0:T(8,128)}, f32[1,32,32,1,1,8]{2,5,4,3,1,0:T(8,128)S(1)}, ...), branch_computations={%region_0.1_spmd, %region_1.14_spmd} | conditional | flops 6159853568 | bytes 172687328 | solution.py:170
  69.4 1.7 broadcast.145.clone
  71.0 1.7 broadcast.145
  72.8 0.0 reduce-scatter.3.cloned.1.call-update
  72.8 0.0 reduce-scatter.5.cloned.1.call-start
  72.8 0.0 copy-start.16
  72.8 0.5 reduce-scatter.5.cloned.1.call-update
  73.4 0.0 copy-start.14
  73.4 0.0 copy-start.15
  73.4 0.0 all-reduce.7.cloned.1.call-start
  73.4 130.4 %reduce-scatter.3.cloned.1.call-done = f32[384,384]{1,0:T(8,128)} async-done(((f32[384,1536]{1,0:T(8,128)}), f32[384,384]{1,0:T(8,128)}) %reduce-scatter.3.cloned.1.call-update) | async-done | bytes 589840 | tf_op jit(solution)/shard_map/reduce_scatter | solution.py:223
  203.9 40.3 %reduce-scatter.5.cloned.1.call-done = f32[384,384]{1,0:T(8,128)} async-done(((f32[384,1536]{1,0:T(8,128)}), f32[384,384]{1,0:T(8,128)}) %reduce-scatter.5.cloned.1.call-update) | async-done | bytes 589840 | tf_op jit(solution)/shard_map/reduce_scatter | solution.py:224
  244.2 0.0 all-reduce.7.cloned.1.call-update
  244.2 40.5 %psum.23 = f32[]{:T(128)} all-reduce(f32[]{:T(128)} %get-tuple-element.93), channel_id=1, replica_groups=mesh['dp'=8,'fsdp'=4] {'dp','fsdp'}, use_global_device_ids=true, to_apply=%region_18.19 | all-reduce | flops 1 | bytes 8 | tf_op jit(solution)/shard_map/psum | solution.py:227
  284.7 0.0 copy-done.16
  284.7 0.2 copy.84
  284.9 0.9 reshape.312
  286.5 20.1 %all-reduce.7.cloned.1.call-done = (f32[384,384]{1,0:T(8,128)}, f32[384,384]{1,0:T(8,128)}) async-done(((f32[384,384]{1,0:T(8,128)}, f32[384,384]{1,0:T(8,128)}), (f32[384,384]{1,0:T(8,128)}, f32[384,384]{1,0:T(8,128)})) %all-reduce.7.cloned.1.call-update) | async-done | bytes 1179664 | tf_op jit(solution)/shard_map/psum | solution.py:226
  306.6 0.0 copy-done.14
  306.6 0.0 copy-done.15
  306.6 2.5 add_multiply_fusion
Async XLA Ops:
  7.2 33.7 %copy-start = (bf16[3,3,512,8]{2,3,1,0:T(8,128)(2,1)S(1)}, bf16[3,3,512,8]{2,3,1,0:T(8,128)(2,1)}, u32[]{:S(2)}) copy-start(bf16[3,3,512,8]{2,3,1,0:T(8,128)(2,1)} %param.19) | copy-start | bytes 221188
  7.2 36.0 %all-gather.3.cloned.1.call-start = ((), (), s32[]{:S(2)}) async-start(), calls=%async_computation.3 | async-start | bytes 1474560 | tf_op jit(solution)/shard_map/all_gather | solution.py:199
  7.9 32.9 %all-to-all-start = ((bf16[8,4,32,512]{3,2,1,0:T(8,128)(2,1)}), bf16[8,4,32,512]{3,2,1,0:T(8,128)(2,1)S(1)}, u32[]{:S(2)}, u32[]{:S(2)}) async-start(bf16[8,4,32,512]{3,2,1,0:T(8,128)(2,1)} %bitcast.106), calls=%async_computation | async-start | bytes 2097152 | tf_op jit(solution)/shard_map/all_to_all | solution.py:195
  14.3 55.0 %all-gather.5.cloned.1.call-start = ((), (), s32[]{:S(2)}) async-start(), calls=%async_computation.4 | async-start | bytes 1474560 | tf_op jit(solution)/shard_map/all_gather | solution.py:200
  15.0 188.8 %reduce-scatter.3.cloned.1.call-start = ((), (), s32[]{:S(2)}) async-start(), calls=%async_computation.5 | async-start | bytes 2949120 | tf_op jit(solution)/shard_map/reduce_scatter | solution.py:223
  41.8 27.5 %copy-start.11 = (bf16[384,1152]{1,0:T(8,128)(2,1)S(1)}, bf16[384,1152]{1,0:T(8,128)(2,1)}, u32[]{:S(2)}) copy-start(bf16[384,1152]{1,0:T(8,128)(2,1)} %param.28) | copy-start | bytes 2654212
  41.9 27.5 %copy-start.18 = (bf16[256,384]{1,0:T(8,128)(2,1)S(1)}, bf16[256,384]{1,0:T(8,128)(2,1)}, u32[]{:S(2)}) copy-start(bf16[256,384]{1,0:T(8,128)(2,1)} %param.27) | copy-start | bytes 589828
  41.9 27.4 %copy-start.21 = (f32[1,1,4096]{2,1,0:T(1,128)S(1)}, f32[1,1,4096]{2,1,0:T(1,128)}, u32[]{:S(2)}) copy-start(f32[1,1,4096]{2,1,0:T(1,128)} %param.20) | copy-start | bytes 49156
  41.9 27.4 %copy-start.23 = (s32[1,1,4,2]{2,3,1,0:T(2,128)S(1)}, s32[1,1,4,2]{2,3,1,0:T(2,128)}, u32[]{:S(2)}) copy-start(s32[1,1,4,2]{2,3,1,0:T(2,128)} %param.22) | copy-start | bytes 100
  41.9 27.4 %copy-start.26 = (s32[1,1,4]{2,1,0:T(1,128)S(1)}, s32[1,1,4]{2,1,0:T(1,128)}, u32[]{:S(2)}) copy-start(s32[1,1,4]{2,1,0:T(1,128)} %param.23) | copy-start | bytes 52
  41.9 27.4 %copy-start.28 = (s32[1,1,4]{2,1,0:T(1,128)S(1)}, s32[1,1,4]{2,1,0:T(1,128)}, u32[]{:S(2)}) copy-start(s32[1,1,4]{2,1,0:T(1,128)} %param.21) | copy-start | bytes 52
  72.8 171.4 %reduce-scatter.5.cloned.1.call-start = ((), (), s32[]{:S(2)}) async-start(), calls=%async_computation.6 | async-start | bytes 2949120 | tf_op jit(solution)/shard_map/reduce_scatter | solution.py:224
  72.8 211.9 %copy-start.16 = (f32[1,32,32,1,1,8]{2,5,4,3,1,0:T(8,128)S(1)}, f32[1,32,32,1,1,8]{2,5,4,3,1,0:T(8,128)}, u32[]{:S(2)}) copy-start(f32[1,32,32,1,1,8]{2,5,4,3,1,0:T(8,128)} %get-tuple-element.230) | copy-start | bytes 98308
  73.4 233.2 %copy-start.14 = (f32[384,384]{1,0:T(8,128)S(1)}, f32[384,384]{1,0:T(8,128)}, u32[]{:S(2)}) copy-start(f32[384,384]{1,0:T(8,128)} %param.33) | copy-start | bytes 1769476
  73.4 233.2 %copy-start.15 = (f32[384,384]{1,0:T(8,128)S(1)}, f32[384,384]{1,0:T(8,128)}, u32[]{:S(2)}) copy-start(f32[384,384]{1,0:T(8,128)} %param.32) | copy-start | bytes 1769476
  73.4 233.2 %all-reduce.7.cloned.1.call-start = ((), (), s32[]{:S(2)}) async-start(), calls=%async_computation.7 | async-start | bytes 2359296 | tf_op jit(solution)/shard_map/psum | solution.py:226
Sparse Core Ops, SparseCore 0:
  9.8 30.1 all-gather.2
  41.8 27.4 all-gather.4
  72.9 130.9 reduce-scatter.2
  206.8 37.3 reduce-scatter.4
  246.4 60.1 all-reduce.6
where the time goes:
time: 317 us
  waiting for transfers between devices  244 us (77%)
  blocking collectives  40.5 us (13%)
  between operations  16.3 us (5%)
  starting transfers between devices  6.56 us (2%)
  local copies, waits for them, and re-layouts  4.58 us (1%)
  other arithmetic  3.67 us (1%)
    reduce_scatter x1, waiting for transfers between devices, per_device(): lax.psum_scatter(summed_fc1, 'fsdp', scatter_dimension=1, tiled=True)  130 us
    psum x1, blocking collectives, per_device(): loss_all = lax.psum(loss_local, ('dp', 'fsdp'))  40.5 us
    reduce_scatter x1, waiting for transfers between devices, per_device(): lax.psum_scatter(summed_fc2, 'fsdp', scatter_dimension=1, tiled=True)  40.3 us
    all_gather x1, waiting for transfers between devices, per_device(): lax.all_gather(w_fc2, 'fsdp', axis=1, tiled=True)  26.2 us
    all_to_all x1, waiting for transfers between devices, per_device(): lax.all_to_all(local_rows, 'dp', split_axis=0, concat_axis=1, tiled=True)  25.1 us
    psum x1, waiting for transfers between devices, per_device(): shard_fc1, shard_fc2 = lax.psum((owned_fc1, owned_fc2), 'dp')  20.1 us
    all_to_all x1, starting transfers between devices, per_device(): lax.all_to_all(local_rows, 'dp', split_axis=0, concat_axis=1, tiled=True)  6.37 us
  transfers between devices with their start and end apart: 6, of which 5 were waited for; matrix products, arithmetic and copies ran while one was open for 1% of the time, Pallas kernels for 0%

commit v1 on v0

v1 whole, which is shorter than its diff:
```python
from functools import partial
import math

import numpy as np

import jax
import jax.numpy as jnp
from jax import lax
from jax.experimental import pallas as pl
from jax.experimental.pallas import tpu as pltpu
from jax.sharding import PartitionSpec as P

TSTEPS = 1000
CORES = 2

clip_offset = 1e-05
noise_weight = 16.0
norm_epsilon = 1e-06

LINK = jnp.bfloat16
HIGHEST = lax.Precision.HIGHEST
F32 = jnp.float32
BF16 = jnp.bfloat16
GELU_C = math.sqrt(2.0 / math.pi)
GELU_A = 0.044715


def noise_tables(horizon):
    beta = np.linspace(0.0001, 0.02, horizon, dtype=np.float32)
    alpha_bar = np.cumprod(np.float32(1.0) - beta, dtype=np.float32)
    return np.stack([np.sqrt(alpha_bar), np.sqrt(np.float32(1.0) - alpha_bar)])


def position_table(side_cells, width):
    quarter = width // 4
    frequency = np.float32(1.0) / np.power(
        np.float32(10000.0), np.arange(quarter, dtype=np.float32) / np.float32(quarter)
    )
    angles = np.arange(side_cells, dtype=np.float32)[:, None] * frequency[None, :]
    line = np.concatenate([np.sin(angles), np.cos(angles)], axis=1).astype(np.float32)
    return np.concatenate(
        [np.repeat(line, side_cells, axis=0), np.tile(line, (side_cells, 1))], axis=1
    )


def time_features(steps_in, width):
    half_width = width // 2
    rates = jnp.exp(-math.log(10000.0) * jnp.arange(half_width, dtype=F32) / half_width)
    phases = steps_in.astype(F32)[:, None] * rates[None, :]
    return jnp.concatenate([jnp.cos(phases), jnp.sin(phases)], axis=1)


def iota(shape, axis):
    return lax.broadcasted_iota(jnp.int32, shape, axis)


def one_hot(condition, dtype):
    return jnp.where(condition, 1.0, 0.0).astype(dtype)


def conv_kernel(rows, side, feat_ref, weight_ref, out_ref, wide_ref):
    images = out_ref.shape[0]
    channels = feat_ref.shape[2]
    outs = weight_ref.shape[2]
    lanes = side * outs
    spread = one_hot(iota((outs, lanes), 1) % outs == iota((outs, lanes), 0), BF16)
    for tap in range(9):
        wide_ref[:, tap * lanes : (tap + 1) * lanes] = jnp.dot(
            weight_ref[tap], spread, preferred_element_type=F32
        ).astype(BF16)
    offset = iota((rows * side, lanes), 1) // outs - iota((rows * side, lanes), 0) % side

    def image(s, carry):
        block = feat_ref[pl.ds(s * rows, rows)].reshape(rows * side, channels)
        out_ref[s] = jnp.zeros(out_ref.shape[1:], F32)
        for row_tap in range(3):
            first = 3 * row_tap * lanes
            products = jnp.dot(
                block, wide_ref[:, first : first + 3 * lanes], preferred_element_type=F32
            )
            placed = jnp.zeros((rows * side, lanes), F32)
            for col_tap in range(3):
                placed = jnp.where(
                    offset == 1 - col_tap,
                    products[:, col_tap * lanes : (col_tap + 1) * lanes],
                    placed,
                )
            line = jnp.sum(placed.reshape(rows, side, lanes), axis=1)
            start = 2 - row_tap
            out_ref[s, start : start + rows, :] += line
        return carry

    lax.fori_loop(0, images, image, 0)


def local_conv(features, conv_weight):
    images, rows, side, channels = features.shape
    outs = conv_weight.shape[3]
    lanes = side * outs
    padded = -(-(rows + 2) // 8) * 8
    return pl.pallas_call(
        partial(conv_kernel, rows, side),
        out_shape=jax.ShapeDtypeStruct((images, padded, lanes), F32),
        in_specs=[pl.BlockSpec(memory_space=pltpu.VMEM)] * 2,
        out_specs=pl.BlockSpec(memory_space=pltpu.VMEM),
        scratch_shapes=[pltpu.VMEM((channels, 9 * lanes), BF16)],
        compiler_params=pltpu.CompilerParams(vmem_limit_bytes=24 << 20),
        cost_estimate=pl.CostEstimate(
            flops=2 * images * rows * lanes * channels * 9,
            bytes_accessed=features.size * 2,
            transcendentals=0,
        ),
        name="local_conv",
    )(features.reshape(images * rows, side, channels), conv_weight.reshape(9, channels, outs))


def row_mean(values):
    return jnp.sum(values, axis=-1, keepdims=True) * (1.0 / values.shape[-1])


def example_kernel(
    rows,
    blocks,
    flags_ref,
    flips_ref,
    crops_ref,
    steps_ref,
    table_ref,
    parts_ref,
    vae_ref,
    noise_ref,
    stamp_ref,
    w_patch_ref,
    w_time_ref,
    w_ada_ref,
    w_final_ref,
    position_ref,
    *rest,
):
    own_fc1, own_fc2 = rest[0], rest[1]
    mine = rest[2 : 2 + blocks - 1]
    theirs = rest[1 + blocks : 2 * blocks]
    outs = rest[2 * blocks :]
    moments_ref, loss_ref = outs[0], outs[1]
    keep_refs = outs[2 : 2 + blocks]
    send_refs = outs[2 + blocks : 2 + 2 * blocks]
    (
        weight_ref,
        mod_ref,
        hidden_ref,
        slope_ref,
        pre_ref,
        branch_ref,
        grad_ref,
        latent_ref,
        modulation_ref,
        patch_ref,
        final_ref,
    ) = outs[2 + 2 * blocks :]

    sources = parts_ref.shape[0]
    lanes = parts_ref.shape[2]
    side = sources * rows
    channels = vae_ref.shape[1] // side
    cells = side * channels
    views = noise_ref.shape[0] * 2 // side
    half = side // 2
    per_view = half * half
    width = w_patch_ref.shape[1]
    piece = own_fc1.shape[1]
    total = piece * blocks
    entries = views * per_view * 4 * channels
    parity = flags_ref[1]

    for source in range(sources):
        moments_ref[source * rows : (source + 1) * rows, :] = parts_ref[source, 1 : rows + 1, :]
    for source in range(sources):
        if source > 0:
            moments_ref[source * rows : source * rows + 1, :] += parts_ref[
                source - 1, rows + 1 : rows + 2, :
            ]
        if source < sources - 1:
            last = (source + 1) * rows - 1
            moments_ref[last : last + 1, :] += parts_ref[source + 1, 0:1, :]

    @pl.when(flags_ref[0] != 1)
    def _():
        loss_ref[...] = jnp.zeros_like(loss_ref)
        for k in range(blocks):
            keep_refs[k][...] = jnp.zeros_like(keep_refs[k])
            send_refs[k][...] = jnp.zeros_like(send_refs[k])

    @pl.when(flags_ref[0] == 1)
    def _():
        weight_ref[0, 0] = own_fc1[...]
        weight_ref[1, 0] = own_fc2[...]
        for k in range(1, blocks):
            weight_ref[parity, k] = mine[k - 1][...]
            weight_ref[1 - parity, k] = theirs[k - 1][...]

        moments = moments_ref[...]
        into, outof = iota((lanes, cells), 0), iota((lanes, cells), 1)
        cell = outof // channels * (2 * channels) + outof % channels
        mean_part = jnp.dot(moments, one_hot(into == cell, F32), precision=HIGHEST)
        logvar = jnp.dot(moments, one_hot(into == cell + channels, F32), precision=HIGHEST)
        latent_ref[...] = mean_part + jnp.exp(0.5 * logvar) * vae_ref[...]

        conditioning = jnp.dot(stamp_ref[...], w_time_ref[...], preferred_element_type=F32)
        conditioning = conditioning * (1.0 / (1.0 + jnp.exp(-conditioning)))
        modulation_ref[...] = jnp.dot(
            conditioning.astype(BF16), w_ada_ref[...], preferred_element_type=F32
        )

        short = 2 * channels
        wide = 2 * cells
        lane, entry = iota((wide, 2 * short), 0), iota((wide, 2 * short), 1)
        spread = one_hot(lane // cells * short + lane % short == entry, BF16)
        patch_ref[...] = jnp.dot(
            spread, w_patch_ref[...], preferred_element_type=F32
        ).astype(BF16)
        final_ref[...] = lax.dot_general(
            w_final_ref[...], spread, (((1,), (1,)), ((), ())), preferred_element_type=F32
        ).astype(BF16)

        in_patch = iota((per_view, wide), 1) % cells // short == iota((per_view, wide), 0) % half

        def view(a, loss_sum):
            keep_part = table_ref[0, steps_ref[a]]
            blend_part = table_ref[1, steps_ref[a]]
            flip = flips_ref[a]
            row_at, col_at = crops_ref[2 * a], crops_ref[2 * a + 1]
            source, target_lane = iota((cells, cells), 0), iota((cells, cells), 1)
            column = target_lane // channels + (col_at - 2)
            valid = (column >= 0) & (column < side)
            column = jnp.where(flip == 1, side - 1 - column, column)
            pick_col = one_hot(
                valid & (source == column * channels + target_lane % channels), F32
            )
            target_row, source_row = iota((side, side), 0), iota((side, side), 1)
            wanted = target_row % half * 2 + target_row // half + (row_at - 2)
            pick_row = one_hot(source_row == wanted, F32)
            moved = jnp.dot(latent_ref[...], pick_col, precision=HIGHEST)
            moved = jnp.dot(pick_row, moved, precision=HIGHEST)
            moved = jnp.concatenate([moved[:half], moved[half:]], axis=1)
            noise = noise_ref[pl.ds(a * half, half), :]
            noised = keep_part * moved + blend_part * noise

            def over_patches(values):
                return jnp.broadcast_to(values[:, None, :], (half, half, wide)).reshape(
                    per_view, wide
                )

            patches = jnp.where(in_patch, over_patches(noised), 0.0).astype(BF16)
            tokens = jnp.dot(patches, patch_ref[...], preferred_element_type=F32)
            tokens = tokens + position_ref[...]
            shift = modulation_ref[pl.ds(a, 1), 0:width]
            scale = modulation_ref[pl.ds(a, 1), width : 2 * width]
            gate = modulation_ref[pl.ds(a, 1), 2 * width : 3 * width]

            center = tokens - row_mean(tokens)
            variance = row_mean(center * center)
            normed = center * lax.rsqrt(variance + norm_epsilon)
            modulated = (normed * (1.0 + scale) + shift).astype(BF16)
            here = pl.ds(a * per_view, per_view)
            mod_ref[here, :] = modulated

            branch = jnp.zeros((per_view, width), F32)
            for k in range(blocks):
                columns = slice(k * piece, (k + 1) * piece)
                x = jnp.dot(modulated, weight_ref[0, k], preferred_element_type=F32)
                square = x * x
                tanh = jnp.tanh(x * (square * (GELU_C * GELU_A) + GELU_C))
                cdf = 0.5 * tanh + 0.5
                hidden = x * cdf
                slope_ref[:, columns] = cdf + (hidden * (1.0 - cdf)) * (
                    square * (6.0 * GELU_C * GELU_A) + 2.0 * GELU_C
                )
                hidden = hidden.astype(BF16)
                hidden_ref[here, columns] = hidden
                branch = branch + lax.dot_general(
                    hidden, weight_ref[1, k], (((1,), (1,)), ((), ())), preferred_element_type=F32
                )
            mixed = tokens + gate * branch

            center = mixed - row_mean(mixed)
            variance = row_mean(center * center)
            inverse = lax.rsqrt(variance + norm_epsilon)
            normed = center * inverse
            predicted = jnp.dot(normed.astype(BF16), final_ref[...], preferred_element_type=F32)
            residue = jnp.where(in_patch, predicted - over_patches(noise), 0.0)
            loss_sum = loss_sum + residue * residue
            grad_pred = (residue * (2.0 / entries)).astype(BF16)
            grad_normed = lax.dot_general(
                grad_pred, final_ref[...], (((1,), (1,)), ((), ())), preferred_element_type=F32
            )
            grad_mixed = inverse * (
                grad_normed - row_mean(grad_normed) - normed * row_mean(grad_normed * normed)
            )
            grad_branch = (gate * grad_mixed).astype(BF16)
            branch_ref[here, :] = grad_branch
            for k in range(blocks):
                columns = slice(k * piece, (k + 1) * piece)
                grad_hidden = jnp.dot(
                    grad_branch, weight_ref[1, k], preferred_element_type=F32
                )
                pre_ref[here, columns] = (slope_ref[:, columns] * grad_hidden).astype(BF16)
            return loss_sum

        loss_sum = lax.fori_loop(0, views, view, jnp.zeros((per_view, wide), F32))
        loss_ref[...] = jnp.broadcast_to(
            jnp.sum(loss_sum, keepdims=True) * (1.0 / entries), loss_ref.shape
        )

        modulated_t = mod_ref[...].T
        branch_t = branch_ref[...].T
        squares = jnp.zeros((1, piece), F32)
        for k in range(blocks):
            columns = slice(k * piece, (k + 1) * piece)
            grad = jnp.dot(modulated_t, pre_ref[:, columns], preferred_element_type=F32)
            grad_ref[0, k] = grad
            squares = squares + jnp.sum(grad * grad, axis=0, keepdims=True)
            grad = jnp.dot(branch_t, hidden_ref[:, columns], preferred_element_type=F32)
            grad_ref[1, k] = grad
            squares = squares + jnp.sum(grad * grad, axis=0, keepdims=True)
        root_mean = jnp.sqrt(jnp.sum(squares, keepdims=True) / (2 * width * total))
        factor = 1.0 / (root_mean + clip_offset)
        for k in range(blocks):
            keep_refs[k][...] = grad_ref[parity, k] * factor
            send_refs[k][...] = (grad_ref[1 - parity, k] * factor).astype(send_refs[k].dtype)


def example_call(scalars, arrays, own, mine, theirs, rows):
    blocks = len(mine) + 1
    parts, vae, noise, stamp, w_patch = arrays[:5]
    lanes = parts.shape[2]
    side = parts.shape[0] * rows
    width = w_patch.shape[1]
    piece = own[0].shape[1]
    views = noise.shape[0] * 2 // side
    tokens = views * side * side // 4
    cells = vae.shape[1]
    vae_lines = vae
    vmem = pl.BlockSpec(memory_space=pltpu.VMEM)
    smem = pl.BlockSpec(memory_space=pltpu.SMEM)
    inputs = list(arrays) + list(own) + list(mine) + list(theirs)
    out_shape = (
        [jax.ShapeDtypeStruct((side, lanes), F32), jax.ShapeDtypeStruct((8, 128), F32)]
        + [jax.ShapeDtypeStruct((width, piece), F32)] * blocks
        + [jax.ShapeDtypeStruct((width, piece), LINK)] * blocks
    )
    total = piece * blocks
    return pl.pallas_call(
        partial(example_kernel, rows, blocks),
        out_shape=out_shape,
        in_specs=[smem] * len(scalars) + [vmem] * len(inputs),
        out_specs=[vmem] * len(out_shape),
        scratch_shapes=[
            pltpu.VMEM((2, blocks, width, piece), BF16),
            pltpu.VMEM((tokens, width), BF16),
            pltpu.VMEM((tokens, total), BF16),
            pltpu.VMEM((tokens // views, total), F32),
            pltpu.VMEM((tokens, total), BF16),
            pltpu.VMEM((tokens, width), BF16),
            pltpu.VMEM((2, blocks, width, piece), F32),
            pltpu.VMEM((side, cells), F32),
            pltpu.VMEM((stamp.shape[0], 3 * width), F32),
            pltpu.VMEM((2 * cells, width), BF16),
            pltpu.VMEM((width, 2 * cells), BF16),
        ],
        compiler_params=pltpu.CompilerParams(vmem_limit_bytes=48 << 20),
        cost_estimate=pl.CostEstimate(
            flops=10 * tokens * width * total,
            bytes_accessed=20 * width * total,
            transcendentals=tokens * total,
        ),
        name="example",
    )(*scalars, *inputs)


def shift(values, axis, flip):
    count = lax.axis_size(axis)
    return lax.ppermute(values, axis, [(i, i ^ flip) for i in range(count)])


def tree_sum(terms):
    while len(terms) > 1:
        terms = [terms[i] + terms[i + 1] for i in range(0, len(terms), 2)]
    return terms[0]


def per_device(
    features,
    conv_weight,
    vae_noise,
    flips,
    crops,
    tsteps,
    diffusion_noise,
    selected,
    w_patch,
    w_time,
    w_ada,
    w_fc1,
    w_fc2,
    w_final,
    noise_fc1,
    noise_fc2,
):
    groups = lax.axis_size("fsdp")
    sources = lax.axis_size("dp")
    parity = lax.axis_index("dp") % CORES
    even = parity == 0
    local_rows = features[0]
    rows, side = local_rows.shape[1], local_rows.shape[2]
    outs = conv_weight.shape[3]
    channels = outs // 2
    width, piece = w_fc1.shape
    views = flips.shape[2]

    own_kind = jnp.where(even, w_fc1, w_fc2)
    mine = [shift(own_kind, "fsdp", k) for k in range(1, groups)]
    theirs = [shift(block, "dp", 1) for block in mine]

    parts = local_conv(local_rows, conv_weight)
    parts = lax.all_to_all(parts, "dp", split_axis=0, concat_axis=0, tiled=True)

    stamp = time_features(tsteps[0, 0], w_time.shape[0]).astype(BF16)
    stamp = jnp.pad(stamp, ((0, 16 - views), (0, 0)))
    flags = jnp.stack([selected[0, 0], parity.astype(jnp.int32)])
    scalars = [
        flags,
        flips[0, 0],
        crops[0, 0].reshape(2 * views),
        tsteps[0, 0],
        jnp.asarray(noise_tables(TSTEPS)),
    ]
    arrays = [
        parts,
        vae_noise.reshape(side, side * channels),
        diffusion_noise.reshape(views * side // 2, 2 * side * channels),
        stamp,
        w_patch,
        w_time,
        w_ada,
        w_final,
        jnp.asarray(position_table(side // 2, width)),
    ]
    own = (w_fc1, w_fc2)
    blocked = piece % 128 == 0
    if not blocked:
        joined = jnp.concatenate([own_kind] + mine, axis=1)
        other = jnp.concatenate([jnp.where(even, w_fc2, w_fc1)] + theirs, axis=1)
        own = (jnp.where(even, joined, other), jnp.where(even, other, joined))
        mine, theirs = [], []
    moments, loss, *grads = example_call(scalars, arrays, own, mine, theirs, rows)
    keep, send = grads[: len(grads) // 2], grads[len(grads) // 2 :]
    if not blocked:
        keep = jnp.split(keep[0], groups, axis=1)
        send = jnp.split(send[0], groups, axis=1)

    loss = loss + shift(loss, "dp", 1)
    pair = [None] * groups
    for k in list(range(groups - 1, -1, -1)):
        pair[k] = keep[k] + shift(send[k], "dp", 1).astype(F32)
    owned = [pair[0]]
    losses = [loss]
    for k in range(1, groups):
        owned.append(shift(pair[k].astype(LINK), "fsdp", k).astype(F32))
        losses.append(shift(loss, "fsdp", k))
    owned = tree_sum(owned)
    loss = tree_sum(losses)
    low = owned.astype(LINK)
    sums = [low.astype(F32)]
    losses = [loss]
    for k in range(1, sources // CORES):
        sums.append(shift(low, "dp", CORES * k).astype(F32))
        losses.append(shift(loss, "dp", CORES * k))
    summed = tree_sum(sums)
    loss_all = tree_sum(losses)[0, 0]
    partner = shift(summed, "dp", 1)

    selected_count = selected.shape[0] * sources * groups // 2
    sum_fc1 = jnp.where(even, summed, partner)
    sum_fc2 = jnp.where(even, partner, summed)
    update_fc1 = (sum_fc1 + noise_weight * noise_fc1) / selected_count
    update_fc2 = (sum_fc2 + noise_weight * noise_fc2) / selected_count
    latent_moments = moments.reshape(1, 1, side * side * outs)
    return (update_fc1, update_fc2, loss_all / selected_count, latent_moments)


def solution(mesh):
    in_specs = (
        P("fsdp", None, "dp", None, None),
        P(),
        P("dp", "fsdp", None),
        P("dp", "fsdp", None),
        P("dp", "fsdp", None, None),
        P("dp", "fsdp", None),
        P("dp", "fsdp", None, None),
        P("dp", "fsdp"),
        P(),
        P(),
        P(),
        P(None, "fsdp"),
        P(None, "fsdp"),
        P(),
        P(None, "fsdp"),
        P(None, "fsdp"),
    )
    out_specs = (P(None, "fsdp"), P(None, "fsdp"), P(), P("dp", "fsdp", None))
    return jax.shard_map(
        per_device, mesh=mesh, in_specs=in_specs, out_specs=out_specs, check_vma=False
    )
```

time: 317 us -> 113 us (0.36)
  waiting for transfers between devices: 244 us -> 45.8 us
  blocking collectives: 40.5 us -> 0 us
  starting transfers between devices: 6.56 us -> 46.8 us
  between operations: 16.3 us -> 3.41 us
  Pallas kernels: 0 us -> 7.63 us
    reduce_scatter x2 -> x0, waiting for transfers between devices: 171 us -> none  [the longest x1 130 us: per_device(): lax.psum_scatter(summed_fc1, 'fsdp', scatter_dimension=1, tiled=True)]
    ppermute x0 -> x24, waiting for transfers between devices: none -> 42.4 us  [shift(): return lax.ppermute(values, axis, [(i, i ^ flip) for i in range(count)])]
    ppermute x0 -> x24, starting transfers between devices: none -> 41.4 us  [shift(): return lax.ppermute(values, axis, [(i, i ^ flip) for i in range(count)])]
    psum x1 -> x0, blocking collectives: 40.5 us -> none  [per_device(): loss_all = lax.psum(loss_local, ('dp', 'fsdp'))]
    all_gather x2 -> x0, waiting for transfers between devices: 26.2 us -> none  [the longest x1 26.2 us: per_device(): lax.all_gather(w_fc2, 'fsdp', axis=1, tiled=True)]
    all_to_all x1, waiting for transfers between devices: 25.1 us -> 3.39 us  [per_device(): parts = lax.all_to_all(parts, 'dp', split_axis=0, concat_axis=0, tiled=True)]
    psum x1 -> x0, waiting for transfers between devices: 20.1 us -> none  [per_device(): shard_fc1, shard_fc2 = lax.psum((owned_fc1, owned_fc2), 'dp')]
    pallas_call x0 -> x2, Pallas kernels: none -> 7.63 us  [the longest x1 5.3 us: local_conv(): pl.pallas_call(partial(conv_kernel, rows, side), out_shape=jax.ShapeDtype...]
  transfers between devices with their start and end apart: 6 -> 25, of which waited for: 5 -> 15; matrix products, arithmetic and copies ran while one was open for 1% -> 3% of each run, Pallas kernels for 0% -> 5%
where the time goes in v1:
time: 113 us; the launch traced here: 112 us
  starting transfers between devices  46.8 us (41%)
  waiting for transfers between devices  45.8 us (41%)
  Pallas kernels  7.63 us (7%)
  local copies, waits for them, and re-layouts  4.92 us (4%)
  other arithmetic  3.74 us (3%)
  between operations  3.41 us (3%)
    ppermute x24, waiting for transfers between devices, shift(): return lax.ppermute(values, axis, [(i, i ^ flip) for i in range(count)])  42.4 us
    ppermute x24, starting transfers between devices, shift(): return lax.ppermute(values, axis, [(i, i ^ flip) for i in range(count)])  41.4 us
    all_to_all x1, starting transfers between devices, per_device(): parts = lax.all_to_all(parts, 'dp', split_axis=0, concat_axis=0, tiled=True)  5.35 us
    pallas_call x1, Pallas kernels, local_conv(): pl.pallas_call(partial(conv_kernel, rows, side), out_shape=jax.ShapeDtype...  5.3 us
    unnamed x35, local copies, waits for them, and re-layouts  3.63 us
    all_to_all x1, waiting for transfers between devices, per_device(): parts = lax.all_to_all(parts, 'dp', split_axis=0, concat_axis=0, tiled=True)  3.39 us
    pallas_call x1, Pallas kernels, example_call(): pl.pallas_call(partial(example_kernel, rows, blocks), out_shape=out_shape...  2.34 us
  transfers between devices with their start and end apart: 25, of which 15 were waited for; matrix products, arithmetic and copies ran while one was open for 3% of the time, Pallas kernels for 5%

profile of v1, /device:TPU:0, one launch (start us, length us, event | category | flops | bytes accessed | tf_op | source)
XLA Modules:
  0.0 112.3 jit_solution(4096485588058118716)
XLA Ops:
  0.7 1.8 %broadcast_select_fusion = bf16[384,384]{1,0:T(8,128)(2,1)} fusion(bf16[384,384]{1,0:T(8,128)(2,1)} %rest_0_.1, bf16[384,384]{1,0:T(8,128)(2,1)} %rest_1_.1, pred[]{:T(512)S(6)} %eq.5), kind=kLoop, calls=%fused_computation.7 | loop fusion | flops 147456 | bytes 884737 | tf_op jit(solution)/shard_map/jit(_where)/select_n | solution.py:420
  2.5 3.9 %collective-permute-start.2 = (bf16[384,384]{1,0:T(8,128)(2,1)}, bf16[384,384]{1,0:T(8,128)(2,1)S(1)}, u32[]{:S(2)}, u32[]{:S(2)}) collective-permute-start(bf16[384,384]{1,0:T(8,128)(2,1)} %broadcast_select_fusion), channel_id=1, source_target_pairs={{0,3},{1,2},{2,1},{3,0},{4,7},{5,6},{6,5},{7,4},{8,11},{9,10},{10,... | collective-permute-start | bytes 884744 | tf_op jit(solution)/shard_map/ppermute | solution.py:382
  6.4 0.5 collective-permute-start.1
  6.9 0.1 collective-permute-start
  7.0 1.4 %copy.26 = bf16[3,3,512,8]{3,2,1,0:T(8,128)(2,1)S(1)} copy(bf16[3,3,512,8]{2,3,1,0:T(8,128)(2,1)} %param.19) | data formatting | bytes 147456 | tf_op args[1]
  8.4 0.0 copy-start.7
  8.4 0.0 copy-start.15
  8.4 0.0 copy-start.14
  8.4 0.0 copy-start.1
  8.5 0.0 copy-start.5
  8.5 0.0 copy-start.6
  8.5 0.0 copy-start.9
  8.5 5.3 %local_conv.1 = f32[8,8,256]{2,1,0:T(8,128)} custom-call(bf16[32,32,512]{2,1,0:T(8,128)(2,1)S(1)} %bitcast.11, bf16[9,512,8]{2,1,0:T(8,128)(2,1)S(1)} %bitcast.10), custom_call_target="tpu_custom_call" | custom-call | flops 75497472 | bytes 1048576 | tf_op jit(solution)/shard_map/local_conv/pallas_call | solution.py:101
  13.8 5.4 %all-to-all-start = ((f32[8,8,256]{2,1,0:T(8,128)}), f32[8,8,256]{2,1,0:T(8,128)S(1)}, u32[]{:S(2)}, u32[]{:S(2)}) async-start(f32[8,8,256]{2,1,0:T(8,128)} %local_conv.1), calls=%async_computation | async-start | bytes 131072 | tf_op jit(solution)/shard_map/all_to_all | solution.py:425
  19.2 0.6 collective-permute-start.5
  19.8 0.2 collective-permute-done.1.rest_3_
  19.9 0.1 collective-permute-start.4
  20.0 0.3 collective-permute-done.rest_2_
  20.3 0.1 collective-permute-start.3
  20.4 0.1 fusion.3
  21.2 0.1 pad_add_fusion.flags_ref
  21.3 0.1 copy.25
  21.4 0.1 reshape_squeeze.6.crops_ref
  21.5 0.1 copy.27.w_final_ref
  21.7 3.4 %all-to-all-done.parts_ref = f32[8,8,256]{2,1,0:T(8,128)S(1)} async-done(((f32[8,8,256]{2,1,0:T(8,128)}), f32[8,8,256]{2,1,0:T(8,128)S(1)}, u32[]{:S(2)}, u32[]{:S(2)}) %all-to-all-start) | async-done | bytes 65568 | tf_op jit(solution)/shard_map/all_to_all | solution.py:425
  25.1 0.0 copy-start.3
  25.1 0.9 copy-done.3
  26.1 1.0 copy-done.8
  27.1 2.3 %example.1 = (f32[32,256]{1,0:T(8,128)S(1)}, f32[8,128]{1,0:T(8,128)S(1)}, f32[384,384]{1,0:T(8,128)S(1)}, f32[384,384]{1,0:T(8,128)S(1)}, f32[384,384]{1,0:T(8,...) custom-call(s32[2]{0:T(128)S(1)} %pad_add_fusion.flags_ref, ...), custom_call_target="tpu_custom_call" | custom-call | flops 6039797760 | bytes 11796480 | tf_op jit(solution)/shard_map/example/pallas_call | solution.py:352
  29.4 18.6 %collective-permute-start.7 = (bf16[384,384]{1,0:T(8,128)(2,1)S(1)}, bf16[384,384]{1,0:T(8,128)(2,1)S(1)}, u32[]{:S(2)}, u32[]{:S(2)}) collective-permute-start(bf16[384,384]{1,0:T(8,128)(2,1)S(1)} %get-tuple-element.17), channel_id=1, source_target_pairs={{0,4},{4,0},{8,12},{12,8},{16,20},{20,16},{24,28},{28,24},{1,5},{5... | collective-permute-start | bytes 884744 | tf_op jit(solution)/shard_map/ppermute | solution.py:382
  48.0 0.5 collective-permute-start.6
  48.5 0.7 collective-permute-done.7
  49.2 0.1 add_convert_fusion.3
  49.3 2.3 %collective-permute-start.8 = (bf16[384,384]{1,0:T(8,128)(2,1)S(1)}, bf16[384,384]{1,0:T(8,128)(2,1)S(1)}, u32[]{:S(2)}, u32[]{:S(2)}) collective-permute-start(bf16[384,384]{1,0:T(8,128)(2,1)S(1)} %add_convert_fusion.3), channel_id=1, source_target_pairs={{0,1},{1,0},{2,3},{3,2},{4,5},{5,4},{6,7},{7,6},{8,9},{9,8},{10,11... | collective-permute-start | bytes 884744 | tf_op jit(solution)/shard_map/ppermute | solution.py:382
  51.5 0.1 add_convert_fusion.2
  51.6 0.1 collective-permute-start.10
  51.7 0.1 add_convert_fusion.1
  51.8 1.8 %collective-permute-start.12 = (bf16[384,384]{1,0:T(8,128)(2,1)S(1)}, bf16[384,384]{1,0:T(8,128)(2,1)S(1)}, u32[]{:S(2)}, u32[]{:S(2)}) collective-permute-start(bf16[384,384]{1,0:T(8,128)(2,1)S(1)} %add_convert_fusion.1), channel_id=1, source_target_pairs={{0,3},{1,2},{2,1},{3,0},{4,7},{5,6},{6,5},{7,4},{8,11},{9,10},{10,... | collective-permute-start | bytes 884744 | tf_op jit(solution)/shard_map/ppermute | solution.py:382
  53.6 5.8 %collective-permute-done.8 = bf16[384,384]{1,0:T(8,128)(2,1)S(1)} collective-permute-done((bf16[384,384]{1,0:T(8,128)(2,1)S(1)}, bf16[384,384]{1,0:T(8,128)(2,1)S(1)}, u32[]{:S(2)}, u32[]{:S(2)}) %collective-permute-start.8) | collective-permute-done | bytes 294944 | tf_op jit(solution)/shard_map/ppermute | solution.py:382
  59.4 7.4 %collective-permute-done.10 = bf16[384,384]{1,0:T(8,128)(2,1)S(1)} collective-permute-done((bf16[384,384]{1,0:T(8,128)(2,1)S(1)}, bf16[384,384]{1,0:T(8,128)(2,1)S(1)}, u32[]{:S(2)}, u32[]{:S(2)}) %collective-permute-start.10) | collective-permute-done | bytes 294944 | tf_op jit(solution)/shard_map/ppermute | solution.py:382
  66.8 0.2 add_convert_fusion
  67.0 0.7 collective-permute-start.15
  67.7 1.3 %collective-permute-start.14 = (bf16[384,384]{1,0:T(8,128)(2,1)S(1)}, bf16[384,384]{1,0:T(8,128)(2,1)S(1)}, u32[]{:S(2)}, u32[]{:S(2)}) collective-permute-start(bf16[384,384]{1,0:T(8,128)(2,1)S(1)} %add_convert_fusion), channel_id=1, source_target_pairs={{0,16},{4,20},{8,24},{12,28},{16,0},{20,4},{24,8},{28,12},{1,17},{... | collective-permute-start | bytes 884744 | tf_op jit(solution)/shard_map/ppermute | solution.py:382
  69.0 2.4 %collective-permute-start.13 = (bf16[384,384]{1,0:T(8,128)(2,1)S(1)}, bf16[384,384]{1,0:T(8,128)(2,1)S(1)}, u32[]{:S(2)}, u32[]{:S(2)}) collective-permute-start(bf16[384,384]{1,0:T(8,128)(2,1)S(1)} %add_convert_fusion), channel_id=1, source_target_pairs={{0,8},{4,12},{8,0},{12,4},{16,24},{20,28},{24,16},{28,20},{1,9},{5... | collective-permute-start | bytes 884744 | tf_op jit(solution)/shard_map/ppermute | solution.py:382
  71.4 7.4 %collective-permute-done.15 = bf16[384,384]{1,0:T(8,128)(2,1)S(1)} collective-permute-done((bf16[384,384]{1,0:T(8,128)(2,1)S(1)}, bf16[384,384]{1,0:T(8,128)(2,1)S(1)}, u32[]{:S(2)}, u32[]{:S(2)}) %collective-permute-start.15) | collective-permute-done | bytes 294944 | tf_op jit(solution)/shard_map/ppermute | solution.py:382
  78.8 15.2 %collective-permute-done.14 = bf16[384,384]{1,0:T(8,128)(2,1)S(1)} collective-permute-done((bf16[384,384]{1,0:T(8,128)(2,1)S(1)}, bf16[384,384]{1,0:T(8,128)(2,1)S(1)}, u32[]{:S(2)}, u32[]{:S(2)}) %collective-permute-start.14) | collective-permute-done | bytes 294944 | tf_op jit(solution)/shard_map/ppermute | solution.py:382
  94.0 0.1 add_add_fusion
  94.2 0.1 collective-permute-start.16
  94.3 0.5 collective-permute-start.17
  94.8 1.5 %collective-permute-done.17 = f32[8,128]{1,0:T(8,128)S(1)} collective-permute-done((f32[8,128]{1,0:T(8,128)S(1)}, f32[8,128]{1,0:T(8,128)S(1)}, u32[]{:S(2)}, u32[]{:S(2)}) %collective-permute-start.17) | collective-permute-done | bytes 4128 | tf_op jit(solution)/shard_map/ppermute | solution.py:382
  96.3 1.3 %collective-permute-start.20 = (f32[8,128]{1,0:T(8,128)S(1)}, f32[8,128]{1,0:T(8,128)S(1)}, u32[]{:S(2)}, u32[]{:S(2)}) collective-permute-start(f32[8,128]{1,0:T(8,128)S(1)} %add.76), channel_id=1, source_target_pairs={{0,3},{1,2},{2,1},{3,0},{4,7},{5,6},{6,5},{7,4},{8,11},{9,10},{10,... | collective-permute-start | bytes 12296 | tf_op jit(solution)/shard_map/ppermute | solution.py:382
  97.5 1.6 %collective-permute-start.19 = (f32[8,128]{1,0:T(8,128)S(1)}, f32[8,128]{1,0:T(8,128)S(1)}, u32[]{:S(2)}, u32[]{:S(2)}) collective-permute-start(f32[8,128]{1,0:T(8,128)S(1)} %add.76), channel_id=1, source_target_pairs={{0,2},{1,3},{2,0},{3,1},{4,6},{5,7},{6,4},{7,5},{8,10},{9,11},{10,... | collective-permute-start | bytes 12296 | tf_op jit(solution)/shard_map/ppermute | solution.py:382
  99.2 0.6 collective-permute-start.18
  99.8 1.0 collective-permute-done.20
  100.8 0.4 collective-permute-done.19
  101.1 1.6 %collective-permute-done.18 = f32[8,128]{1,0:T(8,128)S(1)} collective-permute-done((f32[8,128]{1,0:T(8,128)S(1)}, f32[8,128]{1,0:T(8,128)S(1)}, u32[]{:S(2)}, u32[]{:S(2)}) %collective-permute-start.18) | collective-permute-done | bytes 4128 | tf_op jit(solution)/shard_map/ppermute | solution.py:382
  102.8 1.2 %collective-permute-start.23 = (f32[8,128]{1,0:T(8,128)S(1)}, f32[8,128]{1,0:T(8,128)S(1)}, u32[]{:S(2)}, u32[]{:S(2)}) collective-permute-start(f32[8,128]{1,0:T(8,128)S(1)} %add_add_fusion.2), channel_id=1, source_target_pairs={{0,24},{4,28},{8,16},{12,20},{16,8},{20,12},{24,0},{28,4},{1,25},{... | collective-permute-start | bytes 12296 | tf_op jit(solution)/shard_map/ppermute | solution.py:382
  104.0 3.2 %collective-permute-start.21 = (f32[8,128]{1,0:T(8,128)S(1)}, f32[8,128]{1,0:T(8,128)S(1)}, u32[]{:S(2)}, u32[]{:S(2)}) collective-permute-start(f32[8,128]{1,0:T(8,128)S(1)} %add_add_fusion.2), channel_id=1, source_target_pairs={{0,8},{4,12},{8,0},{12,4},{16,24},{20,28},{24,16},{28,20},{1,9},{5... | collective-permute-start | bytes 12296 | tf_op jit(solution)/shard_map/ppermute | solution.py:382
  107.2 0.6 reshape.35
  107.8 0.4 collective-permute-done.23
  108.2 0.3 collective-permute-done.22
  108.5 0.3 collective-permute-done.21
  108.8 0.5 slice.3
  110.0 1.2 %add_multiply_fusion = (f32[384,384]{1,0:T(8,128)}, f32[384,384]{1,0:T(8,128)}) fusion(f32[384,384]{1,0:T(8,128)S(1)} %copy-done.11, f32[384,384]{1,0:T(8,128)S(1)} %collective-permute-done.16, f32[384,384]{1,0:T(8,128)S(1)} %add_add_fusion, pred[]{:T(512)S(6)} %eq.5, f32[384,384]{1,0:T(8,128)S(1)} %copy-done.12), kind=kLoop, calls=%fused_computation | loop fusion | flops 1179648 | bytes 3538945 | tf_op jit(solution)/shard_map/div | solution.py:486
  (42 shorter events, 0.2 us)
Async XLA Ops:
  0.6 7.7 %copy-start = (bf16[1,8,4,32,512]{4,3,2,1,0:T(8,128)(2,1)S(1)}, bf16[1,8,4,32,512]{4,3,2,1,0:T(8,128)(2,1)}, u32[]{:S(2)}) copy-start(bf16[1,8,4,32,512]{4,3,2,1,0:T(8,128)(2,1)} %param.18) | copy-start | bytes 3145732
  2.5 16.7 %collective-permute-start.2 = (bf16[384,384]{1,0:T(8,128)(2,1)}, bf16[384,384]{1,0:T(8,128)(2,1)S(1)}, u32[]{:S(2)}, u32[]{:S(2)}) collective-permute-start(bf16[384,384]{1,0:T(8,128)(2,1)} %broadcast_select_fusion), channel_id=1, source_target_pairs={{0,3},{1,2},{2,1},{3,0},{4,7},{5,6},{6,5},{7,4},{8,11},{9,10},{10,... | collective-permute-start | bytes 884744 | tf_op jit(solution)/shard_map/ppermute | solution.py:382
  6.4 13.5 %collective-permute-start.1 = (bf16[384,384]{1,0:T(8,128)(2,1)}, bf16[384,384]{1,0:T(8,128)(2,1)S(1)}, u32[]{:S(2)}, u32[]{:S(2)}) collective-permute-start(bf16[384,384]{1,0:T(8,128)(2,1)} %broadcast_select_fusion), channel_id=1, source_target_pairs={{0,2},{1,3},{2,0},{3,1},{4,6},{5,7},{6,4},{7,5},{8,10},{9,11},{10,... | collective-permute-start | bytes 884744 | tf_op jit(solution)/shard_map/ppermute | solution.py:382
  6.9 13.4 %collective-permute-start = (bf16[384,384]{1,0:T(8,128)(2,1)}, bf16[384,384]{1,0:T(8,128)(2,1)}, u32[]{:S(2)}, u32[]{:S(2)}) collective-permute-start(bf16[384,384]{1,0:T(8,128)(2,1)} %broadcast_select_fusion), channel_id=1, source_target_pairs={{0,1},{1,0},{2,3},{3,2},{4,5},{5,4},{6,7},{7,6},{8,9},{9,8},{10,11... | collective-permute-start | bytes 884744 | tf_op jit(solution)/shard_map/ppermute | solution.py:382
  8.4 10.8 %copy-start.7 = (s32[1,1,4]{2,1,0:T(1,128)S(1)}, s32[1,1,4]{2,1,0:T(1,128)}, u32[]{:S(2)}) copy-start(s32[1,1,4]{2,1,0:T(1,128)} %param.23) | copy-start | bytes 52
  8.4 12.9 %copy-start.15 = (s32[1,1,4,2]{2,3,1,0:T(2,128)S(1)}, s32[1,1,4,2]{2,3,1,0:T(2,128)}, u32[]{:S(2)}) copy-start(s32[1,1,4,2]{2,3,1,0:T(2,128)} %param.22) | copy-start | bytes 100
  8.4 13.1 %copy-start.13 = (f32[1,1,4,4096]{3,2,1,0:T(4,128)S(1)}, f32[1,1,4,4096]{3,2,1,0:T(4,128)}, u32[]{:S(2)}) copy-start(f32[1,1,4,4096]{3,2,1,0:T(4,128)} %param.24) | copy-start | bytes 196612
  8.4 13.1 %copy-start.14 = (bf16[384,16]{0,1:T(8,128)(2,1)S(1)}, bf16[384,16]{0,1:T(8,128)(2,1)}, u32[]{:S(2)}) copy-start(bf16[384,16]{0,1:T(8,128)(2,1)} %param.31) | copy-start | bytes 36868
  8.4 16.7 %copy-start.1 = (bf16[384,384]{1,0:T(8,128)(2,1)S(1)}, bf16[384,384]{1,0:T(8,128)(2,1)}, u32[]{:S(2)}) copy-start(bf16[384,384]{1,0:T(8,128)(2,1)} %rest_0_.1) | copy-start | bytes 884740
  8.4 16.7 %copy-start.2 = (bf16[384,384]{1,0:T(8,128)(2,1)S(1)}, bf16[384,384]{1,0:T(8,128)(2,1)}, u32[]{:S(2)}) copy-start(bf16[384,384]{1,0:T(8,128)(2,1)} %rest_1_.1) | copy-start | bytes 884740
  8.4 16.7 %copy-start.4 = (f32[1,1,4096]{2,1,0:T(1,128)S(1)}, f32[1,1,4096]{2,1,0:T(1,128)}, u32[]{:S(2)}) copy-start(f32[1,1,4096]{2,1,0:T(1,128)} %param.20) | copy-start | bytes 49156
  8.5 16.7 %copy-start.5 = (bf16[16,384]{1,0:T(8,128)(2,1)S(1)}, bf16[16,384]{1,0:T(8,128)(2,1)}, u32[]{:S(2)}) copy-start(bf16[16,384]{1,0:T(8,128)(2,1)} %w_patch_ref.1) | copy-start | bytes 36868
  8.5 16.6 %copy-start.6 = (s32[1,1,4]{2,1,0:T(1,128)S(1)}, s32[1,1,4]{2,1,0:T(1,128)}, u32[]{:S(2)}) copy-start(s32[1,1,4]{2,1,0:T(1,128)} %param.21) | copy-start | bytes 52
  8.5 16.6 %copy-start.9 = (f32[2,1000]{1,0:T(2,128)S(1)}, f32[2,1000]{1,0:T(2,128)}, u32[]{:S(2)}) copy-start(f32[2,1000]{1,0:T(2,128)} %constant.40.clone.table_ref) | copy-start | bytes 24004
  13.8 11.3 %all-to-all-start = ((f32[8,8,256]{2,1,0:T(8,128)}), f32[8,8,256]{2,1,0:T(8,128)S(1)}, u32[]{:S(2)}, u32[]{:S(2)}) async-start(f32[8,8,256]{2,1,0:T(8,128)} %local_conv.1), calls=%async_computation | async-start | bytes 131072 | tf_op jit(solution)/shard_map/all_to_all | solution.py:425
  19.2 5.9 %collective-permute-start.5 = (bf16[384,384]{1,0:T(8,128)(2,1)S(1)}, bf16[384,384]{1,0:T(8,128)(2,1)S(1)}, u32[]{:S(2)}, u32[]{:S(2)}) collective-permute-start(bf16[384,384]{1,0:T(8,128)(2,1)S(1)} %collective-permute-done.2.rest_4_), channel_id=1, source_target_pairs={{0,4},{4,0},{8,12},{12,8},{16,20},{20,16},{24,28},{28,24},{1,5},{5... | collective-permute-start | bytes 884744 | tf_op jit(solution)/shard_map/ppermute | solution.py:382
  19.9 5.2 %collective-permute-start.4 = (bf16[384,384]{1,0:T(8,128)(2,1)S(1)}, bf16[384,384]{1,0:T(8,128)(2,1)S(1)}, u32[]{:S(2)}, u32[]{:S(2)}) collective-permute-start(bf16[384,384]{1,0:T(8,128)(2,1)S(1)} %collective-permute-done.1.rest_3_), channel_id=1, source_target_pairs={{0,4},{4,0},{8,12},{12,8},{16,20},{20,16},{24,28},{28,24},{1,5},{5... | collective-permute-start | bytes 884744 | tf_op jit(solution)/shard_map/ppermute | solution.py:382
  20.3 4.8 %collective-permute-start.3 = (bf16[384,384]{1,0:T(8,128)(2,1)}, bf16[384,384]{1,0:T(8,128)(2,1)S(1)}, u32[]{:S(2)}, u32[]{:S(2)}) collective-permute-start(bf16[384,384]{1,0:T(8,128)(2,1)} %collective-permute-done.rest_2_), channel_id=1, source_target_pairs={{0,4},{4,0},{8,12},{12,8},{16,20},{20,16},{24,28},{28,24},{1,5},{5... | collective-permute-start | bytes 884744 | tf_op jit(solution)/shard_map/ppermute | solution.py:382
  25.1 0.9 copy-start.3
  26.1 1.0 copy-start.8
  29.4 19.8 %collective-permute-start.7 = (bf16[384,384]{1,0:T(8,128)(2,1)S(1)}, bf16[384,384]{1,0:T(8,128)(2,1)S(1)}, u32[]{:S(2)}, u32[]{:S(2)}) collective-permute-start(bf16[384,384]{1,0:T(8,128)(2,1)S(1)} %get-tuple-element.17), channel_id=1, source_target_pairs={{0,4},{4,0},{8,12},{12,8},{16,20},{20,16},{24,28},{28,24},{1,5},{5... | collective-permute-start | bytes 884744 | tf_op jit(solution)/shard_map/ppermute | solution.py:382
  48.0 3.6 %collective-permute-start.9 = (bf16[384,384]{1,0:T(8,128)(2,1)S(1)}, bf16[384,384]{1,0:T(8,128)(2,1)S(1)}, u32[]{:S(2)}, u32[]{:S(2)}) collective-permute-start(bf16[384,384]{1,0:T(8,128)(2,1)S(1)} %get-tuple-element.19), channel_id=1, source_target_pairs={{0,4},{4,0},{8,12},{12,8},{16,20},{20,16},{24,28},{28,24},{1,5},{5... | collective-permute-start | bytes 884744 | tf_op jit(solution)/shard_map/ppermute | solution.py:382
  48.0 5.6 %collective-permute-start.6 = (bf16[384,384]{1,0:T(8,128)(2,1)S(1)}, bf16[384,384]{1,0:T(8,128)(2,1)S(1)}, u32[]{:S(2)}, u32[]{:S(2)}) collective-permute-start(bf16[384,384]{1,0:T(8,128)(2,1)S(1)} %get-tuple-element.15), channel_id=1, source_target_pairs={{0,4},{4,0},{8,12},{12,8},{16,20},{20,16},{24,28},{28,24},{1,5},{5... | collective-permute-start | bytes 884744 | tf_op jit(solution)/shard_map/ppermute | solution.py:382
  48.5 3.2 %collective-permute-start.11 = (bf16[384,384]{1,0:T(8,128)(2,1)S(1)}, bf16[384,384]{1,0:T(8,128)(2,1)S(1)}, u32[]{:S(2)}, u32[]{:S(2)}) collective-permute-start(bf16[384,384]{1,0:T(8,128)(2,1)S(1)} %get-tuple-element.21), channel_id=1, source_target_pairs={{0,4},{4,0},{8,12},{12,8},{16,20},{20,16},{24,28},{28,24},{1,5},{5... | collective-permute-start | bytes 884744 | tf_op jit(solution)/shard_map/ppermute | solution.py:382
  49.2 2.5 %copy-start.10 = (f32[384,384]{1,0:T(8,128)S(1)}, f32[384,384]{1,0:T(8,128)}, u32[]{:S(2)}) copy-start(f32[384,384]{1,0:T(8,128)} %get-tuple-element.20) | copy-start | bytes 1769476
  49.3 10.1 %collective-permute-start.8 = (bf16[384,384]{1,0:T(8,128)(2,1)S(1)}, bf16[384,384]{1,0:T(8,128)(2,1)S(1)}, u32[]{:S(2)}, u32[]{:S(2)}) collective-permute-start(bf16[384,384]{1,0:T(8,128)(2,1)S(1)} %add_convert_fusion.3), channel_id=1, source_target_pairs={{0,1},{1,0},{2,3},{3,2},{4,5},{5,4},{6,7},{7,6},{8,9},{9,8},{10,11... | collective-permute-start | bytes 884744 | tf_op jit(solution)/shard_map/ppermute | solution.py:382
  51.6 15.2 %collective-permute-start.10 = (bf16[384,384]{1,0:T(8,128)(2,1)S(1)}, bf16[384,384]{1,0:T(8,128)(2,1)S(1)}, u32[]{:S(2)}, u32[]{:S(2)}) collective-permute-start(bf16[384,384]{1,0:T(8,128)(2,1)S(1)} %add_convert_fusion.2), channel_id=1, source_target_pairs={{0,2},{1,3},{2,0},{3,1},{4,6},{5,7},{6,4},{7,5},{8,10},{9,11},{10,... | collective-permute-start | bytes 884744 | tf_op jit(solution)/shard_map/ppermute | solution.py:382
  51.8 15.0 %collective-permute-start.12 = (bf16[384,384]{1,0:T(8,128)(2,1)S(1)}, bf16[384,384]{1,0:T(8,128)(2,1)S(1)}, u32[]{:S(2)}, u32[]{:S(2)}) collective-permute-start(bf16[384,384]{1,0:T(8,128)(2,1)S(1)} %add_convert_fusion.1), channel_id=1, source_target_pairs={{0,3},{1,2},{2,1},{3,0},{4,7},{5,6},{6,5},{7,4},{8,11},{9,10},{10,... | collective-permute-start | bytes 884744 | tf_op jit(solution)/shard_map/ppermute | solution.py:382
  67.0 43.0 %copy-start.11 = (f32[384,384]{1,0:T(8,128)S(1)}, f32[384,384]{1,0:T(8,128)}, u32[]{:S(2)}) copy-start(f32[384,384]{1,0:T(8,128)} %param.33) | copy-start | bytes 1769476
  67.0 43.0 %copy-start.12 = (f32[384,384]{1,0:T(8,128)S(1)}, f32[384,384]{1,0:T(8,128)}, u32[]{:S(2)}) copy-start(f32[384,384]{1,0:T(8,128)} %param.32) | copy-start | bytes 1769476
  67.0 11.8 %collective-permute-start.15 = (bf16[384,384]{1,0:T(8,128)(2,1)S(1)}, bf16[384,384]{1,0:T(8,128)(2,1)S(1)}, u32[]{:S(2)}, u32[]{:S(2)}) collective-permute-start(bf16[384,384]{1,0:T(8,128)(2,1)S(1)} %add_convert_fusion), channel_id=1, source_target_pairs={{0,24},{4,28},{8,16},{12,20},{16,8},{20,12},{24,0},{28,4},{1,25},{... | collective-permute-start | bytes 884744 | tf_op jit(solution)/shard_map/ppermute | solution.py:382
  67.7 26.3 %collective-permute-start.14 = (bf16[384,384]{1,0:T(8,128)(2,1)S(1)}, bf16[384,384]{1,0:T(8,128)(2,1)S(1)}, u32[]{:S(2)}, u32[]{:S(2)}) collective-permute-start(bf16[384,384]{1,0:T(8,128)(2,1)S(1)} %add_convert_fusion), channel_id=1, source_target_pairs={{0,16},{4,20},{8,24},{12,28},{16,0},{20,4},{24,8},{28,12},{1,17},{... | collective-permute-start | bytes 884744 | tf_op jit(solution)/shard_map/ppermute | solution.py:382
  69.0 25.0 %collective-permute-start.13 = (bf16[384,384]{1,0:T(8,128)(2,1)S(1)}, bf16[384,384]{1,0:T(8,128)(2,1)S(1)}, u32[]{:S(2)}, u32[]{:S(2)}) collective-permute-start(bf16[384,384]{1,0:T(8,128)(2,1)S(1)} %add_convert_fusion), channel_id=1, source_target_pairs={{0,8},{4,12},{8,0},{12,4},{16,24},{20,28},{24,16},{28,20},{1,9},{5... | collective-permute-start | bytes 884744 | tf_op jit(solution)/shard_map/ppermute | solution.py:382
  94.2 15.7 %collective-permute-start.16 = (f32[384,384]{1,0:T(8,128)S(1)}, f32[384,384]{1,0:T(8,128)S(1)}, u32[]{:S(2)}, u32[]{:S(2)}) collective-permute-start(f32[384,384]{1,0:T(8,128)S(1)} %add_add_fusion), channel_id=1, source_target_pairs={{0,4},{4,0},{8,12},{12,8},{16,20},{20,16},{24,28},{28,24},{1,5},{5... | collective-permute-start | bytes 1769480 | tf_op jit(solution)/shard_map/ppermute | solution.py:382
  94.3 2.0 %collective-permute-start.17 = (f32[8,128]{1,0:T(8,128)S(1)}, f32[8,128]{1,0:T(8,128)S(1)}, u32[]{:S(2)}, u32[]{:S(2)}) collective-permute-start(f32[8,128]{1,0:T(8,128)S(1)} %get-tuple-element.22), channel_id=1, source_target_pairs={{0,4},{4,0},{8,12},{12,8},{16,20},{20,16},{24,28},{28,24},{1,5},{5... | collective-permute-start | bytes 12296 | tf_op jit(solution)/shard_map/ppermute | solution.py:382
  96.3 4.5 %collective-permute-start.20 = (f32[8,128]{1,0:T(8,128)S(1)}, f32[8,128]{1,0:T(8,128)S(1)}, u32[]{:S(2)}, u32[]{:S(2)}) collective-permute-start(f32[8,128]{1,0:T(8,128)S(1)} %add.76), channel_id=1, source_target_pairs={{0,3},{1,2},{2,1},{3,0},{4,7},{5,6},{6,5},{7,4},{8,11},{9,10},{10,... | collective-permute-start | bytes 12296 | tf_op jit(solution)/shard_map/ppermute | solution.py:382
  97.5 3.6 %collective-permute-start.19 = (f32[8,128]{1,0:T(8,128)S(1)}, f32[8,128]{1,0:T(8,128)S(1)}, u32[]{:S(2)}, u32[]{:S(2)}) collective-permute-start(f32[8,128]{1,0:T(8,128)S(1)} %add.76), channel_id=1, source_target_pairs={{0,2},{1,3},{2,0},{3,1},{4,6},{5,7},{6,4},{7,5},{8,10},{9,11},{10,... | collective-permute-start | bytes 12296 | tf_op jit(solution)/shard_map/ppermute | solution.py:382
  99.2 3.6 %collective-permute-start.18 = (f32[8,128]{1,0:T(8,128)S(1)}, f32[8,128]{1,0:T(8,128)S(1)}, u32[]{:S(2)}, u32[]{:S(2)}) collective-permute-start(f32[8,128]{1,0:T(8,128)S(1)} %add.76), channel_id=1, source_target_pairs={{0,1},{1,0},{2,3},{3,2},{4,5},{5,4},{6,7},{7,6},{8,9},{9,8},{10,11... | collective-permute-start | bytes 12296 | tf_op jit(solution)/shard_map/ppermute | solution.py:382
  102.8 5.4 %collective-permute-start.23 = (f32[8,128]{1,0:T(8,128)S(1)}, f32[8,128]{1,0:T(8,128)S(1)}, u32[]{:S(2)}, u32[]{:S(2)}) collective-permute-start(f32[8,128]{1,0:T(8,128)S(1)} %add_add_fusion.2), channel_id=1, source_target_pairs={{0,24},{4,28},{8,16},{12,20},{16,8},{20,12},{24,0},{28,4},{1,25},{... | collective-permute-start | bytes 12296 | tf_op jit(solution)/shard_map/ppermute | solution.py:382
  104.0 4.5 %collective-permute-start.22 = (f32[8,128]{1,0:T(8,128)S(1)}, f32[8,128]{1,0:T(8,128)S(1)}, u32[]{:S(2)}, u32[]{:S(2)}) collective-permute-start(f32[8,128]{1,0:T(8,128)S(1)} %add_add_fusion.2), channel_id=1, source_target_pairs={{0,16},{4,20},{8,24},{12,28},{16,0},{20,4},{24,8},{28,12},{1,17},{... | collective-permute-start | bytes 12296 | tf_op jit(solution)/shard_map/ppermute | solution.py:382
  104.0 4.8 %collective-permute-start.21 = (f32[8,128]{1,0:T(8,128)S(1)}, f32[8,128]{1,0:T(8,128)S(1)}, u32[]{:S(2)}, u32[]{:S(2)}) collective-permute-start(f32[8,128]{1,0:T(8,128)S(1)} %add_add_fusion.2), channel_id=1, source_target_pairs={{0,8},{4,12},{8,0},{12,4},{16,24},{20,28},{24,16},{28,20},{1,9},{5... | collective-permute-start | bytes 12296 | tf_op jit(solution)/shard_map/ppermute | solution.py:382

commit v2 on v1

v2 whole, which is shorter than its diff:
```python
from functools import partial
import math

import numpy as np

import jax
import jax.numpy as jnp
from jax import lax
from jax.experimental import pallas as pl
from jax.experimental.pallas import tpu as pltpu
from jax.sharding import PartitionSpec as P


TSTEPS = 1000
CORES = 2

clip_offset = 1e-05
noise_weight = 16.0
norm_epsilon = 1e-06

LINK = jnp.float16
LINK_EXPONENT, LINK_MANTISSA = jnp.finfo(LINK).nexp, jnp.finfo(LINK).nmant
HIGHEST = lax.Precision.HIGHEST
F32 = jnp.float32
BF16 = jnp.bfloat16
GELU_C = math.sqrt(2.0 / math.pi)
GELU_A = 0.044715


def noise_tables(horizon):
    beta = np.linspace(0.0001, 0.02, horizon, dtype=np.float32)
    alpha_bar = np.cumprod(np.float32(1.0) - beta, dtype=np.float32)
    return np.stack([np.sqrt(alpha_bar), np.sqrt(np.float32(1.0) - alpha_bar)])


def position_table(side_cells, width):
    quarter = width // 4
    frequency = np.float32(1.0) / np.power(
        np.float32(10000.0), np.arange(quarter, dtype=np.float32) / np.float32(quarter)
    )
    angles = np.arange(side_cells, dtype=np.float32)[:, None] * frequency[None, :]
    line = np.concatenate([np.sin(angles), np.cos(angles)], axis=1).astype(np.float32)
    blank = np.zeros_like(line)
    return np.stack(
        [np.concatenate([line, blank], axis=1), np.concatenate([blank, line], axis=1)]
    )


def constants(side_cells, width, features):
    half = features // 2
    rates = np.exp(-math.log(10000.0) * np.arange(half, dtype=np.float32) / np.float32(half))
    lines = position_table(side_cells, width)
    rates = np.pad(rates.astype(np.float32), (0, width - half))
    return np.concatenate([lines, np.broadcast_to(rates, lines[:1].shape)]).astype(np.float32)


def iota(shape, axis):
    return lax.broadcasted_iota(jnp.int32, shape, axis)


def one_hot(condition, dtype):
    return jnp.where(condition, 1.0, 0.0).astype(dtype)


def split_float(values):
    high = values.astype(BF16)
    rest = values - high.astype(F32)
    middle = rest.astype(BF16)
    return high, middle, (rest - middle.astype(F32)).astype(BF16)


def conv_kernel(rows, side, outs, feat_ref, weight_ref, out_ref):
    images = out_ref.shape[0]
    cells, channels = feat_ref.shape
    lanes = side * outs
    taps = 128
    weights = jnp.concatenate(
        [weight_ref[...], jnp.zeros((taps - 9 * outs, channels), BF16)], axis=0
    )
    products = lax.dot_general(
        feat_ref[...], weights, (((1,), (1,)), ((), ())), preferred_element_type=F32
    )
    zero_row = jnp.zeros((1, taps), F32)
    before = jnp.concatenate([zero_row, products[: cells - 1]], axis=0)
    after = jnp.concatenate([products[1:], zero_row], axis=0)
    column = iota((cells, taps), 0) % side
    tap = iota((cells, taps), 1) // outs % 3
    chosen = jnp.where(
        tap == 1,
        products,
        jnp.where(
            tap == 0,
            jnp.where(column == 0, 0.0, before),
            jnp.where(column == side - 1, 0.0, after),
        ),
    )
    source, target = iota((taps, 3 * lanes), 0), iota((taps, 3 * lanes), 1)
    wanted = (source // (3 * outs) == target // lanes) & (source % outs == target % outs)
    spread = one_hot(wanted & (source < 9 * outs), BF16)
    wide = jnp.zeros((cells, 3 * lanes), F32)
    for part in split_float(chosen):
        wide = wide + jnp.dot(part, spread, preferred_element_type=F32)
    own = iota((cells, lanes), 1) // outs == iota((cells, lanes), 0) % side
    out_ref[...] = jnp.zeros(out_ref.shape, F32)
    for row_tap in range(3):
        placed = jnp.where(own, wide[:, row_tap * lanes : (row_tap + 1) * lanes], 0.0)
        line = jnp.sum(placed.reshape(images * rows, side, lanes), axis=1)
        line = line.reshape(images, rows, lanes)
        start = 2 - row_tap
        for s in range(images):
            out_ref[s, start : start + rows, :] += line[s]


def local_conv(features, conv_weight):
    images, rows, side, channels = features.shape
    outs = conv_weight.shape[3]
    lanes = side * outs
    padded = -(-(rows + 2) // 8) * 8
    weight = conv_weight.transpose(0, 1, 3, 2).reshape(9 * outs, channels)
    return pl.pallas_call(
        partial(conv_kernel, rows, side, outs),
        out_shape=jax.ShapeDtypeStruct((images, padded, lanes), F32),
        in_specs=[pl.BlockSpec(memory_space=pltpu.VMEM)] * 2,
        out_specs=pl.BlockSpec(memory_space=pltpu.VMEM),
        compiler_params=pltpu.CompilerParams(vmem_limit_bytes=24 << 20),
        cost_estimate=pl.CostEstimate(
            flops=2 * images * rows * lanes * channels * 9,
            bytes_accessed=features.size * 2,
            transcendentals=0,
        ),
        name="local_conv",
    )(features.reshape(images * rows * side, channels), weight)


def row_mean(values):
    return jnp.sum(values, axis=-1, keepdims=True) * (1.0 / values.shape[-1])


def patch_mask(per_view, half, wide, short):
    cells = wide // 2
    return iota((per_view, wide), 1) % cells // short == iota((per_view, wide), 0) % half


def over_patches(values):
    half, wide = values.shape
    return jnp.broadcast_to(values[:, None, :], (half, half, wide)).reshape(half * half, wide)


def prepare_kernel(
    side,
    flips_ref,
    crops_ref,
    steps_ref,
    table_ref,
    constant_hbm,
    noise_hbm,
    w_patch_hbm,
    w_time_hbm,
    w_ada_hbm,
    w_final_hbm,
    modulation_ref,
    patch_ref,
    final_ref,
    place_ref,
    noise_ref,
    column_ref,
    row_ref,
    constant_ref,
    raw_noise_ref,
    w_patch_ref,
    w_time_ref,
    w_ada_ref,
    w_final_ref,
    sems,
):
    views = steps_ref.shape[0]
    half = side // 2
    wide = noise_ref.shape[1]
    cells = wide // 2
    short = cells // half
    channels = short // 2
    width = w_patch_ref.shape[1]
    half_freq = w_time_ref.shape[0] // 2
    sources = (constant_hbm, noise_hbm, w_patch_hbm, w_time_hbm, w_ada_hbm, w_final_hbm)
    targets = (constant_ref, raw_noise_ref, w_patch_ref, w_time_ref, w_ada_ref, w_final_ref)
    copies = [
        pltpu.make_async_copy(source, target, sems.at[n])
        for n, (source, target) in enumerate(zip(sources, targets))
    ]
    for copy in copies:
        copy.start()

    source, target = iota((cells, cells), 0), iota((cells, cells), 1)
    target_row, source_row = iota((side, side), 0), iota((side, side), 1)
    for a in range(views):
        column = target // channels + (crops_ref[1, a] - 2)
        valid = (column >= 0) & (column < side)
        column = jnp.where(flips_ref[a] == 1, side - 1 - column, column)
        column_ref[a] = one_hot(
            valid & (source == column * channels + target % channels), F32
        )
        wanted = target_row % half * 2 + target_row // half + (crops_ref[0, a] - 2)
        row_ref[a] = one_hot(source_row == wanted, F32)

    for copy in copies:
        copy.wait()
    steps = jnp.zeros((modulation_ref.shape[0], half_freq), F32)
    for a in range(views):
        steps = jnp.where(iota(steps.shape, 0) == a, steps_ref[a].astype(F32), steps)
    phases = steps * constant_ref[2, 0:1, :half_freq]
    stamp = jnp.concatenate([jnp.cos(phases), jnp.sin(phases)], axis=1).astype(BF16)
    conditioning = jnp.dot(stamp, w_time_ref[...], preferred_element_type=F32)
    conditioning = conditioning * (1.0 / (1.0 + jnp.exp(-conditioning)))
    modulation_ref[...] = jnp.dot(
        conditioning.astype(BF16), w_ada_ref[...], preferred_element_type=F32
    )
    lane, entry = iota((wide, 2 * short), 0), iota((wide, 2 * short), 1)
    spread = one_hot(lane // cells * short + lane % short == entry, BF16)
    patch_ref[...] = jnp.dot(spread, w_patch_ref[...], preferred_element_type=F32).astype(BF16)
    final_ref[...] = jnp.dot(spread, w_final_ref[...], preferred_element_type=F32).astype(BF16)
    place_ref[...] = (
        jnp.broadcast_to(constant_ref[0][:, None, :], (half, half, width))
        + jnp.broadcast_to(constant_ref[1][None, :, :], (half, half, width))
    ).reshape(half * half, width)
    for a in range(views):
        for line in range(half):
            n = a * half + line
            noise_ref[n : n + 1, :] = raw_noise_ref[a : a + 1, line * wide : (line + 1) * wide]


def token_kernel(
    rows,
    chosen_ref,
    steps_ref,
    table_ref,
    parts_ref,
    vae_ref,
    modulation_ref,
    patch_ref,
    place_ref,
    noise_ref,
    column_ref,
    row_ref,
    moments_ref,
    token_ref,
    mod_ref,
    latent_ref,
):
    sources = parts_ref.shape[0]
    lanes = parts_ref.shape[2]
    side = sources * rows
    channels = vae_ref.shape[1] // side
    cells = side * channels
    views = steps_ref.shape[0]
    half = side // 2
    per_view = half * half
    width = patch_ref.shape[1]
    short = 2 * channels
    wide = 2 * cells

    for source in range(sources):
        moments_ref[source * rows : (source + 1) * rows, :] = parts_ref[source, 1 : rows + 1, :]
    for source in range(sources):
        if source > 0:
            moments_ref[source * rows : source * rows + 1, :] += parts_ref[
                source - 1, rows + 1 : rows + 2, :
            ]
        if source < sources - 1:
            last = (source + 1) * rows - 1
            moments_ref[last : last + 1, :] += parts_ref[source + 1, 0:1, :]

    @pl.when(chosen_ref[0, 0] == 1)
    def _():
        moments = moments_ref[...]
        into, outof = iota((lanes, cells), 0), iota((lanes, cells), 1)
        cell = outof // channels * (2 * channels) + outof % channels
        mean_part = jnp.dot(moments, one_hot(into == cell, F32), precision=HIGHEST)
        logvar = jnp.dot(moments, one_hot(into == cell + channels, F32), precision=HIGHEST)
        latent_ref[...] = mean_part + jnp.exp(0.5 * logvar) * vae_ref[...]
        in_patch = patch_mask(per_view, half, wide, short)

        for a in range(views):
            keep_part = table_ref[0, steps_ref[a]]
            blend_part = table_ref[1, steps_ref[a]]
            moved = jnp.dot(latent_ref[...], column_ref[a], precision=HIGHEST)
            moved = jnp.dot(row_ref[a], moved, precision=HIGHEST)
            moved = jnp.concatenate([moved[:half], moved[half:]], axis=1)
            noised = keep_part * moved + blend_part * noise_ref[a * half : (a + 1) * half, :]
            patches = jnp.where(in_patch, over_patches(noised), 0.0).astype(BF16)
            tokens = jnp.dot(patches, patch_ref[...], preferred_element_type=F32)
            tokens = tokens + place_ref[...]
            shift_row = modulation_ref[a : a + 1, 0:width]
            scale_row = modulation_ref[a : a + 1, width : 2 * width]
            center = tokens - row_mean(tokens)
            variance = row_mean(center * center)
            normed = center * lax.rsqrt(variance + norm_epsilon)
            here = slice(a * per_view, (a + 1) * per_view)
            token_ref[here, :] = tokens
            mod_ref[here, :] = (normed * (1.0 + scale_row) + shift_row).astype(BF16)


def grad_kernel(blocks, views, chosen_ref, parity_ref, noise_ref, token_ref, mod_ref, modulation_ref, final_ref, *rest):
    own_fc1, own_fc2 = rest[0], rest[1]
    mine = rest[2 : 2 + blocks - 1]
    theirs = rest[1 + blocks : 2 * blocks]
    outs = rest[2 * blocks :]
    loss_ref = outs[0]
    keep_refs = outs[1 : 1 + blocks]
    send_refs = outs[1 + blocks : 1 + 2 * blocks]
    weight_ref, hidden_ref, slope_ref, pre_ref, branch_ref, grad_ref = outs[1 + 2 * blocks :]

    tokens_count, width = token_ref.shape
    wide = noise_ref.shape[1]
    half = noise_ref.shape[0] // views
    per_view = half * half
    short = wide // 2 // half
    piece = own_fc1.shape[1]
    total = piece * blocks
    entries = tokens_count * 2 * short
    parity = parity_ref[0]

    @pl.when(chosen_ref[0, 0] != 1)
    def _():
        loss_ref[...] = jnp.zeros_like(loss_ref)
        for k in range(blocks):
            keep_refs[k][...] = jnp.zeros_like(keep_refs[k])
            send_refs[k][...] = jnp.zeros_like(send_refs[k])

    @pl.when(chosen_ref[0, 0] == 1)
    def _():
        weight_ref[0, 0] = own_fc1[...]
        weight_ref[1, 0] = own_fc2[...]
        for k in range(1, blocks):
            weight_ref[parity, k] = mine[k - 1][...]
            weight_ref[1 - parity, k] = theirs[k - 1][...]
        in_patch = patch_mask(per_view, half, wide, short)

        def columns(k):
            return slice(k * piece, (k + 1) * piece)

        def view(a, loss_sum):
            here = pl.ds(a * per_view, per_view)
            gate = modulation_ref[pl.ds(a, 1), 2 * width : 3 * width]
            modulated = mod_ref[here, :]
            branch = jnp.zeros((per_view, width), F32)
            for k in range(blocks):
                x = jnp.dot(modulated, weight_ref[0, k], preferred_element_type=F32)
                square = x * x
                tanh = jnp.tanh(x * (square * (GELU_C * GELU_A) + GELU_C))
                cdf = 0.5 * tanh + 0.5
                hidden = x * cdf
                slope_ref[:, columns(k)] = cdf + (hidden * (1.0 - cdf)) * (
                    square * (6.0 * GELU_C * GELU_A) + 2.0 * GELU_C
                )
                hidden = hidden.astype(BF16)
                hidden_ref[here, columns(k)] = hidden
                branch = branch + lax.dot_general(
                    hidden, weight_ref[1, k], (((1,), (1,)), ((), ())), preferred_element_type=F32
                )
            mixed = token_ref[here, :] + gate * branch
            center = mixed - row_mean(mixed)
            variance = row_mean(center * center)
            inverse = lax.rsqrt(variance + norm_epsilon)
            normed = center * inverse
            predicted = lax.dot_general(
                normed.astype(BF16), final_ref[...], (((1,), (1,)), ((), ())),
                preferred_element_type=F32,
            )
            noise = noise_ref[pl.ds(a * half, half), :]
            residue = jnp.where(in_patch, predicted - over_patches(noise), 0.0)
            loss_sum = loss_sum + jnp.sum(residue * residue, axis=0, keepdims=True)
            grad_pred = (residue * (2.0 / entries)).astype(BF16)
            grad_normed = jnp.dot(grad_pred, final_ref[...], preferred_element_type=F32)
            grad_mixed = inverse * (
                grad_normed - row_mean(grad_normed) - normed * row_mean(grad_normed * normed)
            )
            grad_branch = (gate * grad_mixed).astype(BF16)
            branch_ref[here, :] = grad_branch
            for k in range(blocks):
                grad_hidden = jnp.dot(
                    grad_branch, weight_ref[1, k], preferred_element_type=F32
                )
                pre_ref[here, columns(k)] = (slope_ref[:, columns(k)] * grad_hidden).astype(BF16)
            return loss_sum

        loss_sum = lax.fori_loop(0, views, view, jnp.zeros((1, wide), F32))
        loss_ref[...] = jnp.broadcast_to(
            jnp.sum(loss_sum, keepdims=True) * (1.0 / entries), loss_ref.shape
        )

        modulated_t = mod_ref[...].T
        branch_t = branch_ref[...].T
        squares = jnp.zeros((1, piece), F32)
        for k in range(blocks):
            grad = jnp.dot(modulated_t, pre_ref[:, columns(k)], preferred_element_type=F32)
            grad_ref[0, k] = grad
            squares = squares + jnp.sum(grad * grad, axis=0, keepdims=True)
            grad = jnp.dot(branch_t, hidden_ref[:, columns(k)], preferred_element_type=F32)
            grad_ref[1, k] = grad
            squares = squares + jnp.sum(grad * grad, axis=0, keepdims=True)
        root_mean = jnp.sqrt(jnp.sum(squares, keepdims=True) / (2 * width * total))
        factor = 1.0 / (root_mean + clip_offset)
        for k in range(blocks):
            keep_refs[k][...] = grad_ref[parity, k] * factor
            send_refs[k][...] = grad_ref[1 - parity, k] * factor


VMEM = pl.BlockSpec(memory_space=pltpu.VMEM)
SMEM = pl.BlockSpec(memory_space=pltpu.SMEM)
HBM = pl.BlockSpec(memory_space=pltpu.HBM)


def prepare_call(scalars, constant, noise, weights, side):
    views, flat = noise.shape
    half = side // 2
    wide = flat // half
    cells = wide // 2
    width = weights[0].shape[1]
    inputs = [constant, noise, *weights]
    out_shape = [
        jax.ShapeDtypeStruct((16, 3 * width), F32),
        jax.ShapeDtypeStruct((wide, width), BF16),
        jax.ShapeDtypeStruct((wide, width), BF16),
        jax.ShapeDtypeStruct((half * half, width), F32),
        jax.ShapeDtypeStruct((views * half, wide), F32),
        jax.ShapeDtypeStruct((views, cells, cells), F32),
        jax.ShapeDtypeStruct((views, side, side), F32),
    ]
    return pl.pallas_call(
        partial(prepare_kernel, side),
        out_shape=out_shape,
        in_specs=[SMEM] * len(scalars) + [HBM] * len(inputs),
        out_specs=[VMEM] * len(out_shape),
        scratch_shapes=[pltpu.VMEM(v.shape, v.dtype) for v in inputs]
        + [pltpu.SemaphoreType.DMA((len(inputs),))],
        compiler_params=pltpu.CompilerParams(vmem_limit_bytes=52 << 20),
        cost_estimate=pl.CostEstimate(
            flops=1 << 27, bytes_accessed=1 << 21, transcendentals=0
        ),
        name="prepare",
    )(*scalars, *inputs)


def token_call(scalars, arrays, rows):
    parts, vae, _, patch, place = arrays[:5]
    lanes = parts.shape[2]
    side = parts.shape[0] * rows
    width = patch.shape[1]
    views = scalars[1].shape[0]
    tokens = views * place.shape[0]
    cells = vae.shape[1]
    out_shape = [
        jax.ShapeDtypeStruct((side, lanes), F32),
        jax.ShapeDtypeStruct((tokens, width), F32),
        jax.ShapeDtypeStruct((tokens, width), BF16),
    ]
    return pl.pallas_call(
        partial(token_kernel, rows),
        out_shape=out_shape,
        in_specs=[SMEM] * len(scalars) + [VMEM] * len(arrays),
        out_specs=[VMEM] * len(out_shape),
        scratch_shapes=[pltpu.VMEM((side, cells), F32)],
        compiler_params=pltpu.CompilerParams(vmem_limit_bytes=20 << 20),
        cost_estimate=pl.CostEstimate(
            flops=4 * tokens * width * cells, bytes_accessed=16 * tokens * width, transcendentals=0
        ),
        name="tokens",
    )(*scalars, *arrays)


def grad_call(chosen, parity, views, arrays, own, mine, theirs):
    blocks = len(mine) + 1
    _, token = arrays[:2]
    tokens, width = token.shape
    per_view = tokens // views
    piece = own[0].shape[1]
    total = piece * blocks
    inputs = list(arrays) + list(own) + list(mine) + list(theirs)
    out_shape = [jax.ShapeDtypeStruct((16, 128), F32)] + [
        jax.ShapeDtypeStruct((width, piece), F32)
    ] * (2 * blocks)
    return pl.pallas_call(
        partial(grad_kernel, blocks, views),
        out_shape=out_shape,
        in_specs=[SMEM] * 2 + [VMEM] * len(inputs),
        out_specs=[VMEM] * len(out_shape),
        scratch_shapes=[
            pltpu.VMEM((2, blocks, width, piece), BF16),
            pltpu.VMEM((tokens, total), BF16),
            pltpu.VMEM((per_view, total), F32),
            pltpu.VMEM((tokens, total), BF16),
            pltpu.VMEM((tokens, width), BF16),
            pltpu.VMEM((2, blocks, width, piece), F32),
        ],
        compiler_params=pltpu.CompilerParams(vmem_limit_bytes=36 << 20),
        cost_estimate=pl.CostEstimate(
            flops=10 * tokens * width * total,
            bytes_accessed=20 * width * total,
            transcendentals=tokens * total,
        ),
        name="grads",
    )(chosen, parity, *inputs)


def shift(values, axis, flip):
    count = lax.axis_size(axis)
    return lax.ppermute(values, axis, [(i, i ^ flip) for i in range(count)])


LOSS_SCALE = 64.0
NEXT = 2.0 ** (LINK_MANTISSA + 1)


def to_link(values):
    return lax.reduce_precision(values, LINK_EXPONENT, LINK_MANTISSA)


def pack_loss(loss):
    high = to_link(loss * (1.0 / LOSS_SCALE))
    rest = (loss * (1.0 / LOSS_SCALE) - high) * NEXT
    middle = to_link(rest)
    low = to_link((rest - middle) * NEXT)
    return jnp.concatenate([high, middle, low], axis=1)


def unpack_loss(packed):
    high, middle, low = jnp.split(packed.astype(F32), 3, axis=1)
    return (high + (middle + low * (1.0 / NEXT)) * (1.0 / NEXT)) * LOSS_SCALE


def per_device(
    features,
    conv_weight,
    vae_noise,
    flips,
    crops,
    tsteps,
    diffusion_noise,
    selected,
    w_patch,
    w_time,
    w_ada,
    w_fc1,
    w_fc2,
    w_final,
    noise_fc1,
    noise_fc2,
):
    groups = lax.axis_size("fsdp")
    sources = lax.axis_size("dp")
    parity = lax.axis_index("dp") % CORES
    even = parity == 0
    local_rows = features[0]
    rows, side = local_rows.shape[1], local_rows.shape[2]
    outs = conv_weight.shape[3]
    channels = outs // 2
    width, piece = w_fc1.shape
    views = flips.shape[2]

    own_kind = jnp.where(even, w_fc1, w_fc2)
    mine = [shift(own_kind, "fsdp", k) for k in range(1, groups)]

    local = local_conv(local_rows, conv_weight)
    parts = lax.all_to_all(local, "dp", split_axis=0, concat_axis=0, tiled=True)
    steps = tsteps[0, 0]
    table = jnp.asarray(noise_tables(TSTEPS))
    constant = jnp.asarray(constants(side // 2, width, w_time.shape[0]))
    modulation, patch, final, place, noise, column, row = prepare_call(
        [flips[0, 0], crops[0, 0].T, steps, table],
        constant,
        diffusion_noise[0, 0],
        lax.optimization_barrier((w_patch, w_time, w_ada, w_final.T, local))[:4],
        side,
    )
    *mine, modulation = lax.optimization_barrier((*mine, modulation))
    theirs = [shift(block, "dp", 1) for block in mine]
    own = (w_fc1, w_fc2)
    blocked = piece % 128 == 0
    if not blocked:
        joined = jnp.concatenate([own_kind] + mine, axis=1)
        other = jnp.concatenate([jnp.where(even, w_fc2, w_fc1)] + theirs, axis=1)
        own = (jnp.where(even, joined, other), jnp.where(even, other, joined))
        mine, theirs = [], []
    moments, tokens, modulated = token_call(
        [selected, steps, table],
        [parts, vae_noise.reshape(side, side * channels)]
        + [modulation, patch, place, noise, column, row],
        rows,
    )
    loss, *grads = grad_call(
        selected,
        parity.astype(jnp.int32).reshape(1),
        views,
        [noise, tokens, modulated, modulation, final],
        own,
        mine,
        theirs,
    )
    keep, send = grads[: len(grads) // 2], grads[len(grads) // 2 :]
    if not blocked:
        keep = jnp.split(keep[0], groups, axis=1)
        send = jnp.split(send[0], groups, axis=1)

    loss = loss[:, : piece // 3]
    received = [shift(block, "dp", 1) for block in send]
    *received, other = lax.optimization_barrier((*received, shift(loss, "dp", 1)))
    pair = [kept + block for kept, block in zip(keep, received)]
    loss = loss + other
    middle = width // 2
    halves = [[block[:middle] for block in pair], [block[middle:] for block in pair]]

    def exchange(moving, axis, flips_of):
        packed = pack_loss(loss)
        moved = [
            jnp.concatenate([moving[0], packed], axis=0).astype(LINK),
            moving[1].astype(LINK),
        ]
        moved = [shift(block, axis, flip) for block, flip in zip(moved, flips_of)]
        first, second = [block.astype(F32) for block in lax.optimization_barrier(moved)]
        size = moving[0].shape[0]
        return (first[:size], second), unpack_loss(packed) + unpack_loss(first[size:])

    bits = [1 << b for b in range(groups.bit_length() - 1)]
    for step in range(len(bits)):
        flips_of = (bits[step], bits[-1 - step])
        gone = [
            [k for k in range(groups) if k & bit and half[k] is not None]
            for half, bit in zip(halves, flips_of)
        ]
        moving = [
            jnp.concatenate([half[k] for k in ks], axis=0) for half, ks in zip(halves, gone)
        ]
        received, loss = exchange(moving, "fsdp", flips_of)
        for half, bit, ks, moved in zip(halves, flips_of, gone, received):
            for n, k in enumerate(ks):
                half[k ^ bit] = half[k ^ bit] + moved[n * middle : (n + 1) * middle]
                half[k] = None
    halves = [half[0] for half in halves]
    chips = sources // CORES
    hops = [(2 << b) - 1 for b in range(chips.bit_length() - 1)]
    for step in range(len(hops)):
        halves = [to_link(half) for half in halves]
        flips_of = (CORES * hops[step], CORES * hops[-1 - step])
        received, loss = exchange(halves, "dp", flips_of)
        halves = [half + moved for half, moved in zip(halves, received)]
    partner = [shift(half, "dp", 1) for half in halves]
    summed = jnp.concatenate(halves, axis=0)
    partner = jnp.concatenate(partner, axis=0)
    loss_all = lax.optimization_barrier(loss)[0, 0]

    selected_count = selected.shape[0] * sources * groups // 2
    sum_fc1 = jnp.where(even, summed, partner)
    sum_fc2 = jnp.where(even, partner, summed)
    update_fc1 = (sum_fc1 + noise_weight * noise_fc1) / selected_count
    update_fc2 = (sum_fc2 + noise_weight * noise_fc2) / selected_count
    latent_moments = moments.reshape(1, 1, side * side * outs)
    return (update_fc1, update_fc2, loss_all / selected_count, latent_moments)


def solution(mesh):
    in_specs = (
        P("fsdp", None, "dp", None, None),
        P(),
        P("dp", "fsdp", None),
        P("dp", "fsdp", None),
        P("dp", "fsdp", None, None),
        P("dp", "fsdp", None),
        P("dp", "fsdp", None, None),
        P("dp", "fsdp"),
        P(),
        P(),
        P(),
        P(None, "fsdp"),
        P(None, "fsdp"),
        P(),
        P(None, "fsdp"),
        P(None, "fsdp"),
    )
    out_specs = (P(None, "fsdp"), P(None, "fsdp"), P(), P("dp", "fsdp", None))
    return jax.shard_map(
        per_device, mesh=mesh, in_specs=in_specs, out_specs=out_specs, check_vma=False
    )
```

time: 113 us -> 95.6 us (0.85)
  starting transfers between devices: 46.8 us -> 21.4 us
  Pallas kernels: 7.63 us -> 25 us
  waiting for transfers between devices: 45.8 us -> 35.5 us
    ppermute x24 -> x21, starting transfers between devices: 41.4 us -> 16.4 us  [shift(): return lax.ppermute(values, axis, [(i, i ^ flip) for i in range(count)])]
    pallas_call x2 -> x4, Pallas kernels: 7.63 us -> 25 us  [the longest x1 16.2 us: grad_call(): pl.pallas_call(partial(grad_kernel, blocks, views), out_shape=out_shape,...]
    ppermute x24 -> x21, waiting for transfers between devices: 42.4 us -> 30.2 us  [shift(): return lax.ppermute(values, axis, [(i, i ^ flip) for i in range(count)])]
    all_to_all x1, waiting for transfers between devices: 3.39 us -> 5.27 us  [per_device(): parts = lax.all_to_all(local, 'dp', split_axis=0, concat_axis=0, tiled=True)]
    unnamed x35 -> x37, local copies, waits for them, and re-layouts: 3.63 us -> 3.79 us
  transfers between devices with their start and end apart: 25 -> 22, of which waited for: 15 -> 8; matrix products, arithmetic and copies ran while one was open for 3% -> 2% of each run, Pallas kernels for 5% -> 9%
where the time goes in v2:
time: 95.6 us; the launch traced here: 95.1 us
  waiting for transfers between devices  35.5 us (37%)
  Pallas kernels  25 us (26%)
  starting transfers between devices  21.4 us (22%)
  local copies, waits for them, and re-layouts  5.03 us (5%)
  other arithmetic  4.6 us (5%)
  between operations  3.6 us (4%)
    ppermute x21, waiting for transfers between devices, shift(): return lax.ppermute(values, axis, [(i, i ^ flip) for i in range(count)])  30.2 us
    ppermute x21, starting transfers between devices, shift(): return lax.ppermute(values, axis, [(i, i ^ flip) for i in range(count)])  16.4 us
    pallas_call x1, Pallas kernels, grad_call(): pl.pallas_call(partial(grad_kernel, blocks, views), out_shape=out_shape,...  16.2 us
    all_to_all x1, waiting for transfers between devices, per_device(): parts = lax.all_to_all(local, 'dp', split_axis=0, concat_axis=0, tiled=True)  5.27 us
    all_to_all x1, starting transfers between devices, per_device(): parts = lax.all_to_all(local, 'dp', split_axis=0, concat_axis=0, tiled=True)  4.99 us
    unnamed x37, local copies, waits for them, and re-layouts  3.79 us
    pallas_call x1, Pallas kernels, token_call(): pl.pallas_call(partial(token_kernel, rows), out_shape=out_shape, in_specs...  3.04 us
    pallas_call x1, Pallas kernels, prepare_call(): pl.pallas_call(partial(prepare_kernel, side), out_shape=out_shape, in_spe...  2.95 us
  transfers between devices with their start and end apart: 22, of which 8 were waited for; matrix products, arithmetic and copies ran while one was open for 2% of the time, Pallas kernels for 9%

profile of v2, /device:TPU:0, one launch (start us, length us, event | category | flops | bytes accessed | tf_op | source)
XLA Modules:
  0.0 95.1 jit_solution(2458484770518970402)
XLA Ops:
  0.6 0.0 copy-start.7
  0.6 0.0 copy-start.5
  0.8 1.2 %broadcast_select_fusion = bf16[384,384]{1,0:T(8,128)(2,1)S(1)} fusion(bf16[384,384]{1,0:T(8,128)(2,1)} %rest_0_.1, bf16[384,384]{1,0:T(8,128)(2,1)} %rest_1_.1, pred[]{:T(512)S(6)} %eq.5), kind=kLoop, calls=%fused_computation.23 | loop fusion | flops 147456 | bytes 884737 | tf_op jit(solution)/shard_map/jit(_where)/select_n | solution.py:560
  1.9 4.0 %collective-permute-start.2 = (bf16[384,384]{1,0:T(8,128)(2,1)S(1)}, bf16[384,384]{1,0:T(8,128)(2,1)S(1)}, u32[]{:S(2)}, u32[]{:S(2)}) collective-permute-start(bf16[384,384]{1,0:T(8,128)(2,1)S(1)} %broadcast_select_fusion), channel_id=1, source_target_pairs={{0,3},{1,2},{2,1},{3,0},{4,7},{5,6},{6,5},{7,4},{8,11},{9,10},{10,... | collective-permute-start | bytes 884744 | tf_op jit(solution)/shard_map/ppermute | solution.py:507
  5.9 0.5 collective-permute-start.1
  6.4 0.1 collective-permute-start
  6.5 1.2 %copy-done = bf16[1,8,4,32,512]{4,3,2,1,0:T(8,128)(2,1)S(1)} copy-done((bf16[1,8,4,32,512]{4,3,2,1,0:T(8,128)(2,1)S(1)}, bf16[1,8,4,32,512]{4,3,2,1,0:T(8,128)(2,1)}, u32[]{:S(2)}) %copy-start) | copy-done | bytes 1048600
  7.8 0.9 copy-done.4
  8.7 2.8 %local_conv.1 = f32[8,8,256]{2,1,0:T(8,128)} custom-call(bf16[1024,512]{1,0:T(8,128)(2,1)S(1)} %bitcast.14, bf16[72,512]{1,0:T(8,128)(2,1)S(1)} %bitcast.15), custom_call_target="tpu_custom_call" | custom-call | flops 75497472 | bytes 1048576 | tf_op jit(solution)/shard_map/local_conv/pallas_call | solution.py:120
  11.6 3.0 %prepare.1 = (f32[16,1152]{1,0:T(8,128)S(1)}, bf16[256,384]{1,0:T(8,128)(2,1)S(1)}, bf16[256,384]{1,0:T(8,128)(2,1)S(1)}, f32[256,384]{1,0:T(8,128)S(1)}, f32[64...) custom-call(s32[4]{0:T(128)S(1)} %bitcast.22, s32[2,4]{1,0:T(2,128)S(1)} %bitcast.21, ...), custom_call_target="tpu_custom_call" | custom-call | flops 134217728 | bytes 2097152 | tf_op jit(solution)/shard_map/prepare/pallas_call | solution.py:429
  14.5 0.0 copy-start.14
  14.5 0.7 copy-done.14
  15.2 0.0 collective-permute-done.2.rest_4_
  15.2 4.0 %collective-permute-done.1.rest_3_ = bf16[384,384]{1,0:T(8,128)(2,1)S(1)} collective-permute-done((bf16[384,384]{1,0:T(8,128)(2,1)S(1)}, bf16[384,384]{1,0:T(8,128)(2,1)S(1)}, u32[]{:S(2)}, u32[]{:S(2)}) %collective-permute-start.1) | collective-permute-done | bytes 294944 | tf_op jit(solution)/shard_map/ppermute | solution.py:507
  19.2 0.3 collective-permute-done.rest_2_
  19.5 0.0 collective-permute-start.3
  19.5 0.5 collective-permute-start.4
  20.0 0.0 collective-permute-start.5
  20.0 5.0 %all-to-all-start = ((f32[8,8,256]{2,1,0:T(8,128)}), f32[8,8,256]{2,1,0:T(8,128)S(1)}, u32[]{:S(2)}, u32[]{:S(2)}) async-start(f32[8,8,256]{2,1,0:T(8,128)} %local_conv.1), calls=%async_computation | async-start | bytes 131072 | tf_op jit(solution)/shard_map/all_to_all | solution.py:564
  25.7 5.3 %all-to-all-done.parts_ref = f32[8,8,256]{2,1,0:T(8,128)S(1)} async-done(((f32[8,8,256]{2,1,0:T(8,128)}), f32[8,8,256]{2,1,0:T(8,128)S(1)}, u32[]{:S(2)}, u32[]{:S(2)}) %all-to-all-start) | async-done | bytes 65568 | tf_op jit(solution)/shard_map/all_to_all | solution.py:564
  30.9 3.0 %tokens.1 = (f32[32,256]{1,0:T(8,128)S(1)}, f32[1024,384]{1,0:T(8,128)S(1)}, bf16[1024,384]{1,0:T(8,128)(2,1)S(1)}) custom-call(s32[1,1]{1,0:T(1,128)S(6)} %copy.23.chosen_ref, s32[4]{0:T(128)S(1)} %bitcast.20, f32[2,1000]{1,0:T(2,128)S(1)} %copy-done.7, f32[8,8,256]{2,1,0:T(8,128)S(1)} %all-to-all-done.parts_ref, f32[32,128]{1,0:T(8,128)S(1)} %bitcast.17, ...), custom_call_target="tpu_custom_call" | custom-call | flops 201326592 | bytes 6291456 | tf_op jit(solution)/shard_map/tokens/pallas_call | solution.py:457
  34.0 0.0 copy-start.15
  34.1 0.9 copy-done.15
  35.0 16.2 %grads.1 = (f32[16,128]{1,0:T(8,128)S(1)}, f32[384,384]{1,0:T(8,128)S(1)}, f32[384,384]{1,0:T(8,128)S(1)}, f32[384,384]{1,0:T(8,128)S(1)}, f32[384,384]{1,0:T(8,...) custom-call(s32[1,1]{1,0:T(1,128)S(6)} %copy.23.chosen_ref, ...), custom_call_target="tpu_custom_call" | custom-call | flops 6039797760 | bytes 11796480 | tf_op jit(solution)/shard_map/grads/pallas_call | solution.py:482
  51.2 0.1 collective-permute-start.6
  51.2 0.5 collective-permute-start.7
  51.7 0.1 collective-permute-start.8
  51.8 0.4 collective-permute-start.9
  52.3 0.1 collective-permute-start.10
  52.3 3.4 %collective-permute-done.10 = f32[16,128]{1,0:T(8,128)S(1)} collective-permute-done((f32[16,128]{1,0:T(8,128)S(1)}, f32[16,128]{1,0:T(8,128)S(1)}, u32[]{:S(2)}, u32[]{:S(2)}) %collective-permute-start.10) | collective-permute-done | bytes 8224 | tf_op jit(solution)/shard_map/ppermute | solution.py:507
  55.8 0.1 add_convert_fusion
  55.9 0.1 fusion.52
  56.0 0.1 add.115
  56.1 0.1 add.118
  56.2 0.1 maximum_maximum_fusion
  56.3 0.1 collective-permute-start.11
  56.4 0.1 pad_maximum_fusion.1
  56.5 2.3 %collective-permute-start.12 = (f16[384,384]{1,0:T(8,128)(2,1)S(1)}, f16[384,384]{1,0:T(8,128)(2,1)S(1)}, u32[]{:S(2)}, u32[]{:S(2)}) collective-permute-start(f16[384,384]{1,0:T(8,128)(2,1)S(1)} %pad_maximum_fusion.1), channel_id=1, source_target_pairs={{0,2},{1,3},{2,0},{3,1},{4,6},{5,7},{6,4},{7,5},{8,10},{9,11},{10,... | collective-permute-start | bytes 884744 | tf_op jit(solution)/shard_map/ppermute | solution.py:507
  58.7 7.0 %collective-permute-done.12 = f16[384,384]{1,0:T(8,128)(2,1)S(1)} collective-permute-done((f16[384,384]{1,0:T(8,128)(2,1)S(1)}, f16[384,384]{1,0:T(8,128)(2,1)S(1)}, u32[]{:S(2)}, u32[]{:S(2)}) %collective-permute-start.12) | collective-permute-done | bytes 294944 | tf_op jit(solution)/shard_map/ppermute | solution.py:507
  65.9 0.1 reduce-precision_convert_fusion.5
  66.0 1.8 %collective-permute-start.13 = (f16[208,384]{1,0:T(8,128)(2,1)S(1)}, f16[208,384]{1,0:T(8,128)(2,1)S(1)}, u32[]{:S(2)}, u32[]{:S(2)}) collective-permute-start(f16[208,384]{1,0:T(8,128)(2,1)S(1)} %maximum_maximum_fusion.1), channel_id=1, source_target_pairs={{0,2},{1,3},{2,0},{3,1},{4,6},{5,7},{6,4},{7,5},{8,10},{9,11},{10,... | collective-permute-start | bytes 479240 | tf_op jit(solution)/shard_map/ppermute | solution.py:507
  67.9 1.3 %collective-permute-start.14 = (f16[192,384]{1,0:T(8,128)(2,1)S(1)}, f16[192,384]{1,0:T(8,128)(2,1)S(1)}, u32[]{:S(2)}, u32[]{:S(2)}) collective-permute-start(f16[192,384]{1,0:T(8,128)(2,1)S(1)} %fusion.4), channel_id=1, source_target_pairs={{0,1},{1,0},{2,3},{3,2},{4,5},{5,4},{6,7},{7,6},{8,9},{9,8},{10,11... | collective-permute-start | bytes 442376 | tf_op jit(solution)/shard_map/ppermute | solution.py:507
  69.2 0.1 add.114
  69.3 3.8 %collective-permute-done.14 = f16[192,384]{1,0:T(8,128)(2,1)S(1)} collective-permute-done((f16[192,384]{1,0:T(8,128)(2,1)S(1)}, f16[192,384]{1,0:T(8,128)(2,1)S(1)}, u32[]{:S(2)}, u32[]{:S(2)}) %collective-permute-start.14) | collective-permute-done | bytes 147488 | tf_op jit(solution)/shard_map/ppermute | solution.py:507
  73.2 0.1 reduce-precision_convert_fusion.3
  73.2 0.4 fusion.46
  73.7 0.4 collective-permute-start.15
  74.1 1.6 %collective-permute-start.16 = (f16[192,384]{1,0:T(8,128)(2,1)S(1)}, f16[192,384]{1,0:T(8,128)(2,1)S(1)}, u32[]{:S(2)}, u32[]{:S(2)}) collective-permute-start(f16[192,384]{1,0:T(8,128)(2,1)S(1)} %get-tuple-element.86), channel_id=1, source_target_pairs={{0,24},{4,28},{8,16},{12,20},{16,8},{20,12},{24,0},{28,4},{1,25},{... | collective-permute-start | bytes 442376 | tf_op jit(solution)/shard_map/ppermute | solution.py:507
  75.7 5.6 %collective-permute-done.16 = f16[192,384]{1,0:T(8,128)(2,1)S(1)} collective-permute-done((f16[192,384]{1,0:T(8,128)(2,1)S(1)}, f16[192,384]{1,0:T(8,128)(2,1)S(1)}, u32[]{:S(2)}, u32[]{:S(2)}) %collective-permute-start.16) | collective-permute-done | bytes 147488 | tf_op jit(solution)/shard_map/ppermute | solution.py:507
  81.3 0.1 reduce-precision_convert_fusion.1
  81.4 0.2 fusion.7
  81.7 2.0 %collective-permute-start.17 = (f16[208,384]{1,0:T(8,128)(2,1)S(1)}, f16[208,384]{1,0:T(8,128)(2,1)S(1)}, u32[]{:S(2)}, u32[]{:S(2)}) collective-permute-start(f16[208,384]{1,0:T(8,128)(2,1)S(1)} %maximum_maximum_fusion.3), channel_id=1, source_target_pairs={{0,24},{4,28},{8,16},{12,20},{16,8},{20,12},{24,0},{28,4},{1,25},{... | collective-permute-start | bytes 479240 | tf_op jit(solution)/shard_map/ppermute | solution.py:507
  83.7 0.2 fusion.6
  83.8 0.1 collective-permute-start.18
  83.9 0.6 reshape.25
  84.6 5.9 %collective-permute-done.18 = f16[192,384]{1,0:T(8,128)(2,1)S(1)} collective-permute-done((f16[192,384]{1,0:T(8,128)(2,1)S(1)}, f16[192,384]{1,0:T(8,128)(2,1)S(1)}, u32[]{:S(2)}, u32[]{:S(2)}) %collective-permute-start.18) | collective-permute-done | bytes 147488 | tf_op jit(solution)/shard_map/ppermute | solution.py:507
  90.5 0.0 copy-start.16
  90.5 0.0 copy-start.17
  90.5 0.2 slice_add_fusion
  90.7 0.1 collective-permute-start.19
  90.8 0.2 convert_add_fusion
  91.0 0.6 collective-permute-start.20
  91.6 0.5 slice.102
  92.8 1.2 %add_multiply_fusion = (f32[384,384]{1,0:T(8,128)}, f32[384,384]{1,0:T(8,128)}) fusion(f32[384,384]{1,0:T(8,128)S(1)} %copy-done.16, f32[384,384]{1,0:T(8,128)S(1)} %constant_dynamic-update-slice_fusion, f32[192,384]{1,0:T(8,128)S(1)} %convert_add_fusion, f32[192,384]{1,0:T(8,128)S(1)} %slice_add_fusion, pred[]{:T(512)S(6)} %eq.5, f32[384,384]{1,0:T(8,128)S(1)} %copy-done.17), kind=kLoop, calls=%fused_computation.1 | loop fusion | flops 1327104 | bytes 3538945 | tf_op jit(solution)/shard_map/div | solution.py:655
  (59 shorter events, 0.7 us)
Async XLA Ops:
  0.6 10.8 %copy-start.7 = (f32[2,1000]{1,0:T(2,128)S(1)}, f32[2,1000]{1,0:T(2,128)}, u32[]{:S(2)}) copy-start(f32[2,1000]{1,0:T(2,128)} %constant.44.clone.table_ref) | copy-start | bytes 24004
  0.6 10.8 %copy-start.5 = (f32[3,16,384]{2,1,0:T(8,128)S(1)}, f32[3,16,384]{2,1,0:T(8,128)}, u32[]{:S(2)}) copy-start(f32[3,16,384]{2,1,0:T(8,128)} %constant.45.clone.constant_hbm) | copy-start | bytes 221188
  0.7 10.8 %copy-start.10 = (bf16[384,16]{0,1:T(8,128)(2,1)S(1)}, bf16[384,16]{0,1:T(8,128)(2,1)}, u32[]{:S(2)}) copy-start(bf16[384,16]{0,1:T(8,128)(2,1)} %param.31) | copy-start | bytes 36868
  0.7 10.8 %copy-start.3 = (bf16[256,384]{1,0:T(8,128)(2,1)S(1)}, bf16[256,384]{1,0:T(8,128)(2,1)}, u32[]{:S(2)}) copy-start(bf16[256,384]{1,0:T(8,128)(2,1)} %w_time_hbm) | copy-start | bytes 589828
  0.7 10.8 %copy-start.9 = (bf16[16,384]{1,0:T(8,128)(2,1)S(1)}, bf16[16,384]{1,0:T(8,128)(2,1)}, u32[]{:S(2)}) copy-start(bf16[16,384]{1,0:T(8,128)(2,1)} %w_patch_hbm) | copy-start | bytes 36868
  0.7 10.8 %copy-start.6 = (f32[1,1,4,4096]{3,2,1,0:T(4,128)S(1)}, f32[1,1,4,4096]{3,2,1,0:T(4,128)}, u32[]{:S(2)}) copy-start(f32[1,1,4,4096]{3,2,1,0:T(4,128)} %param.24) | copy-start | bytes 196612
  0.7 10.8 %copy-start.11 = (s32[1,1,4]{2,1,0:T(1,128)S(1)}, s32[1,1,4]{2,1,0:T(1,128)}, u32[]{:S(2)}) copy-start(s32[1,1,4]{2,1,0:T(1,128)} %param.23) | copy-start | bytes 52
  0.7 10.8 %copy-start.12 = (s32[1,1,4,2]{2,3,1,0:T(2,128)S(1)}, s32[1,1,4,2]{2,3,1,0:T(2,128)}, u32[]{:S(2)}) copy-start(s32[1,1,4,2]{2,3,1,0:T(2,128)} %param.22) | copy-start | bytes 100
  0.7 10.8 %copy-start.13 = (s32[1,1,4]{2,1,0:T(1,128)S(1)}, s32[1,1,4]{2,1,0:T(1,128)}, u32[]{:S(2)}) copy-start(s32[1,1,4]{2,1,0:T(1,128)} %param.21) | copy-start | bytes 52
  0.7 30.2 %copy-start.8 = (f32[1,1,4096]{2,1,0:T(1,128)S(1)}, f32[1,1,4096]{2,1,0:T(1,128)}, u32[]{:S(2)}) copy-start(f32[1,1,4096]{2,1,0:T(1,128)} %param.20) | copy-start | bytes 49156
  1.9 13.3 %collective-permute-start.2 = (bf16[384,384]{1,0:T(8,128)(2,1)S(1)}, bf16[384,384]{1,0:T(8,128)(2,1)S(1)}, u32[]{:S(2)}, u32[]{:S(2)}) collective-permute-start(bf16[384,384]{1,0:T(8,128)(2,1)S(1)} %broadcast_select_fusion), channel_id=1, source_target_pairs={{0,3},{1,2},{2,1},{3,0},{4,7},{5,6},{6,5},{7,4},{8,11},{9,10},{10,... | collective-permute-start | bytes 884744 | tf_op jit(solution)/shard_map/ppermute | solution.py:507
  5.9 13.3 %collective-permute-start.1 = (bf16[384,384]{1,0:T(8,128)(2,1)S(1)}, bf16[384,384]{1,0:T(8,128)(2,1)S(1)}, u32[]{:S(2)}, u32[]{:S(2)}) collective-permute-start(bf16[384,384]{1,0:T(8,128)(2,1)S(1)} %broadcast_select_fusion), channel_id=1, source_target_pairs={{0,2},{1,3},{2,0},{3,1},{4,6},{5,7},{6,4},{7,5},{8,10},{9,11},{10,... | collective-permute-start | bytes 884744 | tf_op jit(solution)/shard_map/ppermute | solution.py:507
  6.4 13.1 %collective-permute-start = (bf16[384,384]{1,0:T(8,128)(2,1)S(1)}, bf16[384,384]{1,0:T(8,128)(2,1)S(1)}, u32[]{:S(2)}, u32[]{:S(2)}) collective-permute-start(bf16[384,384]{1,0:T(8,128)(2,1)S(1)} %broadcast_select_fusion), channel_id=1, source_target_pairs={{0,1},{1,0},{2,3},{3,2},{4,5},{5,4},{6,7},{7,6},{8,9},{9,8},{10,11... | collective-permute-start | bytes 884744 | tf_op jit(solution)/shard_map/ppermute | solution.py:507
  6.5 1.2 %copy-start = (bf16[1,8,4,32,512]{4,3,2,1,0:T(8,128)(2,1)S(1)}, bf16[1,8,4,32,512]{4,3,2,1,0:T(8,128)(2,1)}, u32[]{:S(2)}) copy-start(bf16[1,8,4,32,512]{4,3,2,1,0:T(8,128)(2,1)} %param.18) | copy-start | bytes 3145732
  7.8 0.9 copy-start.4
  11.5 22.5 %copy-start.1 = (bf16[384,384]{1,0:T(8,128)(2,1)S(1)}, bf16[384,384]{1,0:T(8,128)(2,1)}, u32[]{:S(2)}) copy-start(bf16[384,384]{1,0:T(8,128)(2,1)} %rest_0_.1) | copy-start | bytes 884740
  11.5 22.6 %copy-start.2 = (bf16[384,384]{1,0:T(8,128)(2,1)S(1)}, bf16[384,384]{1,0:T(8,128)(2,1)}, u32[]{:S(2)}) copy-start(bf16[384,384]{1,0:T(8,128)(2,1)} %rest_1_.1) | copy-start | bytes 884740
  14.5 0.7 copy-start.14
  19.5 14.5 %collective-permute-start.3 = (bf16[384,384]{1,0:T(8,128)(2,1)S(1)}, bf16[384,384]{1,0:T(8,128)(2,1)S(1)}, u32[]{:S(2)}, u32[]{:S(2)}) collective-permute-start(bf16[384,384]{1,0:T(8,128)(2,1)S(1)} %collective-permute-done.rest_2_), channel_id=1, source_target_pairs={{0,4},{4,0},{8,12},{12,8},{16,20},{20,16},{24,28},{28,24},{1,5},{5... | collective-permute-start | bytes 884744 | tf_op jit(solution)/shard_map/ppermute | solution.py:507
  19.5 14.5 %collective-permute-start.4 = (bf16[384,384]{1,0:T(8,128)(2,1)S(1)}, bf16[384,384]{1,0:T(8,128)(2,1)S(1)}, u32[]{:S(2)}, u32[]{:S(2)}) collective-permute-start(bf16[384,384]{1,0:T(8,128)(2,1)S(1)} %collective-permute-done.1.rest_3_), channel_id=1, source_target_pairs={{0,4},{4,0},{8,12},{12,8},{16,20},{20,16},{24,28},{28,24},{1,5},{5... | collective-permute-start | bytes 884744 | tf_op jit(solution)/shard_map/ppermute | solution.py:507
  20.0 14.0 %collective-permute-start.5 = (bf16[384,384]{1,0:T(8,128)(2,1)S(1)}, bf16[384,384]{1,0:T(8,128)(2,1)}, u32[]{:S(2)}, u32[]{:S(2)}) collective-permute-start(bf16[384,384]{1,0:T(8,128)(2,1)S(1)} %collective-permute-done.2.rest_4_), channel_id=1, source_target_pairs={{0,4},{4,0},{8,12},{12,8},{16,20},{20,16},{24,28},{28,24},{1,5},{5... | collective-permute-start | bytes 884744 | tf_op jit(solution)/shard_map/ppermute | solution.py:507
  20.0 10.9 %all-to-all-start = ((f32[8,8,256]{2,1,0:T(8,128)}), f32[8,8,256]{2,1,0:T(8,128)S(1)}, u32[]{:S(2)}, u32[]{:S(2)}) async-start(f32[8,8,256]{2,1,0:T(8,128)} %local_conv.1), calls=%async_computation | async-start | bytes 131072 | tf_op jit(solution)/shard_map/all_to_all | solution.py:564
  34.0 0.9 copy-start.15
  51.2 4.6 %collective-permute-start.6 = (f32[384,384]{1,0:T(8,128)S(1)}, f32[384,384]{1,0:T(8,128)S(1)}, u32[]{:S(2)}, u32[]{:S(2)}) collective-permute-start(f32[384,384]{1,0:T(8,128)S(1)} %get-tuple-element.62), channel_id=1, source_target_pairs={{0,4},{4,0},{8,12},{12,8},{16,20},{20,16},{24,28},{28,24},{1,5},{5... | collective-permute-start | bytes 1769480 | tf_op jit(solution)/shard_map/ppermute | solution.py:507
  51.2 4.5 %collective-permute-start.7 = (f32[384,384]{1,0:T(8,128)S(1)}, f32[384,384]{1,0:T(8,128)S(1)}, u32[]{:S(2)}, u32[]{:S(2)}) collective-permute-start(f32[384,384]{1,0:T(8,128)S(1)} %get-tuple-element.63), channel_id=1, source_target_pairs={{0,4},{4,0},{8,12},{12,8},{16,20},{20,16},{24,28},{28,24},{1,5},{5... | collective-permute-start | bytes 1769480 | tf_op jit(solution)/shard_map/ppermute | solution.py:507
  51.7 4.0 %collective-permute-start.8 = (f32[384,384]{1,0:T(8,128)S(1)}, f32[384,384]{1,0:T(8,128)S(1)}, u32[]{:S(2)}, u32[]{:S(2)}) collective-permute-start(f32[384,384]{1,0:T(8,128)S(1)} %get-tuple-element.64), channel_id=1, source_target_pairs={{0,4},{4,0},{8,12},{12,8},{16,20},{20,16},{24,28},{28,24},{1,5},{5... | collective-permute-start | bytes 1769480 | tf_op jit(solution)/shard_map/ppermute | solution.py:507
  51.8 4.0 %collective-permute-start.9 = (f32[384,384]{1,0:T(8,128)S(1)}, f32[384,384]{1,0:T(8,128)S(1)}, u32[]{:S(2)}, u32[]{:S(2)}) collective-permute-start(f32[384,384]{1,0:T(8,128)S(1)} %get-tuple-element.65), channel_id=1, source_target_pairs={{0,4},{4,0},{8,12},{12,8},{16,20},{20,16},{24,28},{28,24},{1,5},{5... | collective-permute-start | bytes 1769480 | tf_op jit(solution)/shard_map/ppermute | solution.py:507
  52.3 3.5 %collective-permute-start.10 = (f32[16,128]{1,0:T(8,128)S(1)}, f32[16,128]{1,0:T(8,128)S(1)}, u32[]{:S(2)}, u32[]{:S(2)}) collective-permute-start(f32[16,128]{1,0:T(8,128)S(1)} %get-tuple-element.66), channel_id=1, source_target_pairs={{0,4},{4,0},{8,12},{12,8},{16,20},{20,16},{24,28},{28,24},{1,5},{5... | collective-permute-start | bytes 24584 | tf_op jit(solution)/shard_map/ppermute | solution.py:507
  56.3 9.5 %collective-permute-start.11 = (f16[400,384]{1,0:T(8,128)(2,1)S(1)}, f16[400,384]{1,0:T(8,128)(2,1)S(1)}, u32[]{:S(2)}, u32[]{:S(2)}) collective-permute-start(f16[400,384]{1,0:T(8,128)(2,1)S(1)} %maximum_maximum_fusion), channel_id=1, source_target_pairs={{0,1},{1,0},{2,3},{3,2},{4,5},{5,4},{6,7},{7,6},{8,9},{9,8},{10,11... | collective-permute-start | bytes 921608 | tf_op jit(solution)/shard_map/ppermute | solution.py:507
  56.5 9.3 %collective-permute-start.12 = (f16[384,384]{1,0:T(8,128)(2,1)S(1)}, f16[384,384]{1,0:T(8,128)(2,1)S(1)}, u32[]{:S(2)}, u32[]{:S(2)}) collective-permute-start(f16[384,384]{1,0:T(8,128)(2,1)S(1)} %pad_maximum_fusion.1), channel_id=1, source_target_pairs={{0,2},{1,3},{2,0},{3,1},{4,6},{5,7},{6,4},{7,5},{8,10},{9,11},{10,... | collective-permute-start | bytes 884744 | tf_op jit(solution)/shard_map/ppermute | solution.py:507
  66.0 7.1 %collective-permute-start.13 = (f16[208,384]{1,0:T(8,128)(2,1)S(1)}, f16[208,384]{1,0:T(8,128)(2,1)S(1)}, u32[]{:S(2)}, u32[]{:S(2)}) collective-permute-start(f16[208,384]{1,0:T(8,128)(2,1)S(1)} %maximum_maximum_fusion.1), channel_id=1, source_target_pairs={{0,2},{1,3},{2,0},{3,1},{4,6},{5,7},{6,4},{7,5},{8,10},{9,11},{10,... | collective-permute-start | bytes 479240 | tf_op jit(solution)/shard_map/ppermute | solution.py:507
  67.9 5.2 %collective-permute-start.14 = (f16[192,384]{1,0:T(8,128)(2,1)S(1)}, f16[192,384]{1,0:T(8,128)(2,1)S(1)}, u32[]{:S(2)}, u32[]{:S(2)}) collective-permute-start(f16[192,384]{1,0:T(8,128)(2,1)S(1)} %fusion.4), channel_id=1, source_target_pairs={{0,1},{1,0},{2,3},{3,2},{4,5},{5,4},{6,7},{7,6},{8,9},{9,8},{10,11... | collective-permute-start | bytes 442376 | tf_op jit(solution)/shard_map/ppermute | solution.py:507
  73.7 7.7 %collective-permute-start.15 = (f16[208,384]{1,0:T(8,128)(2,1)S(1)}, f16[208,384]{1,0:T(8,128)(2,1)S(1)}, u32[]{:S(2)}, u32[]{:S(2)}) collective-permute-start(f16[208,384]{1,0:T(8,128)(2,1)S(1)} %maximum_maximum_fusion.2), channel_id=1, source_target_pairs={{0,8},{4,12},{8,0},{12,4},{16,24},{20,28},{24,16},{28,20},{1,9},{5... | collective-permute-start | bytes 479240 | tf_op jit(solution)/shard_map/ppermute | solution.py:507
  74.1 7.2 %collective-permute-start.16 = (f16[192,384]{1,0:T(8,128)(2,1)S(1)}, f16[192,384]{1,0:T(8,128)(2,1)S(1)}, u32[]{:S(2)}, u32[]{:S(2)}) collective-permute-start(f16[192,384]{1,0:T(8,128)(2,1)S(1)} %get-tuple-element.86), channel_id=1, source_target_pairs={{0,24},{4,28},{8,16},{12,20},{16,8},{20,12},{24,0},{28,4},{1,25},{... | collective-permute-start | bytes 442376 | tf_op jit(solution)/shard_map/ppermute | solution.py:507
  81.7 8.8 %collective-permute-start.17 = (f16[208,384]{1,0:T(8,128)(2,1)S(1)}, f16[208,384]{1,0:T(8,128)(2,1)S(1)}, u32[]{:S(2)}, u32[]{:S(2)}) collective-permute-start(f16[208,384]{1,0:T(8,128)(2,1)S(1)} %maximum_maximum_fusion.3), channel_id=1, source_target_pairs={{0,24},{4,28},{8,16},{12,20},{16,8},{20,12},{24,0},{28,4},{1,25},{... | collective-permute-start | bytes 479240 | tf_op jit(solution)/shard_map/ppermute | solution.py:507
  83.8 6.6 %collective-permute-start.18 = (f16[192,384]{1,0:T(8,128)(2,1)S(1)}, f16[192,384]{1,0:T(8,128)(2,1)S(1)}, u32[]{:S(2)}, u32[]{:S(2)}) collective-permute-start(f16[192,384]{1,0:T(8,128)(2,1)S(1)} %fusion.6), channel_id=1, source_target_pairs={{0,8},{4,12},{8,0},{12,4},{16,24},{20,28},{24,16},{28,20},{1,9},{5... | collective-permute-start | bytes 442376 | tf_op jit(solution)/shard_map/ppermute | solution.py:507
  90.5 2.3 %copy-start.16 = (f32[384,384]{1,0:T(8,128)S(1)}, f32[384,384]{1,0:T(8,128)}, u32[]{:S(2)}) copy-start(f32[384,384]{1,0:T(8,128)} %param.33) | copy-start | bytes 1769476
  90.5 2.3 %copy-start.17 = (f32[384,384]{1,0:T(8,128)S(1)}, f32[384,384]{1,0:T(8,128)}, u32[]{:S(2)}) copy-start(f32[384,384]{1,0:T(8,128)} %param.32) | copy-start | bytes 1769476
  90.7 2.0 %collective-permute-start.19 = (f32[192,384]{1,0:T(8,128)S(1)}, f32[192,384]{1,0:T(8,128)S(1)}, u32[]{:S(2)}, u32[]{:S(2)}) collective-permute-start(f32[192,384]{1,0:T(8,128)S(1)} %slice_add_fusion), channel_id=1, source_target_pairs={{0,4},{4,0},{8,12},{12,8},{16,20},{20,16},{24,28},{28,24},{1,5},{5... | collective-permute-start | bytes 884744 | tf_op jit(solution)/shard_map/ppermute | solution.py:507
  91.0 1.8 %collective-permute-start.20 = (f32[192,384]{1,0:T(8,128)S(1)}, f32[192,384]{1,0:T(8,128)S(1)}, u32[]{:S(2)}, u32[]{:S(2)}) collective-permute-start(f32[192,384]{1,0:T(8,128)S(1)} %convert_add_fusion), channel_id=1, source_target_pairs={{0,4},{4,0},{8,12},{12,8},{16,20},{20,16},{24,28},{28,24},{1,5},{5... | collective-permute-start | bytes 884744 | tf_op jit(solution)/shard_map/ppermute | solution.py:507

commit v3 on v2

--- a/solution.py
+++ b/solution.py
@@ -122,7 +122,7 @@
         out_shape=jax.ShapeDtypeStruct((images, padded, lanes), F32),
         in_specs=[pl.BlockSpec(memory_space=pltpu.VMEM)] * 2,
         out_specs=pl.BlockSpec(memory_space=pltpu.VMEM),
-        compiler_params=pltpu.CompilerParams(vmem_limit_bytes=24 << 20),
+        compiler_params=pltpu.CompilerParams(vmem_limit_bytes=56 << 20),
         cost_estimate=pl.CostEstimate(
             flops=2 * images * rows * lanes * channels * 9,
             bytes_accessed=features.size * 2,
@@ -383,7 +383,7 @@
                 pre_ref[here, columns(k)] = (slope_ref[:, columns(k)] * grad_hidden).astype(BF16)
             return loss_sum
 
-        loss_sum = lax.fori_loop(0, views, view, jnp.zeros((1, wide), F32))
+        loss_sum = lax.fori_loop(0, views, view, jnp.zeros((1, wide), F32), unroll=2)
         loss_ref[...] = jnp.broadcast_to(
             jnp.sum(loss_sum, keepdims=True) * (1.0 / entries), loss_ref.shape
         )
@@ -602,9 +602,9 @@
         send = jnp.split(send[0], groups, axis=1)
 
     loss = loss[:, : piece // 3]
-    received = [shift(block, "dp", 1) for block in send]
+    received = [shift(block.astype(LINK), "dp", 1) for block in send]
     *received, other = lax.optimization_barrier((*received, shift(loss, "dp", 1)))
-    pair = [kept + block for kept, block in zip(keep, received)]
+    pair = [kept + block.astype(F32) for kept, block in zip(keep, received)]
     loss = loss + other
     middle = width // 2
     halves = [[block[:middle] for block in pair], [block[middle:] for block in pair]]

time: 95.6 us -> 93.6 us (0.979)
  local copies, waits for them, and re-layouts: 5.03 us -> 2.92 us
    unnamed x37 -> x33, local copies, waits for them, and re-layouts: 3.79 us -> 1.68 us
    pallas_call x1, Pallas kernels: 2.82 us -> 4.05 us  [local_conv(): pl.pallas_call(partial(conv_kernel, rows, side, outs), out_shape=jax.Shap...]
  transfers between devices with their start and end apart: 22 -> 22, of which waited for: 8 -> 8; matrix products, arithmetic and copies ran while one was open for 2% -> 2% of each run, Pallas kernels for 9% -> 11%
where the time goes in v3:
time: 93.6 us; the launch traced here: 93.3 us
  waiting for transfers between devices  34.7 us (37%)
  Pallas kernels  25.9 us (28%)
  starting transfers between devices  21.4 us (23%)
  other arithmetic  4.74 us (5%)
  between operations  3.63 us (4%)
  local copies, waits for them, and re-layouts  2.92 us (3%)
    ppermute x21, waiting for transfers between devices, shift(): return lax.ppermute(values, axis, [(i, i ^ flip) for i in range(count)])  29.4 us
    ppermute x21, starting transfers between devices, shift(): return lax.ppermute(values, axis, [(i, i ^ flip) for i in range(count)])  16.4 us
    pallas_call x1, Pallas kernels, grad_call(): pl.pallas_call(partial(grad_kernel, blocks, views), out_shape=out_shape,...  15.8 us
    all_to_all x1, waiting for transfers between devices, per_device(): parts = lax.all_to_all(local, 'dp', split_axis=0, concat_axis=0, tiled=True)  5.27 us
    all_to_all x1, starting transfers between devices, per_device(): parts = lax.all_to_all(local, 'dp', split_axis=0, concat_axis=0, tiled=True)  4.99 us
    pallas_call x1, Pallas kernels, local_conv(): pl.pallas_call(partial(conv_kernel, rows, side, outs), out_shape=jax.Shap...  4.05 us
    pallas_call x1, Pallas kernels, token_call(): pl.pallas_call(partial(token_kernel, rows), out_shape=out_shape, in_specs...  3.05 us
    pallas_call x1, Pallas kernels, prepare_call(): pl.pallas_call(partial(prepare_kernel, side), out_shape=out_shape, in_spe...  2.95 us
  transfers between devices with their start and end apart: 22, of which 8 were waited for; matrix products, arithmetic and copies ran while one was open for 2% of the time, Pallas kernels for 11%

profile of v3, /device:TPU:0, one launch (start us, length us, event | category | flops | bytes accessed | tf_op | source)
XLA Modules:
  0.0 93.3 jit_solution(5496272749211361773)
XLA Ops:
  0.6 0.0 copy-start.5
  0.6 0.0 copy-start.3
  0.8 1.2 %broadcast_select_fusion = bf16[384,384]{1,0:T(8,128)(2,1)S(1)} fusion(bf16[384,384]{1,0:T(8,128)(2,1)} %rest_0_.1, bf16[384,384]{1,0:T(8,128)(2,1)} %rest_1_.1, pred[]{:T(512)S(6)} %eq.5), kind=kLoop, calls=%fused_computation.26 | loop fusion | flops 147456 | bytes 884737 | tf_op jit(solution)/shard_map/jit(_where)/select_n | solution.py:560
  1.9 4.0 %collective-permute-start.2 = (bf16[384,384]{1,0:T(8,128)(2,1)S(1)}, bf16[384,384]{1,0:T(8,128)(2,1)S(1)}, u32[]{:S(2)}, u32[]{:S(2)}) collective-permute-start(bf16[384,384]{1,0:T(8,128)(2,1)S(1)} %broadcast_select_fusion), channel_id=1, source_target_pairs={{0,3},{1,2},{2,1},{3,0},{4,7},{5,6},{6,5},{7,4},{8,11},{9,10},{10,... | collective-permute-start | bytes 884744 | tf_op jit(solution)/shard_map/ppermute | solution.py:507
  5.9 0.5 collective-permute-start.1
  6.4 0.1 collective-permute-start
  6.5 4.0 %local_conv.1 = f32[8,8,256]{2,1,0:T(8,128)} custom-call(bf16[1024,512]{1,0:T(8,128)(2,1)} %bitcast.21, bf16[72,512]{1,0:T(8,128)(2,1)} %bitcast.22), custom_call_target="tpu_custom_call" | custom-call | flops 75497472 | bytes 1048576 | tf_op jit(solution)/shard_map/local_conv/pallas_call | solution.py:120
  10.7 3.0 %prepare.1 = (f32[16,1152]{1,0:T(8,128)S(1)}, bf16[256,384]{1,0:T(8,128)(2,1)S(1)}, bf16[256,384]{1,0:T(8,128)(2,1)S(1)}, f32[256,384]{1,0:T(8,128)S(1)}, f32[64...) custom-call(s32[4]{0:T(128)S(1)} %bitcast.20, s32[2,4]{1,0:T(2,128)S(1)} %bitcast.19, ...), custom_call_target="tpu_custom_call" | custom-call | flops 134217728 | bytes 2097152 | tf_op jit(solution)/shard_map/prepare/pallas_call | solution.py:429
  13.6 0.0 copy-start.12
  13.6 0.7 copy-done.12
  14.3 0.0 collective-permute-done.2.rest_4_
  14.3 4.9 %collective-permute-done.1.rest_3_ = bf16[384,384]{1,0:T(8,128)(2,1)S(1)} collective-permute-done((bf16[384,384]{1,0:T(8,128)(2,1)S(1)}, bf16[384,384]{1,0:T(8,128)(2,1)S(1)}, u32[]{:S(2)}, u32[]{:S(2)}) %collective-permute-start.1) | collective-permute-done | bytes 294944 | tf_op jit(solution)/shard_map/ppermute | solution.py:507
  19.2 0.3 collective-permute-done.rest_2_
  19.5 0.0 collective-permute-start.3
  19.5 0.5 collective-permute-start.4
  20.0 0.0 collective-permute-start.5
  20.0 5.0 %all-to-all-start = ((f32[8,8,256]{2,1,0:T(8,128)}), f32[8,8,256]{2,1,0:T(8,128)S(1)}, u32[]{:S(2)}, u32[]{:S(2)}) async-start(f32[8,8,256]{2,1,0:T(8,128)} %local_conv.1), calls=%async_computation | async-start | bytes 131072 | tf_op jit(solution)/shard_map/all_to_all | solution.py:564
  25.7 5.3 %all-to-all-done.parts_ref = f32[8,8,256]{2,1,0:T(8,128)S(1)} async-done(((f32[8,8,256]{2,1,0:T(8,128)}), f32[8,8,256]{2,1,0:T(8,128)S(1)}, u32[]{:S(2)}, u32[]{:S(2)}) %all-to-all-start) | async-done | bytes 65568 | tf_op jit(solution)/shard_map/all_to_all | solution.py:564
  30.9 3.0 %tokens.1 = (f32[32,256]{1,0:T(8,128)S(1)}, f32[1024,384]{1,0:T(8,128)S(1)}, bf16[1024,384]{1,0:T(8,128)(2,1)S(1)}) custom-call(s32[1,1]{1,0:T(1,128)S(6)} %copy.23.chosen_ref, s32[4]{0:T(128)S(1)} %bitcast.18, f32[2,1000]{1,0:T(2,128)S(1)} %copy-done.5, f32[8,8,256]{2,1,0:T(8,128)S(1)} %all-to-all-done.parts_ref, f32[32,128]{1,0:T(8,128)S(1)} %bitcast.15, ...), custom_call_target="tpu_custom_call" | custom-call | flops 201326592 | bytes 6291456 | tf_op jit(solution)/shard_map/tokens/pallas_call | solution.py:457
  34.0 0.0 collective-permute-done.4.rest_6_
  34.0 0.0 collective-permute-done.5.rest_7_
  34.0 0.0 copy-start.13
  34.1 0.9 copy-done.13
  35.0 15.8 %grads.1 = (f32[16,128]{1,0:T(8,128)S(1)}, f32[384,384]{1,0:T(8,128)S(1)}, f32[384,384]{1,0:T(8,128)S(1)}, f32[384,384]{1,0:T(8,128)S(1)}, f32[384,384]{1,0:T(8,...) custom-call(s32[1,1]{1,0:T(1,128)S(6)} %copy.23.chosen_ref, ...), custom_call_target="tpu_custom_call" | custom-call | flops 6039797760 | bytes 11796480 | tf_op jit(solution)/shard_map/grads/pallas_call | solution.py:482
  51.0 0.1 collective-permute-start.9
  51.1 0.5 collective-permute-start.8
  51.6 0.1 collective-permute-start.7
  51.6 0.4 collective-permute-start.6
  52.1 0.1 collective-permute-start.10
  52.2 1.8 %collective-permute-done.10 = f32[16,128]{1,0:T(8,128)S(1)} collective-permute-done((f32[16,128]{1,0:T(8,128)S(1)}, f32[16,128]{1,0:T(8,128)S(1)}, u32[]{:S(2)}, u32[]{:S(2)}) %collective-permute-start.10) | collective-permute-done | bytes 8224 | tf_op jit(solution)/shard_map/ppermute | solution.py:507
  53.9 0.0 collective-permute-done.9
  53.9 0.1 convert_add_fusion
  54.1 0.1 fusion.52
  54.2 0.1 convert_add_fusion.1
  54.3 0.1 maximum_maximum_fusion
  54.4 0.1 collective-permute-start.11
  54.5 0.1 pad_maximum_fusion.1
  54.6 2.3 %collective-permute-start.12 = (f16[384,384]{1,0:T(8,128)(2,1)S(1)}, f16[384,384]{1,0:T(8,128)(2,1)S(1)}, u32[]{:S(2)}, u32[]{:S(2)}) collective-permute-start(f16[384,384]{1,0:T(8,128)(2,1)S(1)} %pad_maximum_fusion.1), channel_id=1, source_target_pairs={{0,2},{1,3},{2,0},{3,1},{4,6},{5,7},{6,4},{7,5},{8,10},{9,11},{10,... | collective-permute-start | bytes 884744 | tf_op jit(solution)/shard_map/ppermute | solution.py:507
  56.8 7.0 %collective-permute-done.12 = f16[384,384]{1,0:T(8,128)(2,1)S(1)} collective-permute-done((f16[384,384]{1,0:T(8,128)(2,1)S(1)}, f16[384,384]{1,0:T(8,128)(2,1)S(1)}, u32[]{:S(2)}, u32[]{:S(2)}) %collective-permute-start.12) | collective-permute-done | bytes 294944 | tf_op jit(solution)/shard_map/ppermute | solution.py:507
  64.0 0.1 reduce-precision_convert_fusion.5
  64.1 1.8 %collective-permute-start.13 = (f16[208,384]{1,0:T(8,128)(2,1)S(1)}, f16[208,384]{1,0:T(8,128)(2,1)S(1)}, u32[]{:S(2)}, u32[]{:S(2)}) collective-permute-start(f16[208,384]{1,0:T(8,128)(2,1)S(1)} %maximum_maximum_fusion.1), channel_id=1, source_target_pairs={{0,2},{1,3},{2,0},{3,1},{4,6},{5,7},{6,4},{7,5},{8,10},{9,11},{10,... | collective-permute-start | bytes 479240 | tf_op jit(solution)/shard_map/ppermute | solution.py:507
  66.0 1.3 %collective-permute-start.14 = (f16[192,384]{1,0:T(8,128)(2,1)S(1)}, f16[192,384]{1,0:T(8,128)(2,1)S(1)}, u32[]{:S(2)}, u32[]{:S(2)}) collective-permute-start(f16[192,384]{1,0:T(8,128)(2,1)S(1)} %fusion.4), channel_id=1, source_target_pairs={{0,1},{1,0},{2,3},{3,2},{4,5},{5,4},{6,7},{7,6},{8,9},{9,8},{10,11... | collective-permute-start | bytes 442376 | tf_op jit(solution)/shard_map/ppermute | solution.py:507
  67.3 0.1 convert_add_fusion.2
  67.4 3.8 %collective-permute-done.14 = f16[192,384]{1,0:T(8,128)(2,1)S(1)} collective-permute-done((f16[192,384]{1,0:T(8,128)(2,1)S(1)}, f16[192,384]{1,0:T(8,128)(2,1)S(1)}, u32[]{:S(2)}, u32[]{:S(2)}) %collective-permute-start.14) | collective-permute-done | bytes 147488 | tf_op jit(solution)/shard_map/ppermute | solution.py:507
  71.3 0.1 reduce-precision_convert_fusion.3
  71.4 0.4 fusion.46
  71.8 0.4 collective-permute-start.15
  72.2 1.6 %collective-permute-start.16 = (f16[192,384]{1,0:T(8,128)(2,1)S(1)}, f16[192,384]{1,0:T(8,128)(2,1)S(1)}, u32[]{:S(2)}, u32[]{:S(2)}) collective-permute-start(f16[192,384]{1,0:T(8,128)(2,1)S(1)} %get-tuple-element.86), channel_id=1, source_target_pairs={{0,24},{4,28},{8,16},{12,20},{16,8},{20,12},{24,0},{28,4},{1,25},{... | collective-permute-start | bytes 442376 | tf_op jit(solution)/shard_map/ppermute | solution.py:507
  73.8 5.6 %collective-permute-done.16 = f16[192,384]{1,0:T(8,128)(2,1)S(1)} collective-permute-done((f16[192,384]{1,0:T(8,128)(2,1)S(1)}, f16[192,384]{1,0:T(8,128)(2,1)S(1)}, u32[]{:S(2)}, u32[]{:S(2)}) %collective-permute-start.16) | collective-permute-done | bytes 147488 | tf_op jit(solution)/shard_map/ppermute | solution.py:507
  79.4 0.1 reduce-precision_convert_fusion.1
  79.5 0.2 fusion.7
  79.8 2.0 %collective-permute-start.17 = (f16[208,384]{1,0:T(8,128)(2,1)S(1)}, f16[208,384]{1,0:T(8,128)(2,1)S(1)}, u32[]{:S(2)}, u32[]{:S(2)}) collective-permute-start(f16[208,384]{1,0:T(8,128)(2,1)S(1)} %maximum_maximum_fusion.3), channel_id=1, source_target_pairs={{0,24},{4,28},{8,16},{12,20},{16,8},{20,12},{24,0},{28,4},{1,25},{... | collective-permute-start | bytes 479240 | tf_op jit(solution)/shard_map/ppermute | solution.py:507
  81.8 0.2 fusion.6
  82.0 0.1 collective-permute-start.18
  82.0 0.6 reshape.25
  82.7 5.9 %collective-permute-done.18 = f16[192,384]{1,0:T(8,128)(2,1)S(1)} collective-permute-done((f16[192,384]{1,0:T(8,128)(2,1)S(1)}, f16[192,384]{1,0:T(8,128)(2,1)S(1)}, u32[]{:S(2)}, u32[]{:S(2)}) %collective-permute-start.18) | collective-permute-done | bytes 147488 | tf_op jit(solution)/shard_map/ppermute | solution.py:507
  88.6 0.0 copy-start.14
  88.6 0.0 copy-start.15
  88.6 0.2 slice_add_fusion
  88.8 0.1 collective-permute-start.19
  88.9 0.2 convert_add_fusion.3
  89.1 0.6 collective-permute-start.20
  89.7 0.5 slice.102
  90.9 1.2 %add_multiply_fusion = (f32[384,384]{1,0:T(8,128)}, f32[384,384]{1,0:T(8,128)}) fusion(f32[384,384]{1,0:T(8,128)S(1)} %copy-done.14, f32[384,384]{1,0:T(8,128)S(1)} %constant_dynamic-update-slice_fusion, f32[192,384]{1,0:T(8,128)S(1)} %convert_add_fusion.3, f32[192,384]{1,0:T(8,128)S(1)} %slice_add_fusion, pred[]{:T(512)S(6)} %eq.5, f32[384,384]{1,0:T(8,128)S(1)} %copy-done.15), kind=kLoop, calls=%fused_computation.1 | loop fusion | flops 1327104 | bytes 3538945 | tf_op jit(solution)/shard_map/div | solution.py:655
  (58 shorter events, 0.9 us)
Async XLA Ops:
  0.6 10.0 %copy-start.5 = (f32[2,1000]{1,0:T(2,128)S(1)}, f32[2,1000]{1,0:T(2,128)}, u32[]{:S(2)}) copy-start(f32[2,1000]{1,0:T(2,128)} %constant.44.clone.table_ref) | copy-start | bytes 24004
  0.6 10.0 %copy-start.3 = (f32[3,16,384]{2,1,0:T(8,128)S(1)}, f32[3,16,384]{2,1,0:T(8,128)}, u32[]{:S(2)}) copy-start(f32[3,16,384]{2,1,0:T(8,128)} %constant.45.clone.constant_hbm) | copy-start | bytes 221188
  0.7 9.9 %copy-start.8 = (bf16[384,16]{0,1:T(8,128)(2,1)S(1)}, bf16[384,16]{0,1:T(8,128)(2,1)}, u32[]{:S(2)}) copy-start(bf16[384,16]{0,1:T(8,128)(2,1)} %param.31) | copy-start | bytes 36868
  0.7 9.9 %copy-start.2 = (bf16[256,384]{1,0:T(8,128)(2,1)S(1)}, bf16[256,384]{1,0:T(8,128)(2,1)}, u32[]{:S(2)}) copy-start(bf16[256,384]{1,0:T(8,128)(2,1)} %w_time_hbm) | copy-start | bytes 589828
  0.7 9.9 %copy-start.7 = (bf16[16,384]{1,0:T(8,128)(2,1)S(1)}, bf16[16,384]{1,0:T(8,128)(2,1)}, u32[]{:S(2)}) copy-start(bf16[16,384]{1,0:T(8,128)(2,1)} %w_patch_hbm) | copy-start | bytes 36868
  0.7 9.9 %copy-start.4 = (f32[1,1,4,4096]{3,2,1,0:T(4,128)S(1)}, f32[1,1,4,4096]{3,2,1,0:T(4,128)}, u32[]{:S(2)}) copy-start(f32[1,1,4,4096]{3,2,1,0:T(4,128)} %param.24) | copy-start | bytes 196612
  0.7 9.9 %copy-start.9 = (s32[1,1,4]{2,1,0:T(1,128)S(1)}, s32[1,1,4]{2,1,0:T(1,128)}, u32[]{:S(2)}) copy-start(s32[1,1,4]{2,1,0:T(1,128)} %param.23) | copy-start | bytes 52
  0.7 9.9 %copy-start.10 = (s32[1,1,4,2]{2,3,1,0:T(2,128)S(1)}, s32[1,1,4,2]{2,3,1,0:T(2,128)}, u32[]{:S(2)}) copy-start(s32[1,1,4,2]{2,3,1,0:T(2,128)} %param.22) | copy-start | bytes 100
  0.7 9.9 %copy-start.11 = (s32[1,1,4]{2,1,0:T(1,128)S(1)}, s32[1,1,4]{2,1,0:T(1,128)}, u32[]{:S(2)}) copy-start(s32[1,1,4]{2,1,0:T(1,128)} %param.21) | copy-start | bytes 52
  0.7 30.2 %copy-start.6 = (f32[1,1,4096]{2,1,0:T(1,128)S(1)}, f32[1,1,4096]{2,1,0:T(1,128)}, u32[]{:S(2)}) copy-start(f32[1,1,4096]{2,1,0:T(1,128)} %param.20) | copy-start | bytes 49156
  1.9 12.4 %collective-permute-start.2 = (bf16[384,384]{1,0:T(8,128)(2,1)S(1)}, bf16[384,384]{1,0:T(8,128)(2,1)S(1)}, u32[]{:S(2)}, u32[]{:S(2)}) collective-permute-start(bf16[384,384]{1,0:T(8,128)(2,1)S(1)} %broadcast_select_fusion), channel_id=1, source_target_pairs={{0,3},{1,2},{2,1},{3,0},{4,7},{5,6},{6,5},{7,4},{8,11},{9,10},{10,... | collective-permute-start | bytes 884744 | tf_op jit(solution)/shard_map/ppermute | solution.py:507
  5.9 13.3 %collective-permute-start.1 = (bf16[384,384]{1,0:T(8,128)(2,1)S(1)}, bf16[384,384]{1,0:T(8,128)(2,1)S(1)}, u32[]{:S(2)}, u32[]{:S(2)}) collective-permute-start(bf16[384,384]{1,0:T(8,128)(2,1)S(1)} %broadcast_select_fusion), channel_id=1, source_target_pairs={{0,2},{1,3},{2,0},{3,1},{4,6},{5,7},{6,4},{7,5},{8,10},{9,11},{10,... | collective-permute-start | bytes 884744 | tf_op jit(solution)/shard_map/ppermute | solution.py:507
  6.4 13.1 %collective-permute-start = (bf16[384,384]{1,0:T(8,128)(2,1)S(1)}, bf16[384,384]{1,0:T(8,128)(2,1)S(1)}, u32[]{:S(2)}, u32[]{:S(2)}) collective-permute-start(bf16[384,384]{1,0:T(8,128)(2,1)S(1)} %broadcast_select_fusion), channel_id=1, source_target_pairs={{0,1},{1,0},{2,3},{3,2},{4,5},{5,4},{6,7},{7,6},{8,9},{9,8},{10,11... | collective-permute-start | bytes 884744 | tf_op jit(solution)/shard_map/ppermute | solution.py:507
  10.6 23.4 %copy-start = (bf16[384,384]{1,0:T(8,128)(2,1)S(1)}, bf16[384,384]{1,0:T(8,128)(2,1)}, u32[]{:S(2)}) copy-start(bf16[384,384]{1,0:T(8,128)(2,1)} %rest_0_.1) | copy-start | bytes 884740
  10.6 23.4 %copy-start.1 = (bf16[384,384]{1,0:T(8,128)(2,1)S(1)}, bf16[384,384]{1,0:T(8,128)(2,1)}, u32[]{:S(2)}) copy-start(bf16[384,384]{1,0:T(8,128)(2,1)} %rest_1_.1) | copy-start | bytes 884740
  13.6 0.7 copy-start.12
  19.5 14.5 %collective-permute-start.3 = (bf16[384,384]{1,0:T(8,128)(2,1)S(1)}, bf16[384,384]{1,0:T(8,128)(2,1)S(1)}, u32[]{:S(2)}, u32[]{:S(2)}) collective-permute-start(bf16[384,384]{1,0:T(8,128)(2,1)S(1)} %collective-permute-done.rest_2_), channel_id=1, source_target_pairs={{0,4},{4,0},{8,12},{12,8},{16,20},{20,16},{24,28},{28,24},{1,5},{5... | collective-permute-start | bytes 884744 | tf_op jit(solution)/shard_map/ppermute | solution.py:507
  19.5 14.5 %collective-permute-start.4 = (bf16[384,384]{1,0:T(8,128)(2,1)S(1)}, bf16[384,384]{1,0:T(8,128)(2,1)S(1)}, u32[]{:S(2)}, u32[]{:S(2)}) collective-permute-start(bf16[384,384]{1,0:T(8,128)(2,1)S(1)} %collective-permute-done.1.rest_3_), channel_id=1, source_target_pairs={{0,4},{4,0},{8,12},{12,8},{16,20},{20,16},{24,28},{28,24},{1,5},{5... | collective-permute-start | bytes 884744 | tf_op jit(solution)/shard_map/ppermute | solution.py:507
  20.0 14.0 %collective-permute-start.5 = (bf16[384,384]{1,0:T(8,128)(2,1)S(1)}, bf16[384,384]{1,0:T(8,128)(2,1)}, u32[]{:S(2)}, u32[]{:S(2)}) collective-permute-start(bf16[384,384]{1,0:T(8,128)(2,1)S(1)} %collective-permute-done.2.rest_4_), channel_id=1, source_target_pairs={{0,4},{4,0},{8,12},{12,8},{16,20},{20,16},{24,28},{28,24},{1,5},{5... | collective-permute-start | bytes 884744 | tf_op jit(solution)/shard_map/ppermute | solution.py:507
  20.0 10.9 %all-to-all-start = ((f32[8,8,256]{2,1,0:T(8,128)}), f32[8,8,256]{2,1,0:T(8,128)S(1)}, u32[]{:S(2)}, u32[]{:S(2)}) async-start(f32[8,8,256]{2,1,0:T(8,128)} %local_conv.1), calls=%async_computation | async-start | bytes 131072 | tf_op jit(solution)/shard_map/all_to_all | solution.py:564
  34.0 0.9 copy-start.13
  51.0 2.9 %collective-permute-start.9 = (f16[384,384]{1,0:T(8,128)(2,1)S(1)}, f16[384,384]{1,0:T(8,128)(2,1)S(1)}, u32[]{:S(2)}, u32[]{:S(2)}) collective-permute-start(f16[384,384]{1,0:T(8,128)(2,1)S(1)} %convert_element_type.65), channel_id=1, source_target_pairs={{0,4},{4,0},{8,12},{12,8},{16,20},{20,16},{24,28},{28,24},{1,5},{5... | collective-permute-start | bytes 884744 | tf_op jit(solution)/shard_map/ppermute | solution.py:507
  51.1 2.9 %collective-permute-start.8 = (f16[384,384]{1,0:T(8,128)(2,1)S(1)}, f16[384,384]{1,0:T(8,128)(2,1)S(1)}, u32[]{:S(2)}, u32[]{:S(2)}) collective-permute-start(f16[384,384]{1,0:T(8,128)(2,1)S(1)} %convert_element_type.64), channel_id=1, source_target_pairs={{0,4},{4,0},{8,12},{12,8},{16,20},{20,16},{24,28},{28,24},{1,5},{5... | collective-permute-start | bytes 884744 | tf_op jit(solution)/shard_map/ppermute | solution.py:507
  51.6 2.4 %collective-permute-start.7 = (f16[384,384]{1,0:T(8,128)(2,1)S(1)}, f16[384,384]{1,0:T(8,128)(2,1)S(1)}, u32[]{:S(2)}, u32[]{:S(2)}) collective-permute-start(f16[384,384]{1,0:T(8,128)(2,1)S(1)} %convert_element_type.63), channel_id=1, source_target_pairs={{0,4},{4,0},{8,12},{12,8},{16,20},{20,16},{24,28},{28,24},{1,5},{5... | collective-permute-start | bytes 884744 | tf_op jit(solution)/shard_map/ppermute | solution.py:507
  51.6 2.3 %collective-permute-start.6 = (f16[384,384]{1,0:T(8,128)(2,1)S(1)}, f16[384,384]{1,0:T(8,128)(2,1)S(1)}, u32[]{:S(2)}, u32[]{:S(2)}) collective-permute-start(f16[384,384]{1,0:T(8,128)(2,1)S(1)} %convert_element_type.62), channel_id=1, source_target_pairs={{0,4},{4,0},{8,12},{12,8},{16,20},{20,16},{24,28},{28,24},{1,5},{5... | collective-permute-start | bytes 884744 | tf_op jit(solution)/shard_map/ppermute | solution.py:507
  52.1 1.8 %collective-permute-start.10 = (f32[16,128]{1,0:T(8,128)S(1)}, f32[16,128]{1,0:T(8,128)S(1)}, u32[]{:S(2)}, u32[]{:S(2)}) collective-permute-start(f32[16,128]{1,0:T(8,128)S(1)} %get-tuple-element.66), channel_id=1, source_target_pairs={{0,4},{4,0},{8,12},{12,8},{16,20},{20,16},{24,28},{28,24},{1,5},{5... | collective-permute-start | bytes 24584 | tf_op jit(solution)/shard_map/ppermute | solution.py:507
  54.4 9.5 %collective-permute-start.11 = (f16[400,384]{1,0:T(8,128)(2,1)S(1)}, f16[400,384]{1,0:T(8,128)(2,1)S(1)}, u32[]{:S(2)}, u32[]{:S(2)}) collective-permute-start(f16[400,384]{1,0:T(8,128)(2,1)S(1)} %maximum_maximum_fusion), channel_id=1, source_target_pairs={{0,1},{1,0},{2,3},{3,2},{4,5},{5,4},{6,7},{7,6},{8,9},{9,8},{10,11... | collective-permute-start | bytes 921608 | tf_op jit(solution)/shard_map/ppermute | solution.py:507
  54.6 9.3 %collective-permute-start.12 = (f16[384,384]{1,0:T(8,128)(2,1)S(1)}, f16[384,384]{1,0:T(8,128)(2,1)S(1)}, u32[]{:S(2)}, u32[]{:S(2)}) collective-permute-start(f16[384,384]{1,0:T(8,128)(2,1)S(1)} %pad_maximum_fusion.1), channel_id=1, source_target_pairs={{0,2},{1,3},{2,0},{3,1},{4,6},{5,7},{6,4},{7,5},{8,10},{9,11},{10,... | collective-permute-start | bytes 884744 | tf_op jit(solution)/shard_map/ppermute | solution.py:507
  64.1 7.1 %collective-permute-start.13 = (f16[208,384]{1,0:T(8,128)(2,1)S(1)}, f16[208,384]{1,0:T(8,128)(2,1)S(1)}, u32[]{:S(2)}, u32[]{:S(2)}) collective-permute-start(f16[208,384]{1,0:T(8,128)(2,1)S(1)} %maximum_maximum_fusion.1), channel_id=1, source_target_pairs={{0,2},{1,3},{2,0},{3,1},{4,6},{5,7},{6,4},{7,5},{8,10},{9,11},{10,... | collective-permute-start | bytes 479240 | tf_op jit(solution)/shard_map/ppermute | solution.py:507
  66.0 5.2 %collective-permute-start.14 = (f16[192,384]{1,0:T(8,128)(2,1)S(1)}, f16[192,384]{1,0:T(8,128)(2,1)S(1)}, u32[]{:S(2)}, u32[]{:S(2)}) collective-permute-start(f16[192,384]{1,0:T(8,128)(2,1)S(1)} %fusion.4), channel_id=1, source_target_pairs={{0,1},{1,0},{2,3},{3,2},{4,5},{5,4},{6,7},{7,6},{8,9},{9,8},{10,11... | collective-permute-start | bytes 442376 | tf_op jit(solution)/shard_map/ppermute | solution.py:507
  71.8 7.7 %collective-permute-start.15 = (f16[208,384]{1,0:T(8,128)(2,1)S(1)}, f16[208,384]{1,0:T(8,128)(2,1)S(1)}, u32[]{:S(2)}, u32[]{:S(2)}) collective-permute-start(f16[208,384]{1,0:T(8,128)(2,1)S(1)} %maximum_maximum_fusion.2), channel_id=1, source_target_pairs={{0,8},{4,12},{8,0},{12,4},{16,24},{20,28},{24,16},{28,20},{1,9},{5... | collective-permute-start | bytes 479240 | tf_op jit(solution)/shard_map/ppermute | solution.py:507
  72.2 7.2 %collective-permute-start.16 = (f16[192,384]{1,0:T(8,128)(2,1)S(1)}, f16[192,384]{1,0:T(8,128)(2,1)S(1)}, u32[]{:S(2)}, u32[]{:S(2)}) collective-permute-start(f16[192,384]{1,0:T(8,128)(2,1)S(1)} %get-tuple-element.86), channel_id=1, source_target_pairs={{0,24},{4,28},{8,16},{12,20},{16,8},{20,12},{24,0},{28,4},{1,25},{... | collective-permute-start | bytes 442376 | tf_op jit(solution)/shard_map/ppermute | solution.py:507
  79.8 8.8 %collective-permute-start.17 = (f16[208,384]{1,0:T(8,128)(2,1)S(1)}, f16[208,384]{1,0:T(8,128)(2,1)S(1)}, u32[]{:S(2)}, u32[]{:S(2)}) collective-permute-start(f16[208,384]{1,0:T(8,128)(2,1)S(1)} %maximum_maximum_fusion.3), channel_id=1, source_target_pairs={{0,24},{4,28},{8,16},{12,20},{16,8},{20,12},{24,0},{28,4},{1,25},{... | collective-permute-start | bytes 479240 | tf_op jit(solution)/shard_map/ppermute | solution.py:507
  82.0 6.6 %collective-permute-start.18 = (f16[192,384]{1,0:T(8,128)(2,1)S(1)}, f16[192,384]{1,0:T(8,128)(2,1)S(1)}, u32[]{:S(2)}, u32[]{:S(2)}) collective-permute-start(f16[192,384]{1,0:T(8,128)(2,1)S(1)} %fusion.6), channel_id=1, source_target_pairs={{0,8},{4,12},{8,0},{12,4},{16,24},{20,28},{24,16},{28,20},{1,9},{5... | collective-permute-start | bytes 442376 | tf_op jit(solution)/shard_map/ppermute | solution.py:507
  88.6 2.3 %copy-start.14 = (f32[384,384]{1,0:T(8,128)S(1)}, f32[384,384]{1,0:T(8,128)}, u32[]{:S(2)}) copy-start(f32[384,384]{1,0:T(8,128)} %param.33) | copy-start | bytes 1769476
  88.6 2.3 %copy-start.15 = (f32[384,384]{1,0:T(8,128)S(1)}, f32[384,384]{1,0:T(8,128)}, u32[]{:S(2)}) copy-start(f32[384,384]{1,0:T(8,128)} %param.32) | copy-start | bytes 1769476
  88.8 2.0 %collective-permute-start.19 = (f32[192,384]{1,0:T(8,128)S(1)}, f32[192,384]{1,0:T(8,128)S(1)}, u32[]{:S(2)}, u32[]{:S(2)}) collective-permute-start(f32[192,384]{1,0:T(8,128)S(1)} %slice_add_fusion), channel_id=1, source_target_pairs={{0,4},{4,0},{8,12},{12,8},{16,20},{20,16},{24,28},{28,24},{1,5},{5... | collective-permute-start | bytes 884744 | tf_op jit(solution)/shard_map/ppermute | solution.py:507
  89.1 1.8 %collective-permute-start.20 = (f32[192,384]{1,0:T(8,128)S(1)}, f32[192,384]{1,0:T(8,128)S(1)}, u32[]{:S(2)}, u32[]{:S(2)}) collective-permute-start(f32[192,384]{1,0:T(8,128)S(1)} %convert_add_fusion.3), channel_id=1, source_target_pairs={{0,4},{4,0},{8,12},{12,8},{16,20},{20,16},{24,28},{28,24},{1,5},{5... | collective-permute-start | bytes 884744 | tf_op jit(solution)/shard_map/ppermute | solution.py:507

commit v4 on v3

--- a/solution.py
+++ b/solution.py
@@ -117,11 +117,17 @@
     lanes = side * outs
     padded = -(-(rows + 2) // 8) * 8
     weight = conv_weight.transpose(0, 1, 3, 2).reshape(9 * outs, channels)
+    steps = 2 if images % 2 == 0 else 1
+    cells = images * rows * side
     return pl.pallas_call(
         partial(conv_kernel, rows, side, outs),
         out_shape=jax.ShapeDtypeStruct((images, padded, lanes), F32),
-        in_specs=[pl.BlockSpec(memory_space=pltpu.VMEM)] * 2,
-        out_specs=pl.BlockSpec(memory_space=pltpu.VMEM),
+        grid=(steps,),
+        in_specs=[
+            pl.BlockSpec((cells // steps, channels), lambda i: (i, 0)),
+            pl.BlockSpec((9 * outs, channels), lambda i: (0, 0)),
+        ],
+        out_specs=pl.BlockSpec((images // steps, padded, lanes), lambda i: (i, 0, 0)),
         compiler_params=pltpu.CompilerParams(vmem_limit_bytes=56 << 20),
         cost_estimate=pl.CostEstimate(
             flops=2 * images * rows * lanes * channels * 9,
@@ -129,7 +135,7 @@
             transcendentals=0,
         ),
         name="local_conv",
-    )(features.reshape(images * rows * side, channels), weight)
+    )(features.reshape(cells, channels), weight)
 
 
 def row_mean(values):

time: 93.6 us -> 93.6 us (level)
  no operation moved by 1% of the time
where the time goes in v4:
time: 93.6 us; the launch traced here: 93.3 us
  waiting for transfers between devices  34.6 us (37%)
  Pallas kernels  25.9 us (28%)
  starting transfers between devices  21.4 us (23%)
  other arithmetic  4.74 us (5%)
  between operations  3.64 us (4%)
  local copies, waits for them, and re-layouts  2.92 us (3%)
    ppermute x21, waiting for transfers between devices, shift(): return lax.ppermute(values, axis, [(i, i ^ flip) for i in range(count)])  29.3 us
    ppermute x21, starting transfers between devices, shift(): return lax.ppermute(values, axis, [(i, i ^ flip) for i in range(count)])  16.4 us
    pallas_call x1, Pallas kernels, grad_call(): pl.pallas_call(partial(grad_kernel, blocks, views), out_shape=out_shape,...  15.8 us
    all_to_all x1, waiting for transfers between devices, per_device(): parts = lax.all_to_all(local, 'dp', split_axis=0, concat_axis=0, tiled=True)  5.27 us
    all_to_all x1, starting transfers between devices, per_device(): parts = lax.all_to_all(local, 'dp', split_axis=0, concat_axis=0, tiled=True)  4.99 us
    pallas_call x1, Pallas kernels, local_conv(): pl.pallas_call(partial(conv_kernel, rows, side, outs), out_shape=jax.Shap...  4.14 us
    pallas_call x1, Pallas kernels, token_call(): pl.pallas_call(partial(token_kernel, rows), out_shape=out_shape, in_specs...  3.05 us
    pallas_call x1, Pallas kernels, prepare_call(): pl.pallas_call(partial(prepare_kernel, side), out_shape=out_shape, in_spe...  2.95 us
  transfers between devices with their start and end apart: 22, of which 8 were waited for; matrix products, arithmetic and copies ran while one was open for 2% of the time, Pallas kernels for 11%

profile of v4, /device:TPU:0, one launch (start us, length us, event | category | flops | bytes accessed | tf_op | source)
XLA Modules:
  0.0 93.3 jit_solution(17003003467217660808)
XLA Ops:
  0.6 0.0 copy-start.5
  0.6 0.0 copy-start.3
  0.8 1.2 %broadcast_select_fusion = bf16[384,384]{1,0:T(8,128)(2,1)S(1)} fusion(bf16[384,384]{1,0:T(8,128)(2,1)} %rest_0_.1, bf16[384,384]{1,0:T(8,128)(2,1)} %rest_1_.1, pred[]{:T(512)S(6)} %eq.5), kind=kLoop, calls=%fused_computation.26 | loop fusion | flops 147456 | bytes 884737 | tf_op jit(solution)/shard_map/jit(_where)/select_n | solution.py:566
  1.9 4.0 %collective-permute-start.2 = (bf16[384,384]{1,0:T(8,128)(2,1)S(1)}, bf16[384,384]{1,0:T(8,128)(2,1)S(1)}, u32[]{:S(2)}, u32[]{:S(2)}) collective-permute-start(bf16[384,384]{1,0:T(8,128)(2,1)S(1)} %broadcast_select_fusion), channel_id=1, source_target_pairs={{0,3},{1,2},{2,1},{3,0},{4,7},{5,6},{6,5},{7,4},{8,11},{9,10},{10,... | collective-permute-start | bytes 884744 | tf_op jit(solution)/shard_map/ppermute | solution.py:513
  5.9 0.5 collective-permute-start.1
  6.4 0.1 collective-permute-start
  6.5 4.1 %local_conv.1 = f32[8,8,256]{2,1,0:T(8,128)} custom-call(bf16[1024,512]{1,0:T(8,128)(2,1)} %bitcast.21, bf16[72,512]{1,0:T(8,128)(2,1)} %bitcast.22), custom_call_target="tpu_custom_call" | custom-call | flops 75497472 | bytes 1048576 | tf_op jit(solution)/shard_map/local_conv/pallas_call | solution.py:122
  10.8 3.0 %prepare.1 = (f32[16,1152]{1,0:T(8,128)S(1)}, bf16[256,384]{1,0:T(8,128)(2,1)S(1)}, bf16[256,384]{1,0:T(8,128)(2,1)S(1)}, f32[256,384]{1,0:T(8,128)S(1)}, f32[64...) custom-call(s32[4]{0:T(128)S(1)} %bitcast.20, s32[2,4]{1,0:T(2,128)S(1)} %bitcast.19, ...), custom_call_target="tpu_custom_call" | custom-call | flops 134217728 | bytes 2097152 | tf_op jit(solution)/shard_map/prepare/pallas_call | solution.py:435
  13.7 0.0 copy-start.12
  13.7 0.7 copy-done.12
  14.4 0.0 collective-permute-done.2.rest_4_
  14.4 4.8 %collective-permute-done.1.rest_3_ = bf16[384,384]{1,0:T(8,128)(2,1)S(1)} collective-permute-done((bf16[384,384]{1,0:T(8,128)(2,1)S(1)}, bf16[384,384]{1,0:T(8,128)(2,1)S(1)}, u32[]{:S(2)}, u32[]{:S(2)}) %collective-permute-start.1) | collective-permute-done | bytes 294944 | tf_op jit(solution)/shard_map/ppermute | solution.py:513
  19.2 0.3 collective-permute-done.rest_2_
  19.5 0.0 collective-permute-start.3
  19.5 0.5 collective-permute-start.4
  20.0 0.0 collective-permute-start.5
  20.0 5.0 %all-to-all-start = ((f32[8,8,256]{2,1,0:T(8,128)}), f32[8,8,256]{2,1,0:T(8,128)S(1)}, u32[]{:S(2)}, u32[]{:S(2)}) async-start(f32[8,8,256]{2,1,0:T(8,128)} %local_conv.1), calls=%async_computation | async-start | bytes 131072 | tf_op jit(solution)/shard_map/all_to_all | solution.py:570
  25.7 5.3 %all-to-all-done.parts_ref = f32[8,8,256]{2,1,0:T(8,128)S(1)} async-done(((f32[8,8,256]{2,1,0:T(8,128)}), f32[8,8,256]{2,1,0:T(8,128)S(1)}, u32[]{:S(2)}, u32[]{:S(2)}) %all-to-all-start) | async-done | bytes 65568 | tf_op jit(solution)/shard_map/all_to_all | solution.py:570
  30.9 3.0 %tokens.1 = (f32[32,256]{1,0:T(8,128)S(1)}, f32[1024,384]{1,0:T(8,128)S(1)}, bf16[1024,384]{1,0:T(8,128)(2,1)S(1)}) custom-call(s32[1,1]{1,0:T(1,128)S(6)} %copy.23.chosen_ref, s32[4]{0:T(128)S(1)} %bitcast.18, f32[2,1000]{1,0:T(2,128)S(1)} %copy-done.5, f32[8,8,256]{2,1,0:T(8,128)S(1)} %all-to-all-done.parts_ref, f32[32,128]{1,0:T(8,128)S(1)} %bitcast.15, ...), custom_call_target="tpu_custom_call" | custom-call | flops 201326592 | bytes 6291456 | tf_op jit(solution)/shard_map/tokens/pallas_call | solution.py:463
  34.0 0.0 collective-permute-done.4.rest_6_
  34.0 0.0 collective-permute-done.5.rest_7_
  34.0 0.0 copy-start.13
  34.1 0.9 copy-done.13
  35.0 15.8 %grads.1 = (f32[16,128]{1,0:T(8,128)S(1)}, f32[384,384]{1,0:T(8,128)S(1)}, f32[384,384]{1,0:T(8,128)S(1)}, f32[384,384]{1,0:T(8,128)S(1)}, f32[384,384]{1,0:T(8,...) custom-call(s32[1,1]{1,0:T(1,128)S(6)} %copy.23.chosen_ref, ...), custom_call_target="tpu_custom_call" | custom-call | flops 6039797760 | bytes 11796480 | tf_op jit(solution)/shard_map/grads/pallas_call | solution.py:488
  51.0 0.1 collective-permute-start.9
  51.1 0.5 collective-permute-start.8
  51.6 0.1 collective-permute-start.7
  51.6 0.4 collective-permute-start.6
  52.1 0.1 collective-permute-start.10
  52.2 1.8 %collective-permute-done.10 = f32[16,128]{1,0:T(8,128)S(1)} collective-permute-done((f32[16,128]{1,0:T(8,128)S(1)}, f32[16,128]{1,0:T(8,128)S(1)}, u32[]{:S(2)}, u32[]{:S(2)}) %collective-permute-start.10) | collective-permute-done | bytes 8224 | tf_op jit(solution)/shard_map/ppermute | solution.py:513
  53.9 0.0 collective-permute-done.9
  53.9 0.1 convert_add_fusion
  54.1 0.1 fusion.52
  54.2 0.1 convert_add_fusion.1
  54.3 0.1 maximum_maximum_fusion
  54.4 0.1 collective-permute-start.11
  54.5 0.1 pad_maximum_fusion.1
  54.6 2.3 %collective-permute-start.12 = (f16[384,384]{1,0:T(8,128)(2,1)S(1)}, f16[384,384]{1,0:T(8,128)(2,1)S(1)}, u32[]{:S(2)}, u32[]{:S(2)}) collective-permute-start(f16[384,384]{1,0:T(8,128)(2,1)S(1)} %pad_maximum_fusion.1), channel_id=1, source_target_pairs={{0,2},{1,3},{2,0},{3,1},{4,6},{5,7},{6,4},{7,5},{8,10},{9,11},{10,... | collective-permute-start | bytes 884744 | tf_op jit(solution)/shard_map/ppermute | solution.py:513
  56.8 7.0 %collective-permute-done.12 = f16[384,384]{1,0:T(8,128)(2,1)S(1)} collective-permute-done((f16[384,384]{1,0:T(8,128)(2,1)S(1)}, f16[384,384]{1,0:T(8,128)(2,1)S(1)}, u32[]{:S(2)}, u32[]{:S(2)}) %collective-permute-start.12) | collective-permute-done | bytes 294944 | tf_op jit(solution)/shard_map/ppermute | solution.py:513
  64.0 0.1 reduce-precision_convert_fusion.5
  64.1 1.8 %collective-permute-start.13 = (f16[208,384]{1,0:T(8,128)(2,1)S(1)}, f16[208,384]{1,0:T(8,128)(2,1)S(1)}, u32[]{:S(2)}, u32[]{:S(2)}) collective-permute-start(f16[208,384]{1,0:T(8,128)(2,1)S(1)} %maximum_maximum_fusion.1), channel_id=1, source_target_pairs={{0,2},{1,3},{2,0},{3,1},{4,6},{5,7},{6,4},{7,5},{8,10},{9,11},{10,... | collective-permute-start | bytes 479240 | tf_op jit(solution)/shard_map/ppermute | solution.py:513
  66.0 1.3 %collective-permute-start.14 = (f16[192,384]{1,0:T(8,128)(2,1)S(1)}, f16[192,384]{1,0:T(8,128)(2,1)S(1)}, u32[]{:S(2)}, u32[]{:S(2)}) collective-permute-start(f16[192,384]{1,0:T(8,128)(2,1)S(1)} %fusion.4), channel_id=1, source_target_pairs={{0,1},{1,0},{2,3},{3,2},{4,5},{5,4},{6,7},{7,6},{8,9},{9,8},{10,11... | collective-permute-start | bytes 442376 | tf_op jit(solution)/shard_map/ppermute | solution.py:513
  67.3 0.1 convert_add_fusion.2
  67.4 3.8 %collective-permute-done.14 = f16[192,384]{1,0:T(8,128)(2,1)S(1)} collective-permute-done((f16[192,384]{1,0:T(8,128)(2,1)S(1)}, f16[192,384]{1,0:T(8,128)(2,1)S(1)}, u32[]{:S(2)}, u32[]{:S(2)}) %collective-permute-start.14) | collective-permute-done | bytes 147488 | tf_op jit(solution)/shard_map/ppermute | solution.py:513
  71.3 0.1 reduce-precision_convert_fusion.3
  71.4 0.4 fusion.46
  71.8 0.4 collective-permute-start.15
  72.2 1.6 %collective-permute-start.16 = (f16[192,384]{1,0:T(8,128)(2,1)S(1)}, f16[192,384]{1,0:T(8,128)(2,1)S(1)}, u32[]{:S(2)}, u32[]{:S(2)}) collective-permute-start(f16[192,384]{1,0:T(8,128)(2,1)S(1)} %get-tuple-element.86), channel_id=1, source_target_pairs={{0,24},{4,28},{8,16},{12,20},{16,8},{20,12},{24,0},{28,4},{1,25},{... | collective-permute-start | bytes 442376 | tf_op jit(solution)/shard_map/ppermute | solution.py:513
  73.8 5.6 %collective-permute-done.16 = f16[192,384]{1,0:T(8,128)(2,1)S(1)} collective-permute-done((f16[192,384]{1,0:T(8,128)(2,1)S(1)}, f16[192,384]{1,0:T(8,128)(2,1)S(1)}, u32[]{:S(2)}, u32[]{:S(2)}) %collective-permute-start.16) | collective-permute-done | bytes 147488 | tf_op jit(solution)/shard_map/ppermute | solution.py:513
  79.4 0.1 reduce-precision_convert_fusion.1
  79.5 0.2 fusion.7
  79.8 2.0 %collective-permute-start.17 = (f16[208,384]{1,0:T(8,128)(2,1)S(1)}, f16[208,384]{1,0:T(8,128)(2,1)S(1)}, u32[]{:S(2)}, u32[]{:S(2)}) collective-permute-start(f16[208,384]{1,0:T(8,128)(2,1)S(1)} %maximum_maximum_fusion.3), channel_id=1, source_target_pairs={{0,24},{4,28},{8,16},{12,20},{16,8},{20,12},{24,0},{28,4},{1,25},{... | collective-permute-start | bytes 479240 | tf_op jit(solution)/shard_map/ppermute | solution.py:513
  81.8 0.2 fusion.6
  82.0 0.1 collective-permute-start.18
  82.0 0.6 reshape.25
  82.7 5.9 %collective-permute-done.18 = f16[192,384]{1,0:T(8,128)(2,1)S(1)} collective-permute-done((f16[192,384]{1,0:T(8,128)(2,1)S(1)}, f16[192,384]{1,0:T(8,128)(2,1)S(1)}, u32[]{:S(2)}, u32[]{:S(2)}) %collective-permute-start.18) | collective-permute-done | bytes 147488 | tf_op jit(solution)/shard_map/ppermute | solution.py:513
  88.6 0.0 copy-start.14
  88.6 0.0 copy-start.15
  88.6 0.2 slice_add_fusion
  88.8 0.1 collective-permute-start.19
  88.9 0.2 convert_add_fusion.3
  89.1 0.6 collective-permute-start.20
  89.7 0.5 slice.102
  90.9 1.2 %add_multiply_fusion = (f32[384,384]{1,0:T(8,128)}, f32[384,384]{1,0:T(8,128)}) fusion(f32[384,384]{1,0:T(8,128)S(1)} %copy-done.14, f32[384,384]{1,0:T(8,128)S(1)} %constant_dynamic-update-slice_fusion, f32[192,384]{1,0:T(8,128)S(1)} %convert_add_fusion.3, f32[192,384]{1,0:T(8,128)S(1)} %slice_add_fusion, pred[]{:T(512)S(6)} %eq.5, f32[384,384]{1,0:T(8,128)S(1)} %copy-done.15), kind=kLoop, calls=%fused_computation.1 | loop fusion | flops 1327104 | bytes 3538945 | tf_op jit(solution)/shard_map/div | solution.py:661
  (58 shorter events, 0.9 us)
Async XLA Ops:
  0.6 10.1 %copy-start.5 = (f32[2,1000]{1,0:T(2,128)S(1)}, f32[2,1000]{1,0:T(2,128)}, u32[]{:S(2)}) copy-start(f32[2,1000]{1,0:T(2,128)} %constant.44.clone.table_ref) | copy-start | bytes 24004
  0.6 10.0 %copy-start.3 = (f32[3,16,384]{2,1,0:T(8,128)S(1)}, f32[3,16,384]{2,1,0:T(8,128)}, u32[]{:S(2)}) copy-start(f32[3,16,384]{2,1,0:T(8,128)} %constant.45.clone.constant_hbm) | copy-start | bytes 221188
  0.7 10.0 %copy-start.8 = (bf16[384,16]{0,1:T(8,128)(2,1)S(1)}, bf16[384,16]{0,1:T(8,128)(2,1)}, u32[]{:S(2)}) copy-start(bf16[384,16]{0,1:T(8,128)(2,1)} %param.31) | copy-start | bytes 36868
  0.7 10.0 %copy-start.2 = (bf16[256,384]{1,0:T(8,128)(2,1)S(1)}, bf16[256,384]{1,0:T(8,128)(2,1)}, u32[]{:S(2)}) copy-start(bf16[256,384]{1,0:T(8,128)(2,1)} %w_time_hbm) | copy-start | bytes 589828
  0.7 10.0 %copy-start.7 = (bf16[16,384]{1,0:T(8,128)(2,1)S(1)}, bf16[16,384]{1,0:T(8,128)(2,1)}, u32[]{:S(2)}) copy-start(bf16[16,384]{1,0:T(8,128)(2,1)} %w_patch_hbm) | copy-start | bytes 36868
  0.7 10.0 %copy-start.4 = (f32[1,1,4,4096]{3,2,1,0:T(4,128)S(1)}, f32[1,1,4,4096]{3,2,1,0:T(4,128)}, u32[]{:S(2)}) copy-start(f32[1,1,4,4096]{3,2,1,0:T(4,128)} %param.24) | copy-start | bytes 196612
  0.7 10.0 %copy-start.9 = (s32[1,1,4]{2,1,0:T(1,128)S(1)}, s32[1,1,4]{2,1,0:T(1,128)}, u32[]{:S(2)}) copy-start(s32[1,1,4]{2,1,0:T(1,128)} %param.23) | copy-start | bytes 52
  0.7 10.0 %copy-start.10 = (s32[1,1,4,2]{2,3,1,0:T(2,128)S(1)}, s32[1,1,4,2]{2,3,1,0:T(2,128)}, u32[]{:S(2)}) copy-start(s32[1,1,4,2]{2,3,1,0:T(2,128)} %param.22) | copy-start | bytes 100
  0.7 10.0 %copy-start.11 = (s32[1,1,4]{2,1,0:T(1,128)S(1)}, s32[1,1,4]{2,1,0:T(1,128)}, u32[]{:S(2)}) copy-start(s32[1,1,4]{2,1,0:T(1,128)} %param.21) | copy-start | bytes 52
  0.7 30.2 %copy-start.6 = (f32[1,1,4096]{2,1,0:T(1,128)S(1)}, f32[1,1,4096]{2,1,0:T(1,128)}, u32[]{:S(2)}) copy-start(f32[1,1,4096]{2,1,0:T(1,128)} %param.20) | copy-start | bytes 49156
  1.9 12.5 %collective-permute-start.2 = (bf16[384,384]{1,0:T(8,128)(2,1)S(1)}, bf16[384,384]{1,0:T(8,128)(2,1)S(1)}, u32[]{:S(2)}, u32[]{:S(2)}) collective-permute-start(bf16[384,384]{1,0:T(8,128)(2,1)S(1)} %broadcast_select_fusion), channel_id=1, source_target_pairs={{0,3},{1,2},{2,1},{3,0},{4,7},{5,6},{6,5},{7,4},{8,11},{9,10},{10,... | collective-permute-start | bytes 884744 | tf_op jit(solution)/shard_map/ppermute | solution.py:513
  5.9 13.3 %collective-permute-start.1 = (bf16[384,384]{1,0:T(8,128)(2,1)S(1)}, bf16[384,384]{1,0:T(8,128)(2,1)S(1)}, u32[]{:S(2)}, u32[]{:S(2)}) collective-permute-start(bf16[384,384]{1,0:T(8,128)(2,1)S(1)} %broadcast_select_fusion), channel_id=1, source_target_pairs={{0,2},{1,3},{2,0},{3,1},{4,6},{5,7},{6,4},{7,5},{8,10},{9,11},{10,... | collective-permute-start | bytes 884744 | tf_op jit(solution)/shard_map/ppermute | solution.py:513
  6.4 13.1 %collective-permute-start = (bf16[384,384]{1,0:T(8,128)(2,1)S(1)}, bf16[384,384]{1,0:T(8,128)(2,1)S(1)}, u32[]{:S(2)}, u32[]{:S(2)}) collective-permute-start(bf16[384,384]{1,0:T(8,128)(2,1)S(1)} %broadcast_select_fusion), channel_id=1, source_target_pairs={{0,1},{1,0},{2,3},{3,2},{4,5},{5,4},{6,7},{7,6},{8,9},{9,8},{10,11... | collective-permute-start | bytes 884744 | tf_op jit(solution)/shard_map/ppermute | solution.py:513
  10.7 23.4 %copy-start = (bf16[384,384]{1,0:T(8,128)(2,1)S(1)}, bf16[384,384]{1,0:T(8,128)(2,1)}, u32[]{:S(2)}) copy-start(bf16[384,384]{1,0:T(8,128)(2,1)} %rest_0_.1) | copy-start | bytes 884740
  10.7 23.4 %copy-start.1 = (bf16[384,384]{1,0:T(8,128)(2,1)S(1)}, bf16[384,384]{1,0:T(8,128)(2,1)}, u32[]{:S(2)}) copy-start(bf16[384,384]{1,0:T(8,128)(2,1)} %rest_1_.1) | copy-start | bytes 884740
  13.7 0.7 copy-start.12
  19.5 14.5 %collective-permute-start.3 = (bf16[384,384]{1,0:T(8,128)(2,1)S(1)}, bf16[384,384]{1,0:T(8,128)(2,1)S(1)}, u32[]{:S(2)}, u32[]{:S(2)}) collective-permute-start(bf16[384,384]{1,0:T(8,128)(2,1)S(1)} %collective-permute-done.rest_2_), channel_id=1, source_target_pairs={{0,4},{4,0},{8,12},{12,8},{16,20},{20,16},{24,28},{28,24},{1,5},{5... | collective-permute-start | bytes 884744 | tf_op jit(solution)/shard_map/ppermute | solution.py:513
  19.5 14.5 %collective-permute-start.4 = (bf16[384,384]{1,0:T(8,128)(2,1)S(1)}, bf16[384,384]{1,0:T(8,128)(2,1)S(1)}, u32[]{:S(2)}, u32[]{:S(2)}) collective-permute-start(bf16[384,384]{1,0:T(8,128)(2,1)S(1)} %collective-permute-done.1.rest_3_), channel_id=1, source_target_pairs={{0,4},{4,0},{8,12},{12,8},{16,20},{20,16},{24,28},{28,24},{1,5},{5... | collective-permute-start | bytes 884744 | tf_op jit(solution)/shard_map/ppermute | solution.py:513
  20.0 14.0 %collective-permute-start.5 = (bf16[384,384]{1,0:T(8,128)(2,1)S(1)}, bf16[384,384]{1,0:T(8,128)(2,1)}, u32[]{:S(2)}, u32[]{:S(2)}) collective-permute-start(bf16[384,384]{1,0:T(8,128)(2,1)S(1)} %collective-permute-done.2.rest_4_), channel_id=1, source_target_pairs={{0,4},{4,0},{8,12},{12,8},{16,20},{20,16},{24,28},{28,24},{1,5},{5... | collective-permute-start | bytes 884744 | tf_op jit(solution)/shard_map/ppermute | solution.py:513
  20.0 10.9 %all-to-all-start = ((f32[8,8,256]{2,1,0:T(8,128)}), f32[8,8,256]{2,1,0:T(8,128)S(1)}, u32[]{:S(2)}, u32[]{:S(2)}) async-start(f32[8,8,256]{2,1,0:T(8,128)} %local_conv.1), calls=%async_computation | async-start | bytes 131072 | tf_op jit(solution)/shard_map/all_to_all | solution.py:570
  34.0 0.9 copy-start.13
  51.0 2.9 %collective-permute-start.9 = (f16[384,384]{1,0:T(8,128)(2,1)S(1)}, f16[384,384]{1,0:T(8,128)(2,1)S(1)}, u32[]{:S(2)}, u32[]{:S(2)}) collective-permute-start(f16[384,384]{1,0:T(8,128)(2,1)S(1)} %convert_element_type.65), channel_id=1, source_target_pairs={{0,4},{4,0},{8,12},{12,8},{16,20},{20,16},{24,28},{28,24},{1,5},{5... | collective-permute-start | bytes 884744 | tf_op jit(solution)/shard_map/ppermute | solution.py:513
  51.1 2.9 %collective-permute-start.8 = (f16[384,384]{1,0:T(8,128)(2,1)S(1)}, f16[384,384]{1,0:T(8,128)(2,1)S(1)}, u32[]{:S(2)}, u32[]{:S(2)}) collective-permute-start(f16[384,384]{1,0:T(8,128)(2,1)S(1)} %convert_element_type.64), channel_id=1, source_target_pairs={{0,4},{4,0},{8,12},{12,8},{16,20},{20,16},{24,28},{28,24},{1,5},{5... | collective-permute-start | bytes 884744 | tf_op jit(solution)/shard_map/ppermute | solution.py:513
  51.6 2.4 %collective-permute-start.7 = (f16[384,384]{1,0:T(8,128)(2,1)S(1)}, f16[384,384]{1,0:T(8,128)(2,1)S(1)}, u32[]{:S(2)}, u32[]{:S(2)}) collective-permute-start(f16[384,384]{1,0:T(8,128)(2,1)S(1)} %convert_element_type.63), channel_id=1, source_target_pairs={{0,4},{4,0},{8,12},{12,8},{16,20},{20,16},{24,28},{28,24},{1,5},{5... | collective-permute-start | bytes 884744 | tf_op jit(solution)/shard_map/ppermute | solution.py:513
  51.6 2.3 %collective-permute-start.6 = (f16[384,384]{1,0:T(8,128)(2,1)S(1)}, f16[384,384]{1,0:T(8,128)(2,1)S(1)}, u32[]{:S(2)}, u32[]{:S(2)}) collective-permute-start(f16[384,384]{1,0:T(8,128)(2,1)S(1)} %convert_element_type.62), channel_id=1, source_target_pairs={{0,4},{4,0},{8,12},{12,8},{16,20},{20,16},{24,28},{28,24},{1,5},{5... | collective-permute-start | bytes 884744 | tf_op jit(solution)/shard_map/ppermute | solution.py:513
  52.1 1.8 %collective-permute-start.10 = (f32[16,128]{1,0:T(8,128)S(1)}, f32[16,128]{1,0:T(8,128)S(1)}, u32[]{:S(2)}, u32[]{:S(2)}) collective-permute-start(f32[16,128]{1,0:T(8,128)S(1)} %get-tuple-element.66), channel_id=1, source_target_pairs={{0,4},{4,0},{8,12},{12,8},{16,20},{20,16},{24,28},{28,24},{1,5},{5... | collective-permute-start | bytes 24584 | tf_op jit(solution)/shard_map/ppermute | solution.py:513
  54.4 9.5 %collective-permute-start.11 = (f16[400,384]{1,0:T(8,128)(2,1)S(1)}, f16[400,384]{1,0:T(8,128)(2,1)S(1)}, u32[]{:S(2)}, u32[]{:S(2)}) collective-permute-start(f16[400,384]{1,0:T(8,128)(2,1)S(1)} %maximum_maximum_fusion), channel_id=1, source_target_pairs={{0,1},{1,0},{2,3},{3,2},{4,5},{5,4},{6,7},{7,6},{8,9},{9,8},{10,11... | collective-permute-start | bytes 921608 | tf_op jit(solution)/shard_map/ppermute | solution.py:513
  54.6 9.3 %collective-permute-start.12 = (f16[384,384]{1,0:T(8,128)(2,1)S(1)}, f16[384,384]{1,0:T(8,128)(2,1)S(1)}, u32[]{:S(2)}, u32[]{:S(2)}) collective-permute-start(f16[384,384]{1,0:T(8,128)(2,1)S(1)} %pad_maximum_fusion.1), channel_id=1, source_target_pairs={{0,2},{1,3},{2,0},{3,1},{4,6},{5,7},{6,4},{7,5},{8,10},{9,11},{10,... | collective-permute-start | bytes 884744 | tf_op jit(solution)/shard_map/ppermute | solution.py:513
  64.1 7.1 %collective-permute-start.13 = (f16[208,384]{1,0:T(8,128)(2,1)S(1)}, f16[208,384]{1,0:T(8,128)(2,1)S(1)}, u32[]{:S(2)}, u32[]{:S(2)}) collective-permute-start(f16[208,384]{1,0:T(8,128)(2,1)S(1)} %maximum_maximum_fusion.1), channel_id=1, source_target_pairs={{0,2},{1,3},{2,0},{3,1},{4,6},{5,7},{6,4},{7,5},{8,10},{9,11},{10,... | collective-permute-start | bytes 479240 | tf_op jit(solution)/shard_map/ppermute | solution.py:513
  66.0 5.2 %collective-permute-start.14 = (f16[192,384]{1,0:T(8,128)(2,1)S(1)}, f16[192,384]{1,0:T(8,128)(2,1)S(1)}, u32[]{:S(2)}, u32[]{:S(2)}) collective-permute-start(f16[192,384]{1,0:T(8,128)(2,1)S(1)} %fusion.4), channel_id=1, source_target_pairs={{0,1},{1,0},{2,3},{3,2},{4,5},{5,4},{6,7},{7,6},{8,9},{9,8},{10,11... | collective-permute-start | bytes 442376 | tf_op jit(solution)/shard_map/ppermute | solution.py:513
  71.8 7.7 %collective-permute-start.15 = (f16[208,384]{1,0:T(8,128)(2,1)S(1)}, f16[208,384]{1,0:T(8,128)(2,1)S(1)}, u32[]{:S(2)}, u32[]{:S(2)}) collective-permute-start(f16[208,384]{1,0:T(8,128)(2,1)S(1)} %maximum_maximum_fusion.2), channel_id=1, source_target_pairs={{0,8},{4,12},{8,0},{12,4},{16,24},{20,28},{24,16},{28,20},{1,9},{5... | collective-permute-start | bytes 479240 | tf_op jit(solution)/shard_map/ppermute | solution.py:513
  72.2 7.2 %collective-permute-start.16 = (f16[192,384]{1,0:T(8,128)(2,1)S(1)}, f16[192,384]{1,0:T(8,128)(2,1)S(1)}, u32[]{:S(2)}, u32[]{:S(2)}) collective-permute-start(f16[192,384]{1,0:T(8,128)(2,1)S(1)} %get-tuple-element.86), channel_id=1, source_target_pairs={{0,24},{4,28},{8,16},{12,20},{16,8},{20,12},{24,0},{28,4},{1,25},{... | collective-permute-start | bytes 442376 | tf_op jit(solution)/shard_map/ppermute | solution.py:513
  79.8 8.8 %collective-permute-start.17 = (f16[208,384]{1,0:T(8,128)(2,1)S(1)}, f16[208,384]{1,0:T(8,128)(2,1)S(1)}, u32[]{:S(2)}, u32[]{:S(2)}) collective-permute-start(f16[208,384]{1,0:T(8,128)(2,1)S(1)} %maximum_maximum_fusion.3), channel_id=1, source_target_pairs={{0,24},{4,28},{8,16},{12,20},{16,8},{20,12},{24,0},{28,4},{1,25},{... | collective-permute-start | bytes 479240 | tf_op jit(solution)/shard_map/ppermute | solution.py:513
  82.0 6.6 %collective-permute-start.18 = (f16[192,384]{1,0:T(8,128)(2,1)S(1)}, f16[192,384]{1,0:T(8,128)(2,1)S(1)}, u32[]{:S(2)}, u32[]{:S(2)}) collective-permute-start(f16[192,384]{1,0:T(8,128)(2,1)S(1)} %fusion.6), channel_id=1, source_target_pairs={{0,8},{4,12},{8,0},{12,4},{16,24},{20,28},{24,16},{28,20},{1,9},{5... | collective-permute-start | bytes 442376 | tf_op jit(solution)/shard_map/ppermute | solution.py:513
  88.6 2.3 %copy-start.14 = (f32[384,384]{1,0:T(8,128)S(1)}, f32[384,384]{1,0:T(8,128)}, u32[]{:S(2)}) copy-start(f32[384,384]{1,0:T(8,128)} %param.33) | copy-start | bytes 1769476
  88.6 2.3 %copy-start.15 = (f32[384,384]{1,0:T(8,128)S(1)}, f32[384,384]{1,0:T(8,128)}, u32[]{:S(2)}) copy-start(f32[384,384]{1,0:T(8,128)} %param.32) | copy-start | bytes 1769476
  88.8 2.0 %collective-permute-start.19 = (f32[192,384]{1,0:T(8,128)S(1)}, f32[192,384]{1,0:T(8,128)S(1)}, u32[]{:S(2)}, u32[]{:S(2)}) collective-permute-start(f32[192,384]{1,0:T(8,128)S(1)} %slice_add_fusion), channel_id=1, source_target_pairs={{0,4},{4,0},{8,12},{12,8},{16,20},{20,16},{24,28},{28,24},{1,5},{5... | collective-permute-start | bytes 884744 | tf_op jit(solution)/shard_map/ppermute | solution.py:513
  89.1 1.8 %collective-permute-start.20 = (f32[192,384]{1,0:T(8,128)S(1)}, f32[192,384]{1,0:T(8,128)S(1)}, u32[]{:S(2)}, u32[]{:S(2)}) collective-permute-start(f32[192,384]{1,0:T(8,128)S(1)} %convert_add_fusion.3), channel_id=1, source_target_pairs={{0,4},{4,0},{8,12},{12,8},{16,20},{20,16},{24,28},{28,24},{1,5},{5... | collective-permute-start | bytes 884744 | tf_op jit(solution)/shard_map/ppermute | solution.py:513
